TPU v7x, 32 devices: a whole 2x2x4 slice. The times are simulated.
32 devices in a mesh: wide: 8 (over z, y), narrow: 4 (over x, core).
Axes of the slice: x: 2, y: 2, z: 4, core: 2. Of those that a mesh axis runs over, the one named last changes fastest.
Arguments:
- acoustic_features: bfloat16 [16384, 1024], P(('wide', 'narrow')), may hold values from -6 to 6
- utterance_durations: int32 [32, 8], P(('wide', 'narrow')), may hold values from 0 to 256, as said below
- perturbation_samples: bfloat16 [16384, 1024], P(('wide', 'narrow')), may hold values from -3 to 14, as said below
- annealing_level: float32 [1], replicated, may hold values from 0.5 to 2
- result_cotangent: bfloat16 [16384, 1024], P(('wide', 'narrow')), may hold values from -6 to 6
- quantized_cotangent: bfloat16 [16384, 1024], P(('wide', 'narrow')), may hold values from -6 to 6
- early_expanding_projector: bfloat16 [1024, 4096], P('narrow'), may hold values from -0.1875 to 0.1875
- early_contracting_projector: bfloat16 [4096, 1024], P('narrow'), may hold values from -0.25 to 0.25
- query_key_value_projector: bfloat16 [1024, 3072], P('narrow'), may hold values from -0.25 to 0.25
- heads_merging_projector: bfloat16 [1024, 1024], P('narrow'), may hold values from -0.5 to 0.5
- gated_channel_projector: bfloat16 [1024, 2048], P('narrow'), may hold values from -0.1875 to 0.1875
- closing_channel_projector: bfloat16 [1024, 1024], P('narrow'), may hold values from -0.25 to 0.25
- later_expanding_projector: bfloat16 [1024, 4096], P('narrow'), may hold values from -0.1875 to 0.1875
- later_contracting_projector: bfloat16 [4096, 1024], P('narrow'), may hold values from -0.25 to 0.25
- vocabulary_affinity_projector: bfloat16 [1024, 1024], P('narrow'), may hold values from -0.25 to 0.25
- vocabulary_vectors: bfloat16 [1024, 1024], P('narrow'), may hold values from -12 to 12
- normalizer_gains: bfloat16 [6, 1024], P(None, 'narrow'), may hold values from 0.25 to 1.75
- channelwise_kernel_weights: bfloat16 [5, 1024], P(None, 'narrow'), may hold values from -3 to 3
- normalizer_affine_rows: bfloat16 [2, 1024], P(None, 'narrow'), may hold values from 0.5 to 1.5
Outputs:
- output: bfloat16 [16384, 1024], P(('wide', 'narrow'))
- codes: bfloat16 [16384, 1024], P(('wide', 'narrow'))
- frames_gradient: bfloat16 [16384, 1024], P(('wide', 'narrow'))
- first_up_gradient: float32 [1024, 4096], P('narrow')
- first_down_gradient: float32 [4096, 1024], P('narrow')
- attention_in_gradient: float32 [1024, 3072], P('narrow')
- attention_out_gradient: float32 [1024, 1024], P('narrow')
- pointwise_in_gradient: float32 [1024, 2048], P('narrow')
- pointwise_out_gradient: float32 [1024, 1024], P('narrow')
- second_up_gradient: float32 [1024, 4096], P('narrow')
- second_down_gradient: float32 [4096, 1024], P('narrow')
- quantizer_in_gradient: float32 [1024, 1024], P('narrow')
- codebook_gradient: float32 [1024, 1024], P('narrow')
- norm_gains_gradient: float32 [6, 1024], P(None, 'narrow')
- depthwise_kernel_gradient: float32 [5, 1024], P(None, 'narrow')
- batch_affine_gradient: float32 [2, 1024], P(None, 'narrow')
Inputs may be any that keep to these rules, and one draw needn't show every extreme that they name: `utterance_durations`: each entry is 0 (an empty slot) or 64, 128 or 256; in each row the nonempty slots come first and sum to at most 512; in every draw some row sums to exactly 512 and holds an utterance of 256. `perturbation_samples`: standard Gumbel samples.
All inputs are finite; a program needn't handle non-finite values.
Results may differ from a plain program's by a relative error of at most 0.024.
Values may be sent and summed in bfloat16 or wider, within the bound.
A program may use at most 320 MiB of HBM per device.

v0:
```python
import jax
import jax.numpy as jnp
from jax import lax
from jax.sharding import PartitionSpec as P

HEADS = 8


EPSILON = 1e-05
NEGATIVE = -1e30


def split_up(shard, dim, peers):
    before, after = (shard.shape[:dim], shard.shape[dim + 1 :])
    return jnp.moveaxis(shard.reshape(*before, peers, -1, *after), dim, 0)


def summed_on_arrival(shard, axis, dim):
    pieces = split_up(shard, dim, lax.axis_size(axis))
    arrived = lax.all_to_all(pieces, axis, split_axis=0, concat_axis=0, tiled=True)
    return arrived.astype(jnp.float32).sum(axis=0)


def matmul(left, right):
    return jnp.dot(left, right, preferred_element_type=jnp.float32)


def across_rows(left, right):
    return lax.dot_general(
        left, right, (((0,), (0,)), ((), ())), preferred_element_type=jnp.float32
    )


def against(left, right):
    return lax.dot_general(
        left, right, (((1,), (1,)), ((), ())), preferred_element_type=jnp.float32
    )


def swish_slope(values):
    sigmoid = jax.nn.sigmoid(values)
    return sigmoid * (1.0 + values * (1.0 - sigmoid))


def layer_norm(values, gain):
    centred = values - jnp.mean(values, axis=-1, keepdims=True)
    scale = lax.rsqrt(jnp.mean(centred * centred, axis=-1, keepdims=True) + EPSILON)
    normed = centred * scale
    return (normed * gain, normed, scale)


def norm_back(adjoint_out, normed, scale, gain):
    adjoint_normed = adjoint_out * gain
    gain_sum = jnp.sum(adjoint_out * normed, axis=0)
    adjoint_in = scale * (
        adjoint_normed
        - jnp.mean(adjoint_normed, axis=-1, keepdims=True)
        - normed * jnp.mean(adjoint_normed * normed, axis=-1, keepdims=True)
    )
    return (adjoint_in, gain_sum)


def shift_rows(values, offset, fill):
    if offset == 0:
        return values
    padding = jnp.full((abs(offset),) + values.shape[1:], fill, values.dtype)
    if offset > 0:
        return jnp.concatenate([values[offset:], padding], axis=0)
    return jnp.concatenate([padding, values[:offset]], axis=0)


def depthwise(values, kernel, segment):
    taps = kernel.shape[0]
    total = jnp.zeros_like(values)
    for tap_index in range(taps):
        offset = tap_index - taps // 2
        same_segment = (shift_rows(segment, offset, -1) == segment).astype(jnp.float32)[:, None]
        total = total + kernel[tap_index] * shift_rows(values, offset, 0.0) * same_segment
    return total


def depthwise_back(adjoint, values, kernel, segment):
    taps = kernel.shape[0]
    adjoint_values = jnp.zeros_like(values)
    kernel_rows = []
    for tap_index in range(taps):
        offset = tap_index - taps // 2
        same_segment = (shift_rows(segment, offset, -1) == segment).astype(jnp.float32)[:, None]
        masked = adjoint * same_segment
        kernel_rows.append(jnp.sum(masked * shift_rows(values, offset, 0.0), axis=0))
        adjoint_values = adjoint_values + shift_rows(masked * kernel[tap_index], -offset, 0.0)
    return (adjoint_values, jnp.stack(kernel_rows))


def unpack_small(gathered, count):
    parts = gathered.shape[0]
    breadth = gathered.shape[1] // count
    unfolded = jnp.transpose(gathered.reshape(parts, count, breadth), (1, 0, 2))
    return unfolded.reshape(count, parts * breadth).astype(jnp.float32)


def fetch(first, second, small):
    whole = (
        lax.all_gather(first, "narrow", axis=0, tiled=True),
        lax.all_gather(second, "narrow", axis=0, tiled=True),
        lax.all_gather(small.reshape(1, -1), "narrow", axis=0, tiled=True),
    )
    return (whole[0], whole[1], unpack_small(whole[2], small.shape[0]))


def fetch_again(first, second, small):
    whole = (
        lax.all_gather(first, "narrow", axis=0, tiled=True),
        lax.all_gather(second, "narrow", axis=0, tiled=True),
        lax.all_gather(small.reshape(1, -1), "narrow", axis=0, tiled=True),
    )
    return (whole[0], whole[1], unpack_small(whole[2], small.shape[0]))


def again(first, second, small):
    return fetch_again(first, second, small)


def fold_small(full):
    parts = lax.axis_size("narrow")
    count = full.shape[0]
    breadth = full.shape[1] // parts
    return jnp.transpose(full.reshape(count, parts, breadth), (1, 0, 2)).reshape(
        parts, count * breadth
    )


def reduce_sums(first, second, small):
    folded = fold_small(small)
    spread_out = (
        lax.psum_scatter(
            first.astype(jnp.bfloat16), "narrow", scatter_dimension=0, tiled=True
        ).astype(jnp.float32),
        lax.psum_scatter(
            second.astype(jnp.bfloat16), "narrow", scatter_dimension=0, tiled=True
        ).astype(jnp.float32),
        lax.psum_scatter(
            folded.astype(jnp.bfloat16), "narrow", scatter_dimension=0, tiled=True
        ).astype(jnp.float32),
    )
    shares = (
        summed_on_arrival(spread_out[0].astype(jnp.bfloat16), "wide", 1),
        summed_on_arrival(spread_out[1].astype(jnp.bfloat16), "wide", 1),
        summed_on_arrival(spread_out[2].astype(jnp.bfloat16), "wide", 1),
    )
    whole = (
        lax.all_gather(shares[0].astype(jnp.bfloat16), "wide", axis=1, tiled=True).astype(
            jnp.float32
        ),
        lax.all_gather(shares[1].astype(jnp.bfloat16), "wide", axis=1, tiled=True).astype(
            jnp.float32
        ),
        lax.all_gather(shares[2].astype(jnp.bfloat16), "wide", axis=1, tiled=True).astype(
            jnp.float32
        ),
    )
    replicas = float(lax.axis_size("wide"))
    return (
        whole[0] / replicas,
        whole[1] / replicas,
        whole[2].reshape(small.shape[0], -1) / replicas,
    )


def feed_forward(values, weight_in, weight_out, gain):
    normed, normal_hat, scale = layer_norm(values, gain)
    entry = normed.astype(jnp.bfloat16)
    before = matmul(entry, weight_in)
    active = (before * jax.nn.sigmoid(before)).astype(jnp.bfloat16)
    branch = matmul(active, weight_out)
    return (values + 0.5 * branch, (entry, normal_hat, scale, before, active))


def feed_back(adjoint, kept, weight_in, weight_out, gain):
    entry, normal_hat, scale, before, active = kept
    adjoint_branch = (0.5 * adjoint).astype(jnp.bfloat16)
    out_sum = across_rows(active, adjoint_branch)
    adjoint_before = (against(adjoint_branch, weight_out) * swish_slope(before)).astype(
        jnp.bfloat16
    )
    in_sum = across_rows(entry, adjoint_before)
    adjoint_values, gain_sum = norm_back(
        against(adjoint_before, weight_in), normal_hat, scale, gain
    )
    return (adjoint + adjoint_values, in_sum, out_sum, gain_sum)


def masked_scores(query_block, segment_block, keys, segment, factor):
    scores = (
        jnp.einsum("ihd,jhd->hij", query_block, keys, preferred_element_type=jnp.float32) * factor
    )
    allowed = segment_block[:, None] == segment[None, :]
    return jnp.where(allowed[None], scores, NEGATIVE)


def attention_forward(values, weight_in, weight_out, gain, segment, heads):
    normed, normal_hat, scale = layer_norm(values, gain)
    entry = normed.astype(jnp.bfloat16)
    mixed = matmul(entry, weight_in).astype(jnp.bfloat16)
    row_count, width = values.shape
    head_dim = width // heads
    block = min(512, row_count)
    blocks = row_count // block
    queries = mixed[:, :width].reshape(blocks, block, heads, head_dim)
    keys = mixed[:, width : 2 * width].reshape(row_count, heads, head_dim)
    head_values = mixed[:, 2 * width :].reshape(row_count, heads, head_dim)
    segment_blocks = segment.reshape(blocks, block)
    factor = head_dim ** (-0.5)

    def attend(pieces):
        query_block, segment_block = pieces
        scores = masked_scores(query_block, segment_block, keys, segment, factor)
        top = jnp.max(scores, axis=-1, keepdims=True)
        exponent = jnp.exp(scores - top)
        total = jnp.sum(exponent, axis=-1, keepdims=True)
        weights = (exponent / total).astype(jnp.bfloat16)
        result = jnp.einsum(
            "hij,jhd->ihd", weights, head_values, preferred_element_type=jnp.float32
        )
        return (result.astype(jnp.bfloat16), (top + jnp.log(total))[..., 0])

    outputs, log_totals = lax.map(attend, (queries, segment_blocks))
    heads_out = outputs.reshape(row_count, width)
    branch = matmul(heads_out, weight_out)
    kept = (
        entry,
        normal_hat,
        scale,
        queries,
        keys,
        head_values,
        segment_blocks,
        log_totals,
        heads_out,
    )
    return (values + branch, kept)


def attention_back(adjoint, kept, weight_in, weight_out, gain, segment, heads):
    entry, normal_hat, scale, queries, keys, head_values, segment_blocks, log_totals, heads_out = (
        kept
    )
    row_count, width = adjoint.shape
    blocks = queries.shape[0]
    block = queries.shape[1]
    head_dim = width // heads
    factor = head_dim ** (-0.5)
    adjoint_branch = adjoint.astype(jnp.bfloat16)
    out_sum = across_rows(heads_out, adjoint_branch)
    adjoint_heads = (
        against(adjoint_branch, weight_out)
        .astype(jnp.bfloat16)
        .reshape(blocks, block, heads, head_dim)
    )

    def step_back(carry, pieces):
        key_sum, value_sum = carry
        query_block, segment_block, log_block, adjoint_block = pieces
        scores = masked_scores(query_block, segment_block, keys, segment, factor)
        weights = jnp.exp(scores - log_block[..., None])
        value_sum = value_sum + jnp.einsum(
            "hij,ihd->jhd",
            weights.astype(jnp.bfloat16),
            adjoint_block,
            preferred_element_type=jnp.float32,
        )
        adjoint_weights = jnp.einsum(
            "ihd,jhd->hij", adjoint_block, head_values, preferred_element_type=jnp.float32
        )
        adjoint_scores = (
            weights * (adjoint_weights - jnp.sum(weights * adjoint_weights, axis=-1, keepdims=True))
        ).astype(jnp.bfloat16)
        query_adjoint = (
            jnp.einsum("hij,jhd->ihd", adjoint_scores, keys, preferred_element_type=jnp.float32)
            * factor
        )
        key_sum = (
            key_sum
            + jnp.einsum(
                "hij,ihd->jhd", adjoint_scores, query_block, preferred_element_type=jnp.float32
            )
            * factor
        )
        return ((key_sum, value_sum), query_adjoint)

    zeros = jnp.zeros((row_count, heads, head_dim), jnp.float32)
    sums, query_adjoints = lax.scan(
        step_back, (zeros, zeros), (queries, segment_blocks, log_totals, adjoint_heads)
    )
    adjoint_mixed = jnp.concatenate(
        [
            query_adjoints.reshape(row_count, width),
            sums[0].reshape(row_count, width),
            sums[1].reshape(row_count, width),
        ],
        axis=1,
    ).astype(jnp.bfloat16)
    in_sum = across_rows(entry, adjoint_mixed)
    adjoint_values, gain_sum = norm_back(against(adjoint_mixed, weight_in), normal_hat, scale, gain)
    return (adjoint + adjoint_values, in_sum, out_sum, gain_sum)


def convolution_forward(values, weight_in, weight_out, small, segment, valid):
    taps = small.shape[0] - 3
    normed, normal_hat, scale = layer_norm(values, small[0])
    entry = normed.astype(jnp.bfloat16)
    gates = matmul(entry, weight_in)
    width = values.shape[1]
    sigmoid_right = jax.nn.sigmoid(gates[:, width:])
    gated = gates[:, :width] * sigmoid_right
    convolved = depthwise(gated, small[1 : 1 + taps], segment)
    local_count = jnp.sum(valid)
    total, count = lax.psum((jnp.sum(convolved * valid, axis=0), local_count), ("wide", "narrow"))
    mean = total / count
    centred = convolved - mean
    spread = lax.psum(jnp.sum(centred * centred * valid, axis=0), ("wide", "narrow")) / count
    inverse = lax.rsqrt(spread + EPSILON)
    batch_hat = centred * inverse
    batch_out = batch_hat * small[1 + taps] + small[2 + taps]
    active = (batch_out * jax.nn.sigmoid(batch_out)).astype(jnp.bfloat16)
    branch = matmul(active, weight_out)
    kept = (
        entry,
        normal_hat,
        scale,
        gates,
        sigmoid_right,
        gated,
        batch_hat,
        batch_out,
        active,
        inverse,
        count,
    )
    return (values + branch, kept)


def convolution_back(adjoint, kept, weight_in, weight_out, small, segment, valid):
    (
        entry,
        normal_hat,
        scale,
        gates,
        sigmoid_right,
        gated,
        batch_hat,
        batch_out,
        active,
        inverse,
        count,
    ) = kept
    taps = small.shape[0] - 3
    width = adjoint.shape[1]
    adjoint_branch = adjoint.astype(jnp.bfloat16)
    out_sum = across_rows(active, adjoint_branch)
    adjoint_batch = against(adjoint_branch, weight_out) * swish_slope(batch_out)
    shift_sum = jnp.sum(adjoint_batch, axis=0)
    batch_gain_sum = jnp.sum(adjoint_batch * batch_hat, axis=0)
    adjoint_hat = adjoint_batch * small[1 + taps]
    first_total, second_total = lax.psum(
        (jnp.sum(adjoint_hat * valid, axis=0), jnp.sum(adjoint_hat * batch_hat * valid, axis=0)),
        ("wide", "narrow"),
    )
    adjoint_conv = inverse * (
        adjoint_hat - valid * (first_total + batch_hat * second_total) / count
    )
    adjoint_gated, kernel_sum = depthwise_back(adjoint_conv, gated, small[1 : 1 + taps], segment)
    left_half = gates[:, :width]
    adjoint_gates = jnp.concatenate(
        [
            adjoint_gated * sigmoid_right,
            adjoint_gated * left_half * sigmoid_right * (1.0 - sigmoid_right),
        ],
        axis=1,
    ).astype(jnp.bfloat16)
    in_sum = across_rows(entry, adjoint_gates)
    adjoint_values, gain_sum = norm_back(
        against(adjoint_gates, weight_in), normal_hat, scale, small[0]
    )
    small_sum = jnp.concatenate(
        [gain_sum[None], kernel_sum, batch_gain_sum[None], shift_sum[None]], axis=0
    )
    return (adjoint + adjoint_values, in_sum, out_sum, small_sum)


def per_device(
    acoustic_features,
    utterance_durations,
    perturbation_samples,
    annealing_level,
    result_cotangent,
    quantized_cotangent,
    early_expanding_projector,
    early_contracting_projector,
    query_key_value_projector,
    heads_merging_projector,
    gated_channel_projector,
    closing_channel_projector,
    later_expanding_projector,
    later_contracting_projector,
    vocabulary_affinity_projector,
    vocabulary_vectors,
    normalizer_gains,
    channelwise_kernel_weights,
    normalizer_affine_rows,
):
    row_count = acoustic_features.shape[0]
    positions = lax.broadcasted_iota(jnp.int32, (row_count, 1), 0)
    slot_ends = jnp.cumsum(utterance_durations[0])
    segment = jnp.sum((positions >= slot_ends[None, :]).astype(jnp.int32), axis=1)
    valid = (positions < slot_ends[-1]).astype(jnp.float32)
    inputs = acoustic_features.astype(jnp.float32)
    taps = channelwise_kernel_weights.shape[0]
    conv_small = jnp.concatenate(
        [normalizer_gains[3:4], channelwise_kernel_weights, normalizer_affine_rows], axis=0
    )
    quantizer_weights = fetch(
        vocabulary_affinity_projector, vocabulary_vectors, normalizer_gains[0:1]
    )
    quantizer_normed, quantizer_hat, quantizer_scale = layer_norm(inputs, quantizer_weights[2][0])
    quantizer_entry = quantizer_normed.astype(jnp.bfloat16)
    vocabulary_affinity = matmul(quantizer_entry, quantizer_weights[0])
    code_probabilities = jax.nn.softmax(
        (vocabulary_affinity + perturbation_samples.astype(jnp.float32)) / annealing_level[0],
        axis=-1,
    )
    chances_low = code_probabilities.astype(jnp.bfloat16)
    codes = matmul(chances_low, quantizer_weights[1]).astype(jnp.bfloat16)
    first_weights = fetch(
        early_expanding_projector, early_contracting_projector, normalizer_gains[1:2]
    )
    after_first, first_kept = feed_forward(
        inputs, first_weights[0], first_weights[1], first_weights[2][0]
    )
    attend_weights = fetch(
        query_key_value_projector, heads_merging_projector, normalizer_gains[2:3]
    )
    after_attention, attend_kept = attention_forward(
        after_first, attend_weights[0], attend_weights[1], attend_weights[2][0], segment, HEADS
    )
    conv_weights = fetch(gated_channel_projector, closing_channel_projector, conv_small)
    after_conv, conv_kept = convolution_forward(
        after_attention, conv_weights[0], conv_weights[1], conv_weights[2], segment, valid
    )
    second_weights = fetch(
        later_expanding_projector, later_contracting_projector, normalizer_gains[4:6]
    )
    after_second, second_kept = feed_forward(
        after_conv, second_weights[0], second_weights[1], second_weights[2][0]
    )
    final_out, final_hat, final_scale = layer_norm(after_second, second_weights[2][1])
    output = final_out.astype(jnp.bfloat16)
    adjoint_output = result_cotangent.astype(jnp.float32) * valid
    adjoint_codes = quantized_cotangent * valid.astype(jnp.bfloat16)
    adjoint, final_gain_sum = norm_back(
        adjoint_output, final_hat, final_scale, second_weights[2][1]
    )
    weights_now = again(
        later_expanding_projector, later_contracting_projector, normalizer_gains[4:6]
    )
    adjoint, up_sum, down_sum, gain_sum = feed_back(
        adjoint, second_kept, weights_now[0], weights_now[1], weights_now[2][0]
    )
    second_up_gradient, second_down_gradient, second_small = reduce_sums(
        up_sum, down_sum, jnp.stack([gain_sum, final_gain_sum])
    )
    weights_now = again(gated_channel_projector, closing_channel_projector, conv_small)
    adjoint, in_sum, out_sum, small_sum = convolution_back(
        adjoint, conv_kept, weights_now[0], weights_now[1], weights_now[2], segment, valid
    )
    pointwise_in_gradient, pointwise_out_gradient, conv_small_gradient = reduce_sums(
        in_sum, out_sum, small_sum
    )
    weights_now = again(query_key_value_projector, heads_merging_projector, normalizer_gains[2:3])
    adjoint, in_sum, out_sum, gain_sum = attention_back(
        adjoint, attend_kept, weights_now[0], weights_now[1], weights_now[2][0], segment, HEADS
    )
    attention_in_gradient, attention_out_gradient, attend_small = reduce_sums(
        in_sum, out_sum, gain_sum[None]
    )
    weights_now = again(
        early_expanding_projector, early_contracting_projector, normalizer_gains[1:2]
    )
    adjoint, up_sum, down_sum, gain_sum = feed_back(
        adjoint, first_kept, weights_now[0], weights_now[1], weights_now[2][0]
    )
    first_up_gradient, first_down_gradient, first_small = reduce_sums(
        up_sum, down_sum, gain_sum[None]
    )
    weights_now = again(vocabulary_affinity_projector, vocabulary_vectors, normalizer_gains[0:1])
    book_sum = across_rows(chances_low, adjoint_codes)
    adjoint_chances = against(adjoint_codes, weights_now[1])
    adjoint_logits = (
        code_probabilities
        * (adjoint_chances - jnp.sum(code_probabilities * adjoint_chances, axis=-1, keepdims=True))
        / annealing_level[0]
    ).astype(jnp.bfloat16)
    projection_sum = across_rows(quantizer_entry, adjoint_logits)
    adjoint_inputs, quantizer_gain_sum = norm_back(
        against(adjoint_logits, weights_now[0]), quantizer_hat, quantizer_scale, weights_now[2][0]
    )
    frames_gradient = (adjoint + adjoint_inputs).astype(jnp.bfloat16)
    quantizer_in_gradient, codebook_gradient, quantizer_small = reduce_sums(
        projection_sum, book_sum, quantizer_gain_sum[None]
    )
    norm_gains_gradient = jnp.concatenate(
        [quantizer_small, first_small, attend_small, conv_small_gradient[0:1], second_small], axis=0
    )
    depthwise_kernel_gradient = conv_small_gradient[1 : 1 + taps]
    batch_affine_gradient = conv_small_gradient[1 + taps :]
    return (
        output,
        codes,
        frames_gradient,
        first_up_gradient,
        first_down_gradient,
        attention_in_gradient,
        attention_out_gradient,
        pointwise_in_gradient,
        pointwise_out_gradient,
        second_up_gradient,
        second_down_gradient,
        quantizer_in_gradient,
        codebook_gradient,
        norm_gains_gradient,
        depthwise_kernel_gradient,
        batch_affine_gradient,
    )


def solution(mesh):
    in_specs = (
        P(("wide", "narrow"), None),
        P(("wide", "narrow"), None),
        P(("wide", "narrow"), None),
        P(),
        P(("wide", "narrow"), None),
        P(("wide", "narrow"), None),
        P("narrow", None),
        P("narrow", None),
        P("narrow", None),
        P("narrow", None),
        P("narrow", None),
        P("narrow", None),
        P("narrow", None),
        P("narrow", None),
        P("narrow", None),
        P("narrow", None),
        P(None, "narrow"),
        P(None, "narrow"),
        P(None, "narrow"),
    )
    out_specs = (
        P(("wide", "narrow"), None),
        P(("wide", "narrow"), None),
        P(("wide", "narrow"), None),
        P("narrow", None),
        P("narrow", None),
        P("narrow", None),
        P("narrow", None),
        P("narrow", None),
        P("narrow", None),
        P("narrow", None),
        P("narrow", None),
        P("narrow", None),
        P("narrow", None),
        P(None, "narrow"),
        P(None, "narrow"),
        P(None, "narrow"),
    )
    return jax.shard_map(
        per_device, mesh=mesh, in_specs=in_specs, out_specs=out_specs, check_vma=False
    )
```

profile of v0, /device:TPU:0, one launch (start us, length us, event | category | flops | bytes accessed | tf_op | source)
XLA Modules:
  0.0 1316.0 jit_solution(1563185119006189986)
XLA Ops:
  14.8 6.0 all-gather.9
  22.8 12.0 all-gather.44.cloned.1.call-done
  38.6 20.4 %all-gather.46.cloned.1.call-done = bf16[1024,1024]{1,0:T(8,128)(2,1)} async-done(((bf16[256,1024]{1,0:T(8,128)(2,1)}), bf16[1024,1024]{1,0:T(8,128)(2,1)}) %all-gather.46.cloned.1.call-update) | async-done | bytes 2097168 | tf_op jit(solution)/shard_map/all_gather | solution.py:105
  66.8 5.1 all-gather.5
  71.9 5.2 all-gather.6
  77.2 5.5 all-gather.7
  82.8 5.4 all-gather.8
  95.3 23.8 %all-gather.28.cloned.1.call-done = bf16[1024,4096]{1,0:T(8,128)(2,1)} async-done(((bf16[256,4096]{1,0:T(8,128)(2,1)}), bf16[1024,4096]{1,0:T(8,128)(2,1)}) %all-gather.28.cloned.1.call-update) | async-done | bytes 8388624 | tf_op jit(solution)/shard_map/all_gather | solution.py:104
  119.1 10.5 fusion.80
  129.6 49.2 %all-gather.30.cloned.1.call-done = bf16[4096,1024]{1,0:T(8,128)(2,1)} async-done(((bf16[1024,1024]{1,0:T(8,128)(2,1)}), bf16[4096,1024]{1,0:T(8,128)(2,1)}) %all-gather.30.cloned.1.call-update) | async-done | bytes 8388624 | tf_op jit(solution)/shard_map/all_gather | solution.py:105
  178.8 9.6 fusion.92
  188.9 37.8 %all-gather.32.cloned.1.call-done = bf16[1024,3072]{1,0:T(8,128)(2,1)} async-done(((bf16[256,3072]{1,0:T(8,128)(2,1)}), bf16[1024,3072]{1,0:T(8,128)(2,1)}) %all-gather.32.cloned.1.call-update) | async-done | bytes 6291472 | tf_op jit(solution)/shard_map/all_gather | solution.py:104
  226.6 6.6 convolution_convert_fusion.5
  244.3 6.3 all-gather.34.cloned.1.call-done
  255.3 31.4 %all-gather.36.cloned.1.call-done = bf16[1024,2048]{1,0:T(8,128)(2,1)} async-done(((bf16[256,2048]{1,0:T(8,128)(2,1)}), bf16[1024,2048]{1,0:T(8,128)(2,1)}) %all-gather.36.cloned.1.call-update) | async-done | bytes 4194320 | tf_op jit(solution)/shard_map/all_gather | solution.py:104
  286.7 5.3 fusion.82
  297.7 40.3 %all-reduce.20 = (f32[1024]{0:T(1024)S(1)}, f32[]{:T(128)}) all-reduce(f32[1024]{0:T(1024)S(1)} %get-tuple-element.122, f32[]{:T(128)} %fusion.59), channel_id=1, replica_groups=mesh['wide'=8,'narrow'=4] {'wide','narrow'}, use_global_device_ids=true, to_apply=%region_11.12 | all-reduce | flops 1025 | bytes 8200 | tf_op jit(solution)/shard_map/psum | solution.py:318
  339.0 42.2 %psum.37 = f32[1024]{0:T(1024)S(1)} all-reduce(f32[1024]{0:T(1024)S(1)} %multiply_reduce_fusion.20), channel_id=1, replica_groups=mesh['wide'=8,'narrow'=4] {'wide','narrow'}, use_global_device_ids=true, to_apply=%region_15.16 | all-reduce | flops 1024 | bytes 8192 | tf_op jit(solution)/shard_map/psum | solution.py:321
  381.9 4.4 fusion.95
  388.0 11.8 fusion.83
  399.8 32.6 %all-gather.42.cloned.1.call-done = bf16[4096,1024]{1,0:T(8,128)(2,1)} async-done(((bf16[1024,1024]{1,0:T(8,128)(2,1)}), bf16[4096,1024]{1,0:T(8,128)(2,1)}) %all-gather.42.cloned.1.call-update) | async-done | bytes 8388624 | tf_op jit(solution)/shard_map/all_gather | solution.py:105
  432.4 11.0 fusion.96
  446.2 12.6 multiply_convert_fusion.2
  458.8 9.4 multiply_reduce_fusion.2
  474.8 7.8 multiply_reduce_fusion.3
  482.6 40.1 %all-reduce.19 = (f32[1024]{0:T(1024)S(1)}, f32[1024]{0:T(1024)S(1)}) all-reduce(f32[1024]{0:T(1024)S(1)} %get-tuple-element.63, f32[1024]{0:T(1024)S(1)} %get-tuple-element.87), channel_id=1, replica_groups=mesh['wide'=8,'narrow'=4] {'wide','narrow'}, use_global_device_ids=true, to_apply=%region_29.30 | all-reduce | flops 2048 | bytes 16384 | tf_op jit(solution)/shard_map/psum | solution.py:365
  522.6 5.7 multiply_reduce_fusion.4
  536.4 4.5 convolution_convert_fusion.6
  541.1 6.1 multiply_reduce_fusion.9
  553.3 5.6 multiply_reduce_fusion
  567.4 8.8 convolution_convert_fusion.4
  577.4 12.0 convolution_convert_fusion
  591.0 9.6 convolution_convert_fusion.1
  601.9 8.3 multiply_reduce_fusion.10
  611.1 10.9 multiply_convert_fusion
  624.0 7.2 convolution_convert_fusion.3
  636.8 10.9 convolution_convert_fusion.2
  655.0 5.9 all-to-all-start.8
  663.2 12.2 fusion.28
  675.3 6.0 all-to-all-start.9
  681.7 12.3 all-reduce.22
  695.6 5.6 all-to-all-start.11
  702.6 5.1 all-to-all-done.11
  712.3 5.0 all-to-all-done.12
  722.0 5.0 all-to-all-done.10
  752.1 8.2 all-to-all-done.5
  760.3 6.5 all-to-all-start.4
  769.6 17.9 %all-to-all-done.4 = bf16[8,256,256]{2,1,0:T(8,128)(2,1)S(1)} async-done(((bf16[8,256,256]{2,1,0:T(8,128)(2,1)}), bf16[8,256,256]{2,1,0:T(8,128)(2,1)S(1)}, u32[]{:S(2)}, u32[]{:S(2)}) %all-to-all-start.4) | async-done | bytes 1048608 | tf_op jit(solution)/shard_map/all_to_all | solution.py:20
  788.5 10.4 all-to-all-start.2
  802.2 35.4 %all-to-all-done.2 = bf16[8,256,384]{2,1,0:T(8,128)(2,1)S(1)} async-done(((bf16[8,256,384]{2,1,0:T(8,128)(2,1)}), bf16[8,256,384]{2,1,0:T(8,128)(2,1)S(1)}, u32[]{:S(2)}, u32[]{:S(2)}) %all-to-all-start.2) | async-done | bytes 1572896 | tf_op jit(solution)/shard_map/all_to_all | solution.py:20
  838.7 5.5 all-to-all-start.7
  851.8 40.1 %all-to-all-done.7 = bf16[8,1024,128]{2,1,0:T(8,128)(2,1)S(1)} async-done(((bf16[8,1024,128]{2,1,0:T(8,128)(2,1)}), bf16[8,1024,128]{2,1,0:T(8,128)(2,1)S(1)}, u32[]{:S(2)}, u32[]{:S(2)}) %all-to-all-start.7) | async-done | bytes 2097184 | tf_op jit(solution)/shard_map/all_to_all | solution.py:20
  891.9 5.5 all-to-all-start.6
  901.6 44.9 %all-to-all-done.6 = bf16[8,256,512]{2,1,0:T(8,128)(2,1)} async-done(((bf16[8,256,512]{2,1,0:T(8,128)(2,1)}), bf16[8,256,512]{2,1,0:T(8,128)(2,1)}, u32[]{:S(2)}, u32[]{:S(2)}) %all-to-all-start.6) | async-done | bytes 2097184 | tf_op jit(solution)/shard_map/all_to_all | solution.py:20
  946.5 5.5 all-to-all-start
  956.7 4.5 convolution_convert_fusion.12
  963.5 43.2 %all_gather.128 = bf16[256,1024]{1,0:T(8,128)(2,1)} all-gather(bf16[256,128]{1,0:T(8,128)(2,1)S(1)} %reduce_sum.645), channel_id=1, replica_groups=mesh['wide'=8,'narrow'=4] {'wide'}, dimensions={1}, use_global_device_ids=true | all-gather | bytes 589824 | tf_op jit(solution)/shard_map/all_gather | solution.py:152
  1012.9 50.5 %all_gather.129 = bf16[256,1024]{1,0:T(8,128)(2,1)S(1)} all-gather(bf16[256,128]{1,0:T(8,128)(2,1)S(1)} %reduce_sum.646), channel_id=1, replica_groups=mesh['wide'=8,'narrow'=4] {'wide'}, dimensions={1}, use_global_device_ids=true | all-gather | bytes 589824 | tf_op jit(solution)/shard_map/all_gather | solution.py:155
  1080.0 32.7 %all-reduce.21 = (bf16[256]{0:T(256)(128)(2,1)S(1)}, bf16[256]{0:T(256)(128)(2,1)S(1)}, bf16[256]{0:T(256)(128)(2,1)S(1)}, bf16[512]{0:T(512)(128)(2,1)S(1)}) all-reduce(bf16[256]{0:T(256)(128)(2,1)S(1)} %dynamic-update-slice, bf16[256]{0:T(256)(128)(2,1)S(1)} %dynamic-update-slice.1, ...), channel_id=2, replica_groups=mesh['wide'=8,'narrow'=4] {'wide'}, use_global_device_ids=true, to_apply=%add.10 | all-reduce | flops 1280 | bytes 5120
  1112.9 28.9 %all-gather.10 = bf16[8,1,256]{2,1,0:T(2,128)(2,1)S(1)} all-gather(bf16[1,1,256]{2,1,0:T(2,128)(2,1)S(1)} %reshape.501), channel_id=5, replica_groups=mesh['wide'=8,'narrow'=4] {'wide'}, dimensions={0}, use_global_device_ids=true | all-gather | bytes 4608 | tf_op jit(solution)/shard_map/all_gather | solution.py:158
  1145.9 28.0 %all_gather.125 = bf16[256,1024]{1,0:T(8,128)(2,1)S(1)} all-gather(bf16[256,128]{1,0:T(8,128)(2,1)S(1)} %reduce_sum.642), channel_id=1, replica_groups=mesh['wide'=8,'narrow'=4] {'wide'}, dimensions={1}, use_global_device_ids=true | all-gather | bytes 589824 | tf_op jit(solution)/shard_map/all_gather | solution.py:155
  1173.9 29.3 %all_gather.123 = bf16[256,1024]{1,0:T(8,128)(2,1)S(1)} all-gather(bf16[256,128]{1,0:T(8,128)(2,1)S(1)} %reduce_sum.640), channel_id=1, replica_groups=mesh['wide'=8,'narrow'=4] {'wide'}, dimensions={1}, use_global_device_ids=true | all-gather | bytes 589824 | tf_op jit(solution)/shard_map/all_gather | solution.py:155
  1221.1 32.7 %all-gather.48.cloned.1.call-done = bf16[256,4096]{1,0:T(8,128)(2,1)} async-done(((bf16[256,512]{1,0:T(8,128)(2,1)}), bf16[256,4096]{1,0:T(8,128)(2,1)}) %all-gather.48.cloned.1.call-update) | async-done | bytes 2097168 | tf_op jit(solution)/shard_map/all_gather | solution.py:152
  1257.9 46.9 %all-gather.50.cloned.1.call-done = bf16[1024,1024]{1,0:T(8,128)(2,1)} async-done(((bf16[1024,128]{1,0:T(8,128)(2,1)}), bf16[1024,1024]{1,0:T(8,128)(2,1)}) %all-gather.50.cloned.1.call-update) | async-done | bytes 2097168 | tf_op jit(solution)/shard_map/all_gather | solution.py:155
  (447 shorter events, 222.3 us)
Async XLA Ops:
  7.2 27.7 %all-gather.44.cloned.1.call-start = ((), (), s32[]{:S(2)}) async-start(), calls=%async_computation.33 | async-start | bytes 2621440 | tf_op jit(solution)/shard_map/all_gather | solution.py:104
  7.9 51.1 %all-gather.46.cloned.1.call-start = ((), (), s32[]{:S(2)}) async-start(), calls=%async_computation.34 | async-start | bytes 2621440 | tf_op jit(solution)/shard_map/all_gather | solution.py:105
  8.7 110.5 %all-gather.28.cloned.1.call-start = ((), (), s32[]{:S(2)}) async-start(), calls=%async_computation.25 | async-start | bytes 10485760 | tf_op jit(solution)/shard_map/all_gather | solution.py:104
  9.4 169.4 %all-gather.30.cloned.1.call-start = ((), (), s32[]{:S(2)}) async-start(), calls=%async_computation.26 | async-start | bytes 10485760 | tf_op jit(solution)/shard_map/all_gather | solution.py:105
  10.0 216.7 %all-gather.32.cloned.1.call-start = ((), (), s32[]{:S(2)}) async-start(), calls=%async_computation.27 | async-start | bytes 7864320 | tf_op jit(solution)/shard_map/all_gather | solution.py:104
  10.6 240.1 %all-gather.34.cloned.1.call-start = ((), (), s32[]{:S(2)}) async-start(), calls=%async_computation.28 | async-start | bytes 2621440 | tf_op jit(solution)/shard_map/all_gather | solution.py:105
  11.1 275.6 %all-gather.36.cloned.1.call-start = ((), (), s32[]{:S(2)}) async-start(), calls=%async_computation.29 | async-start | bytes 5242880 | tf_op jit(solution)/shard_map/all_gather | solution.py:104
  11.9 370.0 %all-gather.38.cloned.1.call-start = ((), (), s32[]{:S(2)}) async-start(), calls=%async_computation.30 | async-start | bytes 2621440 | tf_op jit(solution)/shard_map/all_gather | solution.py:105
  12.7 375.3 %all-gather.40.cloned.1.call-start = ((), (), s32[]{:S(2)}) async-start(), calls=%async_computation.31 | async-start | bytes 10485760 | tf_op jit(solution)/shard_map/all_gather | solution.py:104
  13.4 419.0 %all-gather.42.cloned.1.call-start = ((), (), s32[]{:S(2)}) async-start(), calls=%async_computation.32 | async-start | bytes 10485760 | tf_op jit(solution)/shard_map/all_gather | solution.py:105
  14.0 639.1 %reduce-scatter.27.cloned.1.call-start = ((), (), s32[]{:S(2)}) async-start(), calls=%async_computation.49 | async-start | bytes 2621440 | tf_op jit(solution)/shard_map/reduce_scatter | solution.py:136
  20.8 42.2 %copy-start.55 = (f32[4,1,256]{2,1,0:T(1,128)}, f32[4,1,256]{2,1,0:T(1,128)S(1)}, u32[]{:S(2)}) copy-start(f32[4,1,256]{2,1,0:T(1,128)S(1)} %convert_element_type.468) | copy-start | bytes 12292
  22.4 96.7 %copy-start.53 = (f32[512]{0:T(512)}, f32[512]{0:T(512)S(1)}, u32[]{:S(2)}) copy-start(f32[512]{0:T(512)S(1)} %broadcast_multiply_fusion.20) | copy-start | bytes 6148
  22.8 96.3 %copy-start.73 = (f32[512]{0:T(512)}, f32[512]{0:T(512)S(1)}, u32[]{:S(2)}) copy-start(f32[512]{0:T(512)S(1)} %add_rsqrt_fusion.5) | copy-start | bytes 6148
  38.1 52.5 %copy-start.32 = (f32[512,1024]{1,0:T(8,128)}, f32[512,1024]{1,0:T(8,128)S(1)}, u32[]{:S(2)}) copy-start(f32[512,1024]{1,0:T(8,128)S(1)} %get-tuple-element.173) | copy-start | bytes 6291460
  38.1 52.5 %copy-start.69 = (f32[512]{0:T(512)}, f32[512]{0:T(512)S(1)}, u32[]{:S(2)}) copy-start(f32[512]{0:T(512)S(1)} %get-tuple-element.172) | copy-start | bytes 6148
  38.6 52.1 %copy-start.71 = (f32[512]{0:T(512)}, f32[512]{0:T(512)S(1)}, u32[]{:S(2)}) copy-start(f32[512]{0:T(512)S(1)} %fusion.36) | copy-start | bytes 6148
  66.8 594.2 %reduce-scatter.29.cloned.1.call-start = ((), (), s32[]{:S(2)}) async-start(), calls=%async_computation.50 | async-start | bytes 2621440 | tf_op jit(solution)/shard_map/reduce_scatter | solution.py:139
  71.9 47.2 %copy-start.57 = (f32[4,1,256]{2,1,0:T(1,128)}, f32[4,1,256]{2,1,0:T(1,128)S(1)}, u32[]{:S(2)}) copy-start(f32[4,1,256]{2,1,0:T(1,128)S(1)} %convert_element_type.466) | copy-start | bytes 12292
  77.1 149.5 %copy-start.59 = (f32[4,1,256]{2,1,0:T(1,128)}, f32[4,1,256]{2,1,0:T(1,128)S(1)}, u32[]{:S(2)}) copy-start(f32[4,1,256]{2,1,0:T(1,128)S(1)} %convert_element_type.467) | copy-start | bytes 12292
  94.8 645.2 %reduce-scatter.21.cloned.1.call-start = ((), (), s32[]{:S(2)}) async-start(), calls=%async_computation.44 | async-start | bytes 2621440 | tf_op jit(solution)/shard_map/reduce_scatter | solution.py:139
  188.5 44.8 %copy-start.22 = (f32[512,1024]{1,0:T(8,128)}, f32[512,1024]{1,0:T(8,128)S(1)}, u32[]{:S(2)}) copy-start(f32[512,1024]{1,0:T(8,128)S(1)} %get-tuple-element.162) | copy-start | bytes 6291460
  188.5 44.8 %copy-start.51 = (f32[512]{0:T(512)}, f32[512]{0:T(512)S(1)}, u32[]{:S(2)}) copy-start(f32[512]{0:T(512)S(1)} %broadcast_multiply_fusion.19) | copy-start | bytes 6148
  188.8 44.4 %copy-start.62 = (f32[512]{0:T(512)}, f32[512]{0:T(512)S(1)}, u32[]{:S(2)}) copy-start(f32[512]{0:T(512)S(1)} %add_rsqrt_fusion.4) | copy-start | bytes 6148
  297.7 88.6 %copy-start.3 = (f32[512,1024]{1,0:T(8,128)}, f32[512,1024]{1,0:T(8,128)S(1)}, u32[]{:S(2)}) copy-start(f32[512,1024]{1,0:T(8,128)S(1)} %get-tuple-element.123) | copy-start | bytes 6291460
  474.7 275.2 %reduce-scatter.19.cloned.1.call-start = ((), (), s32[]{:S(2)}) async-start(), calls=%async_computation.42 | async-start | bytes 5242880 | tf_op jit(solution)/shard_map/reduce_scatter | solution.py:136
  541.0 225.9 %reduce-scatter.15.cloned.1.call-start = ((), (), s32[]{:S(2)}) async-start(), calls=%async_computation.39 | async-start | bytes 7864320 | tf_op jit(solution)/shard_map/reduce_scatter | solution.py:136
  576.2 222.7 %reduce-scatter.25.cloned.1.call-start = ((), (), s32[]{:S(2)}) async-start(), calls=%async_computation.47 | async-start | bytes 10485760 | tf_op jit(solution)/shard_map/reduce_scatter | solution.py:139
  589.4 259.3 %reduce-scatter.23.cloned.1.call-start = ((), (), s32[]{:S(2)}) async-start(), calls=%async_computation.45 | async-start | bytes 10485760 | tf_op jit(solution)/shard_map/reduce_scatter | solution.py:136
  600.6 297.9 %reduce-scatter.11.cloned.1.call-start = ((), (), s32[]{:S(2)}) async-start(), calls=%async_computation.35 | async-start | bytes 10485760 | tf_op jit(solution)/shard_map/reduce_scatter | solution.py:136
  631.3 375.5 %reduce-scatter.17.cloned.1.call-start = ((), (), s32[]{:S(2)}) async-start(), calls=%async_computation.41 | async-start | bytes 2621440 | tf_op jit(solution)/shard_map/reduce_scatter | solution.py:139
  635.2 431.4 %reduce-scatter.13.cloned.1.call-start = ((), (), s32[]{:S(2)}) async-start(), calls=%async_computation.37 | async-start | bytes 10485760 | tf_op jit(solution)/shard_map/reduce_scatter | solution.py:139
  655.0 20.3 %all-to-all-start.8 = ((bf16[8,256,128]{2,1,0:T(8,128)(2,1)}), bf16[8,256,128]{2,1,0:T(8,128)(2,1)S(1)}, u32[]{:S(2)}, u32[]{:S(2)}) async-start(bf16[8,256,128]{2,1,0:T(8,128)(2,1)} %bitcast_bitcast_fusion.7), calls=%async_computation.17 | async-start | bytes 1048576 | tf_op jit(solution)/shard_map/all_to_all | solution.py:20
  663.1 18.3 %copy-start.68 = (bf16[1024]{0:T(1024)(128)(2,1)S(1)}, bf16[1024]{0:T(1024)(128)(2,1)}, u32[]{:S(2)}) copy-start(bf16[1024]{0:T(1024)(128)(2,1)} %get-tuple-element.118) | copy-start | bytes 6148
  663.1 18.3 %copy-start.67 = (bf16[1024]{0:T(1024)(128)(2,1)S(1)}, bf16[1024]{0:T(1024)(128)(2,1)}, u32[]{:S(2)}) copy-start(bf16[1024]{0:T(1024)(128)(2,1)} %get-tuple-element.133) | copy-start | bytes 6148
  663.1 18.3 %copy-start.66 = (bf16[1024]{0:T(1024)(128)(2,1)S(1)}, bf16[1024]{0:T(1024)(128)(2,1)}, u32[]{:S(2)}) copy-start(bf16[1024]{0:T(1024)(128)(2,1)} %get-tuple-element.130) | copy-start | bytes 6148
  663.1 18.3 %copy-start.65 = (bf16[1024]{0:T(1024)(128)(2,1)S(1)}, bf16[1024]{0:T(1024)(128)(2,1)}, u32[]{:S(2)}) copy-start(bf16[1024]{0:T(1024)(128)(2,1)} %get-tuple-element.131) | copy-start | bytes 6148
  663.1 18.3 %copy-start.64 = (bf16[1024]{0:T(1024)(128)(2,1)S(1)}, bf16[1024]{0:T(1024)(128)(2,1)}, u32[]{:S(2)}) copy-start(bf16[1024]{0:T(1024)(128)(2,1)} %get-tuple-element.111) | copy-start | bytes 6148
  663.1 18.3 %copy-start.79 = (bf16[1024]{0:T(1024)(128)(2,1)S(1)}, bf16[1024]{0:T(1024)(128)(2,1)}, u32[]{:S(2)}) copy-start(bf16[1024]{0:T(1024)(128)(2,1)} %get-tuple-element.62) | copy-start | bytes 6148
  663.1 18.3 %copy-start.78 = (bf16[1024]{0:T(1024)(128)(2,1)S(1)}, bf16[1024]{0:T(1024)(128)(2,1)}, u32[]{:S(2)}) copy-start(bf16[1024]{0:T(1024)(128)(2,1)} %get-tuple-element.93) | copy-start | bytes 6148
  663.1 18.4 %copy-start.77 = (bf16[1024]{0:T(1024)(128)(2,1)S(1)}, bf16[1024]{0:T(1024)(128)(2,1)}, u32[]{:S(2)}) copy-start(bf16[1024]{0:T(1024)(128)(2,1)} %get-tuple-element.64) | copy-start | bytes 6148
  663.2 18.4 %copy-start.61 = (bf16[1024]{0:T(1024)(128)(2,1)S(1)}, bf16[1024]{0:T(1024)(128)(2,1)}, u32[]{:S(2)}) copy-start(bf16[1024]{0:T(1024)(128)(2,1)} %get-tuple-element.81) | copy-start | bytes 6148
  675.3 76.8 %copy-start.41 = (bf16[8,256,128]{2,1,0:T(8,128)(2,1)}, bf16[8,256,128]{2,1,0:T(8,128)(2,1)S(1)}, u32[]{:S(2)}) copy-start(bf16[8,256,128]{2,1,0:T(8,128)(2,1)S(1)} %all-to-all-done.8) | copy-start | bytes 1572868
  675.3 20.3 %all-to-all-start.9 = ((bf16[8,256,128]{2,1,0:T(8,128)(2,1)}), bf16[8,256,128]{2,1,0:T(8,128)(2,1)S(1)}, u32[]{:S(2)}, u32[]{:S(2)}) async-start(bf16[8,256,128]{2,1,0:T(8,128)(2,1)} %bitcast_bitcast_fusion.6), calls=%async_computation.19 | async-start | bytes 1048576 | tf_op jit(solution)/shard_map/all_to_all | solution.py:20
  695.6 56.5 %copy-start.42 = (bf16[8,256,128]{2,1,0:T(8,128)(2,1)}, bf16[8,256,128]{2,1,0:T(8,128)(2,1)S(1)}, u32[]{:S(2)}) copy-start(bf16[8,256,128]{2,1,0:T(8,128)(2,1)S(1)} %all-to-all-done.9) | copy-start | bytes 1572868
  695.6 12.0 all-to-all-start.11
  707.6 9.7 all-to-all-start.12
  717.3 9.7 all-to-all-start.10
  727.0 9.7 all-to-all-start.14
  736.7 9.7 all-to-all-start.13
  746.3 14.0 %all-to-all-start.5 = ((bf16[8,256,128]{2,1,0:T(8,128)(2,1)}), bf16[8,256,128]{2,1,0:T(8,128)(2,1)S(1)}, u32[]{:S(2)}, u32[]{:S(2)}) async-start(bf16[8,256,128]{2,1,0:T(8,128)(2,1)} %bitcast_bitcast_fusion.8), calls=%async_computation.11 | async-start | bytes 1048576 | tf_op jit(solution)/shard_map/all_to_all | solution.py:20
  760.3 27.2 %all-to-all-start.4 = ((bf16[8,256,256]{2,1,0:T(8,128)(2,1)}), bf16[8,256,256]{2,1,0:T(8,128)(2,1)S(1)}, u32[]{:S(2)}, u32[]{:S(2)}) async-start(bf16[8,256,256]{2,1,0:T(8,128)(2,1)} %bitcast.172), calls=%async_computation.9 | async-start | bytes 2097152 | tf_op jit(solution)/shard_map/all_to_all | solution.py:20
  788.5 49.1 %all-to-all-start.2 = ((bf16[8,256,384]{2,1,0:T(8,128)(2,1)}), bf16[8,256,384]{2,1,0:T(8,128)(2,1)S(1)}, u32[]{:S(2)}, u32[]{:S(2)}) async-start(bf16[8,256,384]{2,1,0:T(8,128)(2,1)} %bitcast.187), calls=%async_computation.5 | async-start | bytes 3145728 | tf_op jit(solution)/shard_map/all_to_all | solution.py:20
  838.7 53.2 %all-to-all-start.7 = ((bf16[8,1024,128]{2,1,0:T(8,128)(2,1)}), bf16[8,1024,128]{2,1,0:T(8,128)(2,1)S(1)}, u32[]{:S(2)}, u32[]{:S(2)}) async-start(bf16[8,1024,128]{2,1,0:T(8,128)(2,1)} %bitcast_bitcast_fusion), calls=%async_computation.15 | async-start | bytes 4194304 | tf_op jit(solution)/shard_map/all_to_all | solution.py:20
  844.2 362.3 %all-gather.54.cloned.1.call-start = ((), (), s32[]{:S(2)}) async-start(), calls=%async_computation.43 | async-start | bytes 1179648 | tf_op jit(solution)/shard_map/all_gather | solution.py:152
  846.3 363.0 %all-gather.52.cloned.1.call-start = ((), (), s32[]{:S(2)}) async-start(), calls=%async_computation.40 | async-start | bytes 1769472 | tf_op jit(solution)/shard_map/all_gather | solution.py:152
  891.9 54.6 %all-to-all-start.6 = ((bf16[8,256,512]{2,1,0:T(8,128)(2,1)}), bf16[8,256,512]{2,1,0:T(8,128)(2,1)}, u32[]{:S(2)}, u32[]{:S(2)}) async-start(bf16[8,256,512]{2,1,0:T(8,128)(2,1)} %bitcast.186), calls=%async_computation.13 | async-start | bytes 4194304 | tf_op jit(solution)/shard_map/all_to_all | solution.py:20
  897.4 315.4 %all-gather.58.cloned.1.call-start = ((), (), s32[]{:S(2)}) async-start(), calls=%async_computation.48 | async-start | bytes 2359296 | tf_op jit(solution)/shard_map/all_gather | solution.py:155
  946.5 62.2 %all-to-all-start = ((bf16[8,256,512]{2,1,0:T(8,128)(2,1)}), bf16[8,256,512]{2,1,0:T(8,128)(2,1)S(1)}, u32[]{:S(2)}, u32[]{:S(2)}) async-start(bf16[8,256,512]{2,1,0:T(8,128)(2,1)} %bitcast.185), calls=%async_computation.1 | async-start | bytes 4194304 | tf_op jit(solution)/shard_map/all_to_all | solution.py:20
  952.1 264.9 %all-gather.56.cloned.1.call-start = ((), (), s32[]{:S(2)}) async-start(), calls=%async_computation.46 | async-start | bytes 2359296 | tf_op jit(solution)/shard_map/all_gather | solution.py:152
  1008.7 62.3 %all-to-all-start.3 = ((bf16[8,256,128]{2,1,0:T(8,128)(2,1)}), bf16[8,256,128]{2,1,0:T(8,128)(2,1)}, u32[]{:S(2)}, u32[]{:S(2)}) async-start(bf16[8,256,128]{2,1,0:T(8,128)(2,1)} %bitcast_bitcast_fusion.9), calls=%async_computation.7 | async-start | bytes 1048576 | tf_op jit(solution)/shard_map/all_to_all | solution.py:20
  1012.8 240.9 %all-gather.48.cloned.1.call-start = ((), (), s32[]{:S(2)}) async-start(), calls=%async_computation.36 | async-start | bytes 2359296 | tf_op jit(solution)/shard_map/all_gather | solution.py:152
  1071.0 134.4 %all-to-all-start.1 = ((bf16[8,1024,128]{2,1,0:T(8,128)(2,1)}), bf16[8,1024,128]{2,1,0:T(8,128)(2,1)S(1)}, u32[]{:S(2)}, u32[]{:S(2)}) async-start(bf16[8,1024,128]{2,1,0:T(8,128)(2,1)} %bitcast_bitcast_fusion.2), calls=%async_computation.3 | async-start | bytes 4194304 | tf_op jit(solution)/shard_map/all_to_all | solution.py:20
  1074.6 230.2 %all-gather.50.cloned.1.call-start = ((), (), s32[]{:S(2)}) async-start(), calls=%async_computation.38 | async-start | bytes 2359296 | tf_op jit(solution)/shard_map/all_gather | solution.py:155
  (66 other events, 297.6 us)
Sparse Core Ops, SparseCore 0:
  9.5 25.2 all-gather.43
  36.4 22.5 all-gather.45
  60.6 58.4 all-gather.27
  120.5 58.2 all-gather.29
  180.2 46.3 all-gather.31
  228.0 22.5 all-gather.33
  252.2 34.4 all-gather.35
  288.2 23.0 all-gather.37
  312.9 59.8 all-gather.39
  374.2 58.1 all-gather.41
  435.0 31.1 reduce-scatter.26
  468.5 31.8 reduce-scatter.28
  502.9 31.1 reduce-scatter.20
  541.1 45.4 reduce-scatter.18
  589.0 58.8 reduce-scatter.14
  650.3 71.9 reduce-scatter.24
  724.7 71.4 reduce-scatter.22
  798.6 71.4 reduce-scatter.10
  872.6 31.1 reduce-scatter.16
  906.2 71.3 reduce-scatter.12
  979.7 43.7 all-gather.53
  1025.6 54.0 all-gather.51
  1081.7 63.1 all-gather.57
  1147.4 53.6 all-gather.55
  1203.8 49.9 all-gather.47
  1256.3 48.5 all-gather.49
where the time goes:
time: 1320 us
  waiting for transfers between devices  470 us (36%)
  blocking collectives  375 us (28%)
  matrix products  226 us (17%)
  other arithmetic  80.6 us (6%)
  starting transfers between devices  77.7 us (6%)
  local copies, waits for them, and re-layouts  68.7 us (5%)
  between operations  18 us (1%)
    all_to_all x15, waiting for transfers between devices, summed_on_arrival(): lax.all_to_all(pieces, axis, split_axis=0, concat_axis=0, tiled=True)  170 us
    all_gather x5, waiting for transfers between devices, fetch(): lax.all_gather(second, 'narrow', axis=0, tiled=True)  109 us
    all_gather x3, blocking collectives, reduce_sums(): lax.all_gather(shares[1].astype(jnp.bfloat16), 'wide', axis=1, tiled=True)  108 us
    all_gather x5, waiting for transfers between devices, fetch(): lax.all_gather(first, 'narrow', axis=0, tiled=True)  105 us
    dot_general x10, matrix products, against(): lax.dot_general(left, right, (((1,), (1,)), ((), ())), preferred_element_...  77.1 us
    all_to_all x15, starting transfers between devices, summed_on_arrival(): lax.all_to_all(pieces, axis, split_axis=0, concat_axis=0, tiled=True)  75.4 us
    dot_general x10, matrix products, matmul(): return jnp.dot(left, right, preferred_element_type=jnp.float32)  70 us
    dot_general x10, matrix products, across_rows(): lax.dot_general(left, right, (((0,), (0,)), ((), ())), preferred_element_...  66.5 us
  transfers between devices with their start and end apart: 41, of which 21 were waited for; matrix products, arithmetic and copies ran while one was open for 26% of the time, Pallas kernels for 0%

commit v1 on v0

--- a/solution.py
+++ b/solution.py
@@ -1,24 +1,554 @@
+import functools
+
 import jax
 import jax.numpy as jnp
 from jax import lax
+from jax.experimental import pallas as pl
+from jax.experimental.pallas import tpu as pltpu
 from jax.sharding import PartitionSpec as P
 
 HEADS = 8
-
+MESH = pl.DeviceIdType.MESH
 
 EPSILON = 1e-05
 NEGATIVE = -1e30
 
 
-def split_up(shard, dim, peers):
-    before, after = (shard.shape[:dim], shard.shape[dim + 1 :])
-    return jnp.moveaxis(shard.reshape(*before, peers, -1, *after), dim, 0)
-
-
-def summed_on_arrival(shard, axis, dim):
-    pieces = split_up(shard, dim, lax.axis_size(axis))
-    arrived = lax.all_to_all(pieces, axis, split_axis=0, concat_axis=0, tiled=True)
-    return arrived.astype(jnp.float32).sum(axis=0)
+def flipped(index, bit):
+    step = 1 << bit
+    return index + step * (1 - 2 * ((index // step) % 2))
+
+
+def bit_of(index, bit):
+    return (index // (1 << bit)) % 2
+
+
+def bits_of(size):
+    return size.bit_length() - 1
+
+
+def gather_kernel(count, direct, *refs):
+    shards, wholes = refs[:count], refs[count : 2 * count]
+    send, recv, own_in, own_out = refs[2 * count : 2 * count + 4]
+    held = refs[2 * count + 4 :]
+    me, wide = lax.axis_index("narrow"), lax.axis_index("wide")
+    near, far = {"narrow": flipped(me, 0)}, {"narrow": flipped(me, 1)}
+    across = flipped(me, 1)
+    sides = ({"wide": flipped(wide, 0)}, {"wide": flipped(wide, 1)})
+    side_bits = (bit_of(wide, 0), bit_of(wide, 1))
+    barrier = pltpu.get_barrier_semaphore()
+    for peer in (near, far) + sides:
+        pl.semaphore_signal(barrier, inc=1, device_id=peer, device_id_type=MESH)
+    pl.semaphore_wait(barrier, 4)
+    started = []
+
+    def start(k, slot, src, dst, peer):
+        copy = pltpu.make_async_remote_copy(
+            src_ref=src,
+            dst_ref=dst,
+            send_sem=send.at[k, slot],
+            recv_sem=recv.at[k, slot],
+            device_id=peer,
+            device_id_type=MESH,
+        )
+        copy.start()
+        started.append(copy)
+        return copy
+
+    def rows(k, block, first, size):
+        begin = pl.multiple_of(block * shards[k].shape[0] + first, 16)
+        return wholes[k].at[pl.ds(begin, size)]
+
+    plan, crossing = [], []
+    turn = 0
+    for k in range(count):
+        depth = shards[k].shape[0]
+        if direct[k]:
+            plan.append(None)
+            crossing.append(start(k, 0, shards[k], rows(k, me, 0, depth), far))
+        else:
+            a, b = turn, 1 - turn
+            turn = b
+            quarter = depth // 4
+            first = (side_bits[b] * 2 + side_bits[a]) * quarter
+            plan.append((a, b, quarter, first))
+            piece = shards[k].at[pl.ds(pl.multiple_of(first, 16), quarter)]
+            crossing.append(start(k, 0, piece, rows(k, me, first, quarter), far))
+    taken = [pltpu.make_async_copy(shards[k], held[k], own_in.at[k]) for k in range(count)]
+    for copy in taken:
+        copy.start()
+    own = [
+        start(k, 1, shards[k], rows(k, me, 0, shards[k].shape[0]), near) for k in range(count)
+    ]
+    placed, second, third, last = [], {}, {}, []
+    for step in range(count + 2):
+        k = step
+        if k < count:
+            crossing[k].wait_recv()
+            depth = shards[k].shape[0]
+            if plan[k] is None:
+                block = rows(k, across, 0, depth)
+                last.append(start(k, 2, block, block, near))
+            else:
+                a, b, quarter, first = plan[k]
+                block = rows(k, across, first, quarter)
+                second[k] = start(k, 2, block, block, sides[a])
+            taken[k].wait()
+            placed.append(
+                pltpu.make_async_copy(held[k], rows(k, me, 0, depth), own_out.at[k])
+            )
+            placed[-1].start()
+        k = step - 1
+        if k in second:
+            second[k].wait_recv()
+            a, b, quarter, first = plan[k]
+            block = rows(k, across, side_bits[b] * 2 * quarter, 2 * quarter)
+            third[k] = start(k, 3, block, block, sides[b])
+            last.append(start(k, 4, block, block, near))
+        k = step - 2
+        if k in third:
+            third[k].wait_recv()
+            a, b, quarter, first = plan[k]
+            block = rows(k, across, (1 - side_bits[b]) * 2 * quarter, 2 * quarter)
+            last.append(start(k, 5, block, block, near))
+    for copy in own + last:
+        copy.wait_recv()
+    for copy in started:
+        copy.wait_send()
+    for copy in placed:
+        copy.wait()
+
+
+def gather_all(shards, direct):
+    count = len(shards)
+    parts = lax.axis_size("narrow")
+    return pl.pallas_call(
+        functools.partial(gather_kernel, count, direct),
+        out_shape=[
+            jax.ShapeDtypeStruct((shard.shape[0] * parts, shard.shape[1]), shard.dtype)
+            for shard in shards
+        ],
+        in_specs=[pl.BlockSpec(memory_space=pl.ANY)] * count,
+        out_specs=[pl.BlockSpec(memory_space=pl.ANY)] * count,
+        scratch_shapes=[
+            pltpu.SemaphoreType.DMA((count, 6)),
+            pltpu.SemaphoreType.DMA((count, 6)),
+            pltpu.SemaphoreType.DMA((count,)),
+            pltpu.SemaphoreType.DMA((count,)),
+        ]
+        + [pltpu.VMEM(shard.shape, shard.dtype) for shard in shards],
+        compiler_params=pltpu.CompilerParams(collective_id=0, has_side_effects=True),
+    )(*shards)
+
+
+def spread_kernel(across, within, sliced, mine_ref, all_ref, send, recv):
+    total = across * within
+    me = lax.axis_index("wide") * within + lax.axis_index("narrow")
+
+    def peer_of(step):
+        peer = lax.rem(me + step, total)
+        return (peer // within, lax.rem(peer, within))
+
+    barrier = pltpu.get_barrier_semaphore()
+
+    def greet(step, carry):
+        pl.semaphore_signal(barrier, inc=1, device_id=peer_of(step), device_id_type=MESH)
+        return carry
+
+    lax.fori_loop(1, total, greet, 0)
+    pl.semaphore_wait(barrier, total - 1)
+
+    def copy_of(step):
+        return pltpu.make_async_remote_copy(
+            src_ref=mine_ref.at[lax.rem(me + step, within) if sliced else 0],
+            dst_ref=all_ref.at[me],
+            send_sem=send.at[step],
+            recv_sem=recv.at[step],
+            device_id=peer_of(step),
+            device_id_type=MESH,
+        )
+
+    def begin(step, carry):
+        copy_of(step).start()
+        return carry
+
+    lax.fori_loop(1, total, begin, 0)
+    all_ref[me] = mine_ref[lax.axis_index("narrow") if sliced else 0]
+
+    def finish(step, carry):
+        copy_of(step).wait()
+        return carry
+
+    lax.fori_loop(1, total, finish, 0)
+
+
+def from_all(mine, identity, sliced=False):
+    across, within = lax.axis_size("wide"), lax.axis_size("narrow")
+    total = across * within
+    rows, width = mine.shape
+    pieces = within if sliced else 1
+    split = jnp.transpose(mine.reshape(rows, pieces, width // pieces), (1, 0, 2))
+    split = split.reshape(pieces, rows * width // pieces // 128, 128)
+    everyone = pl.pallas_call(
+        functools.partial(spread_kernel, across, within, sliced),
+        out_shape=jax.ShapeDtypeStruct((total,) + split.shape[1:], split.dtype),
+        in_specs=[pl.BlockSpec(memory_space=pltpu.VMEM)],
+        out_specs=pl.BlockSpec(memory_space=pltpu.VMEM),
+        scratch_shapes=[pltpu.SemaphoreType.DMA((total,)), pltpu.SemaphoreType.DMA((total,))],
+        compiler_params=pltpu.CompilerParams(collective_id=identity, has_side_effects=True),
+    )(split)
+    return everyone.reshape(total, rows, width // pieces)
+
+
+COLS = 512
+ROWS = 256
+LAGS = 10
+
+
+def gradient_kernel(plan, depth, extra, scale, *refs):
+    count = len(plan)
+    lefts, rights, outs = refs[:count], refs[count : 2 * count], refs[2 * count : 3 * count]
+    (
+        left_buf,
+        right_buf,
+        near_send,
+        near_recv,
+        held,
+        far_send,
+        far_recv,
+        kept,
+        half_send,
+        half_recv,
+        half_kept,
+        quarter_send,
+        quarter_recv,
+        quarter_kept,
+        eighth_send,
+        eighth_recv,
+        eighth_kept,
+        whole_send,
+        whole_recv,
+        back_eighth,
+        back_eighth_recv,
+        back_quarter,
+        back_quarter_recv,
+        back_half,
+        back_half_recv,
+        out_buf,
+        fetch_sem,
+        out_sem,
+        sends,
+        recvs,
+    ) = refs[3 * count :]
+    total = sum(units for _, units, _, _ in plan)
+    me, wide = lax.axis_index("narrow"), lax.axis_index("wide")
+    core, side = bit_of(me, 0), bit_of(me, 1)
+    near, far = {"narrow": flipped(me, 0)}, {"narrow": flipped(me, 1)}
+    bits = [bit_of(wide, i) for i in range(3)]
+    peers = [near, far] + [{"wide": flipped(wide, i)} for i in range(3 + extra)]
+    barrier = pltpu.get_barrier_semaphore()
+    for peer in peers:
+        pl.semaphore_signal(barrier, inc=1, device_id=peer, device_id_type=MESH)
+    pl.semaphore_wait(barrier, len(peers))
+
+    def order_of(unit):
+        turn = lax.rem(unit, 2)
+        first = bits[0] * (1 - turn) + bits[1] * turn
+        second = bits[1] * (1 - turn) + bits[0] * turn
+        near_step, far_step = 1 - 2 * bits[0], 2 * (1 - 2 * bits[1])
+        first_peer = {"wide": wide + near_step * (1 - turn) + far_step * turn}
+        second_peer = {"wide": wide + far_step * (1 - turn) + near_step * turn}
+        return first, second, bits[2], first_peer, second_peer, {"wide": flipped(wide, 2)}
+
+    def exchange(stage, unit, slots, source, target, peer):
+        slot = lax.rem(unit, slots)
+        return pltpu.make_async_remote_copy(
+            src_ref=source.at[slot],
+            dst_ref=target.at[slot],
+            send_sem=sends.at[stage, slot],
+            recv_sem=recvs.at[stage, slot],
+            device_id=peer,
+            device_id_type=MESH,
+        )
+
+    def fetches(i, unit, slot):
+        first, _, width, per_row = plan[i]
+        place = unit - first
+        deep, col = place // per_row, lax.rem(place, per_row)
+        copies = []
+        for n in range(4):
+            begin = pl.multiple_of(n * (width // 4) + deep * ROWS, ROWS)
+            copies.append(
+                pltpu.make_async_copy(
+                    lefts[i].at[:, pl.ds(begin, ROWS)],
+                    left_buf.at[slot, n],
+                    fetch_sem.at[slot, n],
+                )
+            )
+        begin = pl.multiple_of(col * COLS, COLS)
+        copies.append(
+            pltpu.make_async_copy(
+                rights[i].at[:, pl.ds(begin, COLS)], right_buf.at[slot], fetch_sem.at[slot, 4]
+            )
+        )
+        return copies
+
+    def fetch(unit):
+        for i, (first, units, _, _) in enumerate(plan):
+
+            @pl.when((unit >= first) & (unit < first + units))
+            def _(i=i):
+                for copy in fetches(i, unit, lax.rem(unit, 2)):
+                    copy.start()
+
+    def placing(i, unit, slot):
+        first, _, _, per_row = plan[i]
+        place = unit - first
+        deep, col = place // per_row, lax.rem(place, per_row)
+        block = outs[i].at[
+            pl.ds(pl.multiple_of(deep * ROWS, ROWS), ROWS),
+            pl.ds(pl.multiple_of(col * COLS, COLS), COLS),
+        ]
+        return pltpu.make_async_copy(out_buf.at[slot], block, out_sem.at[slot])
+
+    def by_rows(rows, body):
+        def step(r, carry):
+            body(pl.multiple_of(r * 32, 32))
+            return carry
+
+        if rows == 32:
+            body(0)
+        else:
+            lax.fori_loop(0, rows // 32, step, 0)
+
+    def added(first, first_slot, first_row, second, second_slot, second_row):
+        return first[first_slot, pl.ds(first_row, 32), :].astype(jnp.float32) + second[
+            second_slot, pl.ds(second_row, 32), :
+        ].astype(jnp.float32)
+
+    def stage_of(lag, tick, body):
+        unit = tick - lag
+
+        @pl.when((unit >= 0) & (unit < total))
+        def _():
+            body(unit)
+
+    def split(unit, rows, bit, kept_in, arrived, slot, send_to, keep_in):
+        half = rows // 2
+
+        def body(r):
+            theirs, mine = (1 - bit) * half + r, bit * half + r
+            send_to[slot, pl.ds(r, 32), :] = added(
+                kept_in, slot, theirs, arrived, slot, theirs
+            ).astype(jnp.bfloat16)
+            keep_in[slot, pl.ds(r, 32), :] = added(kept_in, slot, mine, arrived, slot, mine)
+
+        by_rows(half, body)
+
+    def joined(rows, bit, mine, arrived, slot, target, convert):
+        half = rows // 2
+
+        def body(r):
+            target[slot, pl.ds(bit * half + r, 32), :] = convert(mine[slot, pl.ds(r, 32), :])
+            target[slot, pl.ds((1 - bit) * half + r, 32), :] = convert(
+                arrived[slot, pl.ds(r, 32), :]
+            )
+
+        by_rows(half, body)
+
+    def finish(unit):
+        first, _, _, first_peer, _, _ = order_of(unit)
+        exchange(7, unit, 4, back_half, back_half_recv, first_peer).wait()
+        slot = lax.rem(unit, 4)
+
+        @pl.when(unit >= 4)
+        def _():
+            placing(0, unit * 0, slot).wait()
+
+        joined(
+            ROWS, first, back_half, back_half_recv, slot, out_buf,
+            lambda v: v.astype(jnp.float32) * scale,
+        )
+        for i, (start, units, _, _) in enumerate(plan):
+
+            @pl.when((unit >= start) & (unit < start + units))
+            def _(i=i):
+                placing(i, unit, slot).start()
+
+    def double_last(unit):
+        _, second, _, first_peer, second_peer, _ = order_of(unit)
+        exchange(6, unit, 4, back_quarter, back_quarter_recv, second_peer).wait()
+        joined(
+            ROWS // 2, second, back_quarter, back_quarter_recv, lax.rem(unit, 4), back_half,
+            lambda v: v,
+        )
+        exchange(7, unit, 4, back_half, back_half_recv, first_peer).start()
+
+    def double_first(unit):
+        _, _, third, _, second_peer, third_peer = order_of(unit)
+        exchange(5, unit, 4, back_eighth, back_eighth_recv, third_peer).wait()
+        joined(
+            ROWS // 4, third, back_eighth, back_eighth_recv, lax.rem(unit, 4), back_quarter,
+            lambda v: v,
+        )
+        exchange(6, unit, 4, back_quarter, back_quarter_recv, second_peer).start()
+
+    def turn_back(unit):
+        _, _, _, _, _, third_peer = order_of(unit)
+        slot = lax.rem(unit, 4)
+        exchange(4, unit, 4, eighth_send, eighth_recv, third_peer).wait()
+        value = added(eighth_kept, slot, 0, eighth_recv, slot, 0)
+        for bit in range(3, 3 + extra):
+            whole_send[slot] = value.astype(jnp.bfloat16)
+            copy = exchange(5 + bit, unit, 4, whole_send, whole_recv.at[bit - 3], {"wide": flipped(wide, bit)})
+            copy.start()
+            copy.wait()
+            value = value + whole_recv[bit - 3, slot].astype(jnp.float32)
+        back_eighth[slot] = value.astype(jnp.bfloat16)
+        exchange(5, unit, 4, back_eighth, back_eighth_recv, third_peer).start()
+
+    def halve_third(unit):
+        _, _, third, _, second_peer, third_peer = order_of(unit)
+        slot = lax.rem(unit, 4)
+        exchange(3, unit, 4, quarter_send, quarter_recv, second_peer).wait()
+        split(unit, ROWS // 4, third, quarter_kept, quarter_recv, slot, eighth_send, eighth_kept)
+        exchange(4, unit, 4, eighth_send, eighth_recv, third_peer).start()
+
+    def halve_second(unit):
+        _, second, _, first_peer, second_peer, _ = order_of(unit)
+        slot = lax.rem(unit, 4)
+        exchange(2, unit, 4, half_send, half_recv, first_peer).wait()
+        split(unit, ROWS // 2, second, half_kept, half_recv, slot, quarter_send, quarter_kept)
+        exchange(3, unit, 4, quarter_send, quarter_recv, second_peer).start()
+
+    def halve_first(unit):
+        first, _, _, first_peer, _, _ = order_of(unit)
+        slot = lax.rem(unit, 4)
+        exchange(1, unit, 4, far_send, far_recv, far).wait()
+        split(unit, ROWS, first, kept, far_recv, slot, half_send, half_kept)
+        exchange(2, unit, 4, half_send, half_recv, first_peer).start()
+
+    def cross(unit):
+        slot, near_slot = lax.rem(unit, 4), lax.rem(unit, 2)
+        exchange(0, unit, 2, near_send, near_recv, near).wait()
+
+        def body(r):
+            far_send[slot, pl.ds(r, 32), :] = (
+                held[near_slot, 0, pl.ds(r, 32), :]
+                + near_recv[near_slot, 0, pl.ds(r, 32), :].astype(jnp.float32)
+            ).astype(jnp.bfloat16)
+            kept[slot, pl.ds(r, 32), :] = held[near_slot, 1, pl.ds(r, 32), :] + near_recv[
+                near_slot, 1, pl.ds(r, 32), :
+            ].astype(jnp.float32)
+
+        by_rows(ROWS, body)
+        exchange(1, unit, 4, far_send, far_recv, far).start()
+
+    def multiply(unit):
+        slot = lax.rem(unit, 2)
+        for copy in fetches(0, unit * 0, slot):
+            copy.wait()
+
+        @pl.when(unit + 1 < total)
+        def _():
+            fetch(unit + 1)
+
+        def product(block, first):
+            return lax.dot_general(
+                left_buf[slot, block],
+                right_buf[slot, :, pl.ds(first, 256)],
+                (((0,), (0,)), ((), ())),
+                preferred_element_type=jnp.float32,
+            )
+
+        for which in range(2):
+            block = 2 * (side * which + (1 - side) * (1 - which)) + 1 - core
+            for first in range(0, COLS, 256):
+                near_send[slot, which, :, pl.ds(first, 256)] = product(block, first).astype(
+                    jnp.bfloat16
+                )
+        exchange(0, unit, 2, near_send, near_recv, near).start()
+        for which in range(2):
+            block = 2 * (side * which + (1 - side) * (1 - which)) + core
+            for first in range(0, COLS, 256):
+                held[slot, which, :, pl.ds(first, 256)] = product(block, first)
+
+    fetch(me * 0)
+
+    def tick(step, carry):
+        stage_of(9, step, finish)
+        stage_of(8, step, double_last)
+        stage_of(7, step, double_first)
+        stage_of(6, step, turn_back)
+        stage_of(5, step, halve_third)
+        stage_of(4, step, halve_second)
+        stage_of(3, step, halve_first)
+        stage_of(1, step, cross)
+        stage_of(0, step, multiply)
+        return carry
+
+    lax.fori_loop(0, total + LAGS - 1, tick, 0)
+    for slot in range(4):
+        placing(0, me * 0, slot).wait()
+
+
+def gradients(pairs):
+    parts, copies = lax.axis_size("narrow"), lax.axis_size("wide")
+    extra = bits_of(copies) - 3
+    plan, begun = [], 0
+    for left, right in pairs:
+        per_row = right.shape[1] // COLS
+        units = per_row * (left.shape[1] // (parts * ROWS))
+        plan.append((begun, units, left.shape[1], per_row))
+        begun += units
+    rows = pairs[0][0].shape[0]
+    low, high = jnp.bfloat16, jnp.float32
+
+    def pair_of(size, slots=4):
+        return [pltpu.VMEM((slots, size, COLS), low)] * 2
+
+    def trio_of(size):
+        return pair_of(size) + [pltpu.VMEM((4, size, COLS), high)]
+
+    scratch = (
+        [
+            pltpu.VMEM((2, 4, rows, ROWS), low),
+            pltpu.VMEM((2, rows, COLS), low),
+            pltpu.VMEM((2, 2, ROWS, COLS), low),
+            pltpu.VMEM((2, 2, ROWS, COLS), low),
+            pltpu.VMEM((2, 2, ROWS, COLS), high),
+        ]
+        + trio_of(ROWS)
+        + trio_of(ROWS // 2)
+        + trio_of(ROWS // 4)
+        + trio_of(ROWS // 8)
+        + [
+            pltpu.VMEM((4, ROWS // 8, COLS), low),
+            pltpu.VMEM((max(extra, 1), 4, ROWS // 8, COLS), low),
+        ]
+        + pair_of(ROWS // 8)
+        + pair_of(ROWS // 4)
+        + pair_of(ROWS // 2)
+        + [
+            pltpu.VMEM((4, ROWS, COLS), high),
+            pltpu.SemaphoreType.DMA((2, 5)),
+            pltpu.SemaphoreType.DMA((4,)),
+            pltpu.SemaphoreType.DMA((8 + extra, 4)),
+            pltpu.SemaphoreType.DMA((8 + extra, 4)),
+        ]
+    )
+    count = len(pairs)
+    return pl.pallas_call(
+        functools.partial(gradient_kernel, tuple(plan), rows, extra, 1.0 / copies),
+        out_shape=[
+            jax.ShapeDtypeStruct((left.shape[1] // parts, right.shape[1]), high)
+            for left, right in pairs
+        ],
+        in_specs=[pl.BlockSpec(memory_space=pl.ANY)] * (2 * count),
+        out_specs=[pl.BlockSpec(memory_space=pl.ANY)] * count,
+        scratch_shapes=scratch,
+        compiler_params=pltpu.CompilerParams(collective_id=4, has_side_effects=True),
+    )(*[left for left, _ in pairs], *[right for _, right in pairs])
 
 
 def matmul(left, right):
@@ -92,81 +622,6 @@
     return (adjoint_values, jnp.stack(kernel_rows))
 
 
-def unpack_small(gathered, count):
-    parts = gathered.shape[0]
-    breadth = gathered.shape[1] // count
-    unfolded = jnp.transpose(gathered.reshape(parts, count, breadth), (1, 0, 2))
-    return unfolded.reshape(count, parts * breadth).astype(jnp.float32)
-
-
-def fetch(first, second, small):
-    whole = (
-        lax.all_gather(first, "narrow", axis=0, tiled=True),
-        lax.all_gather(second, "narrow", axis=0, tiled=True),
-        lax.all_gather(small.reshape(1, -1), "narrow", axis=0, tiled=True),
-    )
-    return (whole[0], whole[1], unpack_small(whole[2], small.shape[0]))
-
-
-def fetch_again(first, second, small):
-    whole = (
-        lax.all_gather(first, "narrow", axis=0, tiled=True),
-        lax.all_gather(second, "narrow", axis=0, tiled=True),
-        lax.all_gather(small.reshape(1, -1), "narrow", axis=0, tiled=True),
-    )
-    return (whole[0], whole[1], unpack_small(whole[2], small.shape[0]))
-
-
-def again(first, second, small):
-    return fetch_again(first, second, small)
-
-
-def fold_small(full):
-    parts = lax.axis_size("narrow")
-    count = full.shape[0]
-    breadth = full.shape[1] // parts
-    return jnp.transpose(full.reshape(count, parts, breadth), (1, 0, 2)).reshape(
-        parts, count * breadth
-    )
-
-
-def reduce_sums(first, second, small):
-    folded = fold_small(small)
-    spread_out = (
-        lax.psum_scatter(
-            first.astype(jnp.bfloat16), "narrow", scatter_dimension=0, tiled=True
-        ).astype(jnp.float32),
-        lax.psum_scatter(
-            second.astype(jnp.bfloat16), "narrow", scatter_dimension=0, tiled=True
-        ).astype(jnp.float32),
-        lax.psum_scatter(
-            folded.astype(jnp.bfloat16), "narrow", scatter_dimension=0, tiled=True
-        ).astype(jnp.float32),
-    )
-    shares = (
-        summed_on_arrival(spread_out[0].astype(jnp.bfloat16), "wide", 1),
-        summed_on_arrival(spread_out[1].astype(jnp.bfloat16), "wide", 1),
-        summed_on_arrival(spread_out[2].astype(jnp.bfloat16), "wide", 1),
-    )
-    whole = (
-        lax.all_gather(shares[0].astype(jnp.bfloat16), "wide", axis=1, tiled=True).astype(
-            jnp.float32
-        ),
-        lax.all_gather(shares[1].astype(jnp.bfloat16), "wide", axis=1, tiled=True).astype(
-            jnp.float32
-        ),
-        lax.all_gather(shares[2].astype(jnp.bfloat16), "wide", axis=1, tiled=True).astype(
-            jnp.float32
-        ),
-    )
-    replicas = float(lax.axis_size("wide"))
-    return (
-        whole[0] / replicas,
-        whole[1] / replicas,
-        whole[2].reshape(small.shape[0], -1) / replicas,
-    )
-
-
 def feed_forward(values, weight_in, weight_out, gain):
     normed, normal_hat, scale = layer_norm(values, gain)
     entry = normed.astype(jnp.bfloat16)
@@ -179,15 +634,18 @@
 def feed_back(adjoint, kept, weight_in, weight_out, gain):
     entry, normal_hat, scale, before, active = kept
     adjoint_branch = (0.5 * adjoint).astype(jnp.bfloat16)
-    out_sum = across_rows(active, adjoint_branch)
     adjoint_before = (against(adjoint_branch, weight_out) * swish_slope(before)).astype(
         jnp.bfloat16
     )
-    in_sum = across_rows(entry, adjoint_before)
     adjoint_values, gain_sum = norm_back(
         against(adjoint_before, weight_in), normal_hat, scale, gain
     )
-    return (adjoint + adjoint_values, in_sum, out_sum, gain_sum)
+    return (
+        adjoint + adjoint_values,
+        (entry, adjoint_before),
+        (active, adjoint_branch),
+        gain_sum,
+    )
 
 
 def masked_scores(query_block, segment_block, keys, segment, factor):
@@ -251,7 +709,6 @@
     head_dim = width // heads
     factor = head_dim ** (-0.5)
     adjoint_branch = adjoint.astype(jnp.bfloat16)
-    out_sum = across_rows(heads_out, adjoint_branch)
     adjoint_heads = (
         against(adjoint_branch, weight_out)
         .astype(jnp.bfloat16)
@@ -300,9 +757,13 @@
         ],
         axis=1,
     ).astype(jnp.bfloat16)
-    in_sum = across_rows(entry, adjoint_mixed)
     adjoint_values, gain_sum = norm_back(against(adjoint_mixed, weight_in), normal_hat, scale, gain)
-    return (adjoint + adjoint_values, in_sum, out_sum, gain_sum)
+    return (
+        adjoint + adjoint_values,
+        (entry, adjoint_mixed),
+        (heads_out, adjoint_branch),
+        gain_sum,
+    )
 
 
 def convolution_forward(values, weight_in, weight_out, small, segment, valid):
@@ -314,11 +775,17 @@
     sigmoid_right = jax.nn.sigmoid(gates[:, width:])
     gated = gates[:, :width] * sigmoid_right
     convolved = depthwise(gated, small[1 : 1 + taps], segment)
-    local_count = jnp.sum(valid)
-    total, count = lax.psum((jnp.sum(convolved * valid, axis=0), local_count), ("wide", "narrow"))
-    mean = total / count
+    here = jnp.sum(valid)
+    total_here = jnp.sum(convolved * valid, axis=0)
+    off = (convolved - total_here / jnp.maximum(here, 1.0)) * valid
+    mine = jnp.stack([jnp.full((width,), here), total_here, jnp.sum(off * off, axis=0)])
+    everyone = from_all(mine, 1)
+    counts, totals, squares = everyone[:, 0], everyone[:, 1], everyone[:, 2]
+    count = jnp.sum(counts, axis=0)
+    mean = jnp.sum(totals, axis=0) / count
+    apart = totals / jnp.maximum(counts, 1.0) - mean
+    spread = jnp.sum(squares + counts * apart * apart, axis=0) / count
     centred = convolved - mean
-    spread = lax.psum(jnp.sum(centred * centred * valid, axis=0), ("wide", "narrow")) / count
     inverse = lax.rsqrt(spread + EPSILON)
     batch_hat = centred * inverse
     batch_out = batch_hat * small[1 + taps] + small[2 + taps]
@@ -357,15 +824,23 @@
     taps = small.shape[0] - 3
     width = adjoint.shape[1]
     adjoint_branch = adjoint.astype(jnp.bfloat16)
-    out_sum = across_rows(active, adjoint_branch)
     adjoint_batch = against(adjoint_branch, weight_out) * swish_slope(batch_out)
     shift_sum = jnp.sum(adjoint_batch, axis=0)
     batch_gain_sum = jnp.sum(adjoint_batch * batch_hat, axis=0)
     adjoint_hat = adjoint_batch * small[1 + taps]
-    first_total, second_total = lax.psum(
-        (jnp.sum(adjoint_hat * valid, axis=0), jnp.sum(adjoint_hat * batch_hat * valid, axis=0)),
-        ("wide", "narrow"),
-    )
+    sums = jnp.sum(
+        from_all(
+            jnp.stack(
+                [
+                    jnp.sum(adjoint_hat * valid, axis=0),
+                    jnp.sum(adjoint_hat * batch_hat * valid, axis=0),
+                ]
+            ),
+            2,
+        ),
+        axis=0,
+    )
+    first_total, second_total = sums[0], sums[1]
     adjoint_conv = inverse * (
         adjoint_hat - valid * (first_total + batch_hat * second_total) / count
     )
@@ -378,14 +853,18 @@
         ],
         axis=1,
     ).astype(jnp.bfloat16)
-    in_sum = across_rows(entry, adjoint_gates)
     adjoint_values, gain_sum = norm_back(
         against(adjoint_gates, weight_in), normal_hat, scale, small[0]
     )
     small_sum = jnp.concatenate(
         [gain_sum[None], kernel_sum, batch_gain_sum[None], shift_sum[None]], axis=0
     )
-    return (adjoint + adjoint_values, in_sum, out_sum, small_sum)
+    return (
+        adjoint + adjoint_values,
+        (entry, adjoint_gates),
+        (active, adjoint_branch),
+        small_sum,
+    )
 
 
 def per_device(
@@ -416,103 +895,138 @@
     valid = (positions < slot_ends[-1]).astype(jnp.float32)
     inputs = acoustic_features.astype(jnp.float32)
     taps = channelwise_kernel_weights.shape[0]
-    conv_small = jnp.concatenate(
-        [normalizer_gains[3:4], channelwise_kernel_weights, normalizer_affine_rows], axis=0
-    )
-    quantizer_weights = fetch(
-        vocabulary_affinity_projector, vocabulary_vectors, normalizer_gains[0:1]
-    )
-    quantizer_normed, quantizer_hat, quantizer_scale = layer_norm(inputs, quantizer_weights[2][0])
+    gain_rows = normalizer_gains.shape[0]
+    small = jnp.concatenate(
+        [normalizer_gains, channelwise_kernel_weights, normalizer_affine_rows], axis=0
+    )
+    small_rows = small.shape[0]
+    padding = -small_rows % 16
+    small = jnp.pad(small, ((0, padding), (0, 0)))
+    parts = lax.axis_size("narrow")
+    order = (
+        heads_merging_projector,
+        gated_channel_projector,
+        query_key_value_projector,
+        early_expanding_projector,
+        early_contracting_projector,
+        later_expanding_projector,
+        later_contracting_projector,
+        closing_channel_projector,
+        vocabulary_affinity_projector,
+        vocabulary_vectors,
+        small,
+    )
+    (
+        attention_out,
+        pointwise_in,
+        attention_in,
+        first_up,
+        first_down,
+        second_up,
+        second_down,
+        pointwise_out,
+        quantizer_in,
+        codebook,
+        small_blocks,
+    ) = gather_all(order, (False,) * 7 + (True,) * 4)
+    small_whole = (
+        jnp.transpose(small_blocks.reshape(parts, small_rows + padding, -1), (1, 0, 2))
+        .reshape(small_rows + padding, -1)
+        .astype(jnp.float32)
+    )
+    gains = small_whole[:gain_rows]
+    conv_small = jnp.concatenate([gains[3:4], small_whole[gain_rows:small_rows]], axis=0)
+
+    quantizer_normed, quantizer_hat, quantizer_scale = layer_norm(inputs, gains[0])
     quantizer_entry = quantizer_normed.astype(jnp.bfloat16)
-    vocabulary_affinity = matmul(quantizer_entry, quantizer_weights[0])
+    vocabulary_affinity = matmul(quantizer_entry, quantizer_in)
     code_probabilities = jax.nn.softmax(
         (vocabulary_affinity + perturbation_samples.astype(jnp.float32)) / annealing_level[0],
         axis=-1,
     )
     chances_low = code_probabilities.astype(jnp.bfloat16)
-    codes = matmul(chances_low, quantizer_weights[1]).astype(jnp.bfloat16)
-    first_weights = fetch(
-        early_expanding_projector, early_contracting_projector, normalizer_gains[1:2]
-    )
-    after_first, first_kept = feed_forward(
-        inputs, first_weights[0], first_weights[1], first_weights[2][0]
-    )
-    attend_weights = fetch(
-        query_key_value_projector, heads_merging_projector, normalizer_gains[2:3]
-    )
-    after_attention, attend_kept = attention_forward(
-        after_first, attend_weights[0], attend_weights[1], attend_weights[2][0], segment, HEADS
-    )
-    conv_weights = fetch(gated_channel_projector, closing_channel_projector, conv_small)
-    after_conv, conv_kept = convolution_forward(
-        after_attention, conv_weights[0], conv_weights[1], conv_weights[2], segment, valid
-    )
-    second_weights = fetch(
-        later_expanding_projector, later_contracting_projector, normalizer_gains[4:6]
-    )
-    after_second, second_kept = feed_forward(
-        after_conv, second_weights[0], second_weights[1], second_weights[2][0]
-    )
-    final_out, final_hat, final_scale = layer_norm(after_second, second_weights[2][1])
-    output = final_out.astype(jnp.bfloat16)
-    adjoint_output = result_cotangent.astype(jnp.float32) * valid
+    codes = matmul(chances_low, codebook).astype(jnp.bfloat16)
     adjoint_codes = quantized_cotangent * valid.astype(jnp.bfloat16)
-    adjoint, final_gain_sum = norm_back(
-        adjoint_output, final_hat, final_scale, second_weights[2][1]
-    )
-    weights_now = again(
-        later_expanding_projector, later_contracting_projector, normalizer_gains[4:6]
-    )
-    adjoint, up_sum, down_sum, gain_sum = feed_back(
-        adjoint, second_kept, weights_now[0], weights_now[1], weights_now[2][0]
-    )
-    second_up_gradient, second_down_gradient, second_small = reduce_sums(
-        up_sum, down_sum, jnp.stack([gain_sum, final_gain_sum])
-    )
-    weights_now = again(gated_channel_projector, closing_channel_projector, conv_small)
-    adjoint, in_sum, out_sum, small_sum = convolution_back(
-        adjoint, conv_kept, weights_now[0], weights_now[1], weights_now[2], segment, valid
-    )
-    pointwise_in_gradient, pointwise_out_gradient, conv_small_gradient = reduce_sums(
-        in_sum, out_sum, small_sum
-    )
-    weights_now = again(query_key_value_projector, heads_merging_projector, normalizer_gains[2:3])
-    adjoint, in_sum, out_sum, gain_sum = attention_back(
-        adjoint, attend_kept, weights_now[0], weights_now[1], weights_now[2][0], segment, HEADS
-    )
-    attention_in_gradient, attention_out_gradient, attend_small = reduce_sums(
-        in_sum, out_sum, gain_sum[None]
-    )
-    weights_now = again(
-        early_expanding_projector, early_contracting_projector, normalizer_gains[1:2]
-    )
-    adjoint, up_sum, down_sum, gain_sum = feed_back(
-        adjoint, first_kept, weights_now[0], weights_now[1], weights_now[2][0]
-    )
-    first_up_gradient, first_down_gradient, first_small = reduce_sums(
-        up_sum, down_sum, gain_sum[None]
-    )
-    weights_now = again(vocabulary_affinity_projector, vocabulary_vectors, normalizer_gains[0:1])
-    book_sum = across_rows(chances_low, adjoint_codes)
-    adjoint_chances = against(adjoint_codes, weights_now[1])
+    adjoint_chances = against(adjoint_codes, codebook)
     adjoint_logits = (
         code_probabilities
         * (adjoint_chances - jnp.sum(code_probabilities * adjoint_chances, axis=-1, keepdims=True))
         / annealing_level[0]
     ).astype(jnp.bfloat16)
-    projection_sum = across_rows(quantizer_entry, adjoint_logits)
     adjoint_inputs, quantizer_gain_sum = norm_back(
-        against(adjoint_logits, weights_now[0]), quantizer_hat, quantizer_scale, weights_now[2][0]
+        against(adjoint_logits, quantizer_in), quantizer_hat, quantizer_scale, gains[0]
+    )
+
+    after_first, first_kept = feed_forward(inputs, first_up, first_down, gains[1])
+    after_attention, attend_kept = attention_forward(
+        after_first, attention_in, attention_out, gains[2], segment, HEADS
+    )
+    after_conv, conv_kept = convolution_forward(
+        after_attention, pointwise_in, pointwise_out, conv_small, segment, valid
+    )
+    after_second, second_kept = feed_forward(after_conv, second_up, second_down, gains[4])
+    final_out, final_hat, final_scale = layer_norm(after_second, gains[5])
+    output = final_out.astype(jnp.bfloat16)
+
+    adjoint_output = result_cotangent.astype(jnp.float32) * valid
+    adjoint, final_gain_sum = norm_back(adjoint_output, final_hat, final_scale, gains[5])
+    adjoint, second_up_pair, second_down_pair, second_gain_sum = feed_back(
+        adjoint, second_kept, second_up, second_down, gains[4]
+    )
+    adjoint, pointwise_in_pair, pointwise_out_pair, conv_small_sum = convolution_back(
+        adjoint, conv_kept, pointwise_in, pointwise_out, conv_small, segment, valid
+    )
+    adjoint, attention_in_pair, attention_out_pair, attend_gain_sum = attention_back(
+        adjoint, attend_kept, attention_in, attention_out, gains[2], segment, HEADS
+    )
+    adjoint, first_up_pair, first_down_pair, first_gain_sum = feed_back(
+        adjoint, first_kept, first_up, first_down, gains[1]
+    )
+    (
+        first_up_gradient,
+        first_down_gradient,
+        attention_in_gradient,
+        attention_out_gradient,
+        pointwise_in_gradient,
+        pointwise_out_gradient,
+        second_up_gradient,
+        second_down_gradient,
+        quantizer_in_gradient,
+        codebook_gradient,
+    ) = gradients(
+        (
+            first_up_pair,
+            first_down_pair,
+            attention_in_pair,
+            attention_out_pair,
+            pointwise_in_pair,
+            pointwise_out_pair,
+            second_up_pair,
+            second_down_pair,
+            (quantizer_entry, adjoint_logits),
+            (chances_low, adjoint_codes),
+        )
     )
     frames_gradient = (adjoint + adjoint_inputs).astype(jnp.bfloat16)
-    quantizer_in_gradient, codebook_gradient, quantizer_small = reduce_sums(
-        projection_sum, book_sum, quantizer_gain_sum[None]
-    )
-    norm_gains_gradient = jnp.concatenate(
-        [quantizer_small, first_small, attend_small, conv_small_gradient[0:1], second_small], axis=0
-    )
-    depthwise_kernel_gradient = conv_small_gradient[1 : 1 + taps]
-    batch_affine_gradient = conv_small_gradient[1 + taps :]
+    small_sums = jnp.concatenate(
+        [
+            quantizer_gain_sum[None],
+            first_gain_sum[None],
+            attend_gain_sum[None],
+            conv_small_sum[:1],
+            second_gain_sum[None],
+            final_gain_sum[None],
+            conv_small_sum[1:],
+        ],
+        axis=0,
+    )
+    small_sums = jnp.pad(small_sums, ((0, padding), (0, 0)))
+    small_gradient = jnp.sum(from_all(small_sums, 3, sliced=True), axis=0) / float(
+        lax.axis_size("wide")
+    )
+    norm_gains_gradient = small_gradient[:gain_rows]
+    depthwise_kernel_gradient = small_gradient[gain_rows : gain_rows + taps]
+    batch_affine_gradient = small_gradient[gain_rows + taps : small_rows]
     return (
         output,
         codes,

time: 1320 us -> 774 us (0.59)
  Pallas kernels: 0 us -> 529 us
  waiting for transfers between devices: 470 us -> 0 us
  blocking collectives: 375 us -> 0 us
  matrix products: 226 us -> 119 us
  starting transfers between devices: 77.7 us -> 0 us
  other arithmetic: 80.6 us -> 49.7 us
  between operations: 18 us -> 3.73 us
    pallas_call x0 -> x5, Pallas kernels: none -> 529 us  [the longest x1 360 us: gradients(): pl.pallas_call(functools.partial(gradient_kernel, tuple(plan), rows, extr...]
    all_gather x16 -> x0, waiting for transfers between devices: 293 us -> none  [the longest x5 109 us: fetch(): lax.all_gather(second, 'narrow', axis=0, tiled=True)]
    all_gather x10 -> x0, blocking collectives: 207 us -> none  [the longest x3 108 us: reduce_sums(): lax.all_gather(shares[1].astype(jnp.bfloat16), 'wide', axis=1, tiled=True)]
    all_to_all x15 -> x0, waiting for transfers between devices: 170 us -> none  [summed_on_arrival(): lax.all_to_all(pieces, axis, split_axis=0, concat_axis=0, tiled=True)]
    psum x3 -> x0, blocking collectives: 123 us -> none  [the longest x1 42.2 us: convolution_forward(): lax.psum(jnp.sum(centred * centred * valid, axis=0), ('wide', 'narrow'))]
    all_to_all x15 -> x0, starting transfers between devices: 75.4 us -> none  [summed_on_arrival(): lax.all_to_all(pieces, axis, split_axis=0, concat_axis=0, tiled=True)]
    dot_general x10 -> x0, matrix products: 66.5 us -> none  [across_rows(): lax.dot_general(left, right, (((0,), (0,)), ((), ())), preferred_element_...]
    unnamed x2 -> x0, blocking collectives: 45 us -> none
  transfers between devices with their start and end apart: 41 -> 0, of which waited for: 21 -> 0; matrix products, arithmetic and copies ran while one was open for 26% -> 0% of each run, Pallas kernels for 0% -> 0%
where the time goes in v1:
time: 774 us; the launch traced here: 766 us
  Pallas kernels  529 us (68%)
  matrix products  119 us (15%)
  local copies, waits for them, and re-layouts  65.4 us (8%)
  other arithmetic  49.7 us (6%)
    pallas_call x1, Pallas kernels, gradients(): pl.pallas_call(functools.partial(gradient_kernel, tuple(plan), rows, extr...  360 us
    pallas_call x1, Pallas kernels, gather_all(): pl.pallas_call(functools.partial(gather_kernel, count, direct), out_shape...  124 us
    dot_general x10, matrix products, against(): lax.dot_general(left, right, (((1,), (1,)), ((), ())), preferred_element_...  55.6 us
    unnamed x207, local copies, waits for them, and re-layouts  45.7 us
    pallas_call x3, Pallas kernels, from_all(): pl.pallas_call(functools.partial(spread_kernel, across, within, sliced),...  44.8 us
    dot_general x10, matrix products, matmul(): return jnp.dot(left, right, preferred_element_type=jnp.float32)  44.5 us

profile of v1, /device:TPU:0, one launch (start us, length us, event | category | flops | bytes accessed | tf_op | source)
XLA Modules:
  0.0 766.2 jit_solution(15722262014088934758)
XLA Ops:
  0.6 1.3 fusion.54.refs_10_
  2.0 124.1 %shard_map.306 = (bf16[1024,1024]{1,0:T(8,128)(2,1)}, bf16[1024,2048]{1,0:T(8,128)(2,1)}, bf16[1024,3072]{1,0:T(8,128)(2,1)}, bf16[1024,4096]{1,0:T(8,128)(2,1)}...) custom-call(bf16[256,1024]{1,0:T(8,128)(2,1)} %refs_0_.1, ...), custom_call_target="tpu_custom_call" | custom-call | tf_op jit(solution)/shard_map/pallas_call | solution.py:125
  127.6 1.5 fusion.17
  129.1 11.4 %multiply_convert_fusion.4 = (bf16[512,4096]{1,0:T(8,128)(2,1)S(1)}, f32[512,4096]{1,0:T(8,128)}) fusion(bf16[512,1024]{1,0:T(8,128)(2,1)S(1)} %get-tuple-element.178.refs_0_, bf16[1024,4096]{1,0:T(8,128)(2,1)} %get-tuple-element.95), kind=kOutput, calls=%fused_computation.10 | convolution fusion | flops 4305453056 | bytes 22020096 | tf_op jit(solution)/shard_map/dot_general | solution.py:555
  140.6 4.7 fusion.72
  146.2 3.7 convolution_convert_fusion
  149.9 1.7 slice_bitcast_fusion
  151.7 1.5 copy.104
  153.2 2.4 copy.105
  156.1 2.9 fusion.73
  160.2 2.2 copy-done
  162.5 1.6 fusion.37
  164.1 1.4 fusion.74
  168.8 2.4 fusion.78
  175.7 2.4 multiply_reduce_fusion.21
  181.7 13.4 %shard_map.307 = f32[32,24,128]{2,1,0:T(8,128)} custom-call(f32[1,24,128]{2,1,0:T(8,128)} %reshape_transpose_reshape.6.mine_ref), custom_call_target="tpu_custom_call" | custom-call | tf_op jit(solution)/shard_map/pallas_call | solution.py:192
  195.1 1.9 reshape.351
  197.1 1.9 slice_reduce_fusion
  199.8 1.4 fusion.75
  202.9 7.5 multiply_convert_fusion.3
  210.5 8.5 %fusion.76 = (f32[512]{0:T(512)S(1)}, f32[512,1024]{1,0:T(8,128)S(1)}) fusion(f32[512,1024]{1,0:T(8,128)S(1)} %get-tuple-element.214, bf16[512,4096]{1,0:T(8,128)(2,1)S(1)} %get-tuple-element.215.refs_7_, bf16[4096,1024]{1,0:T(8,128)(2,1)} %get-tuple-element.102), kind=kOutput, calls=%fused_computation.212 | convolution fusion | flops 4296539648 | bytes 16779264 | tf_op jit(solution)/shard_map/dot_general | solution.py:555
  223.1 10.1 %multiply_convert_fusion.2.refs_16_ = bf16[512,4096]{1,0:T(8,128)(2,1)S(1)} fusion(f32[512,4096]{1,0:T(8,128)} %get-tuple-element.216, bf16[512,1024]{1,0:T(8,128)(2,1)S(1)} %multiply_convert_fusion.10.refs_17_, bf16[4096,1024]{1,0:T(8,128)(2,1)} %get-tuple-element.102), kind=kOutput, calls=%fused_computation.4 | convolution fusion | flops 4313841664 | bytes 22020096 | tf_op jit(solution)/shard_map/dot_general | solution.py:565
  233.2 9.0 %multiply_reduce_fusion.8 = (f32[1024]{0:T(1024)S(1)}, f32[512]{0:T(512)S(1)}, f32[512]{0:T(512)S(1)}, f32[512,1024]{1,0:T(8,128)S(1)}) fusion(f32[512,1024]{1,0:T(8,128)S(1)} %get-tuple-element.214, f32[512]{0:T(512)S(1)} %add_rsqrt_fusion.2, f32[512]{0:T(512)S(1)} %broadcast_multiply_fusion.19, f32[1024]{0:T(1024)S(1)} %bitcast.163, ...), kind=kOutput, calls=%fused_computation.62 | convolution fusion | flops 4299159552 | bytes 16793600 | tf_op jit(solution)/shard_map/dot_general | solution.py:565
  242.2 2.8 fusion.66
  245.0 3.8 multiply_reduce_fusion.1
  249.4 14.2 %shard_map.308 = f32[32,16,128]{2,1,0:T(8,128)} custom-call(f32[1,16,128]{2,1,0:T(8,128)} %reshape_transpose_reshape.7.mine_ref), custom_call_target="tpu_custom_call" | custom-call | tf_op jit(solution)/shard_map/pallas_call | solution.py:192
  264.6 3.4 multiply_reduce_fusion.2
  269.9 2.2 multiply_reduce_fusion.6
  273.6 1.9 multiply_convert_fusion.9
  277.7 1.4 copy-done.79
  279.0 2.8 multiply_reduce_fusion.9
  281.9 2.0 fusion.65
  284.9 2.3 convolution_convert_fusion.1
  287.2 1.6 copy.106
  288.8 4.8 multiply_reduce_fusion
  294.7 2.6 multiply_convert_fusion.1
  299.3 1.3 copy.96
  300.6 3.7 multiply_convert_fusion.6
  304.3 1.5 copy.97
  305.8 5.0 fusion.38
  310.8 1.3 copy.98
  312.8 7.6 multiply_reduce_fusion.10
  320.4 2.1 multiply_convert_fusion.5
  322.6 10.8 %multiply_convert_fusion.refs_10_ = bf16[512,4096]{1,0:T(8,128)(2,1)S(1)} fusion(f32[512,4096]{1,0:T(8,128)} %get-tuple-element.206, bf16[512,1024]{1,0:T(8,128)(2,1)S(1)} %get-tuple-element.151.refs_11_, bf16[4096,1024]{1,0:T(8,128)(2,1)} %get-tuple-element.96), kind=kOutput, calls=%fused_computation | convolution fusion | flops 4313841664 | bytes 22020096 | tf_op jit(solution)/shard_map/dot_general | solution.py:565
  334.0 1.4 fusion.77
  337.3 1.5 multiply_reduce_fusion.11
  338.8 1.6 divide_convert_fusion.2
  341.5 1.3 fusion.79
  344.0 6.5 fusion.28
  351.3 17.3 %shard_map.310 = f32[32,32,128]{2,1,0:T(8,128)} custom-call(f32[4,32,128]{2,1,0:T(8,128)} %reshape.356.mine_ref), custom_call_target="tpu_custom_call" | custom-call | tf_op jit(solution)/shard_map/pallas_call | solution.py:192
  371.5 1.5 pad_maximum_fusion.1.refs_14_
  374.1 1.8 pad_maximum_fusion.refs_12_
  375.9 1.3 copy.95.refs_3_
  377.2 359.7 %shard_map.309 = (f32[256,4096]{1,0:T(8,128)}, f32[1024,1024]{1,0:T(8,128)}, f32[256,3072]{1,0:T(8,128)}, f32[256,1024]{1,0:T(8,128)}, f32[256,2048]{1,0:T(8,128...) custom-call(bf16[512,1024]{1,0:T(8,128)(2,1)} %copy-done.35, ...), custom_call_target="tpu_custom_call" | custom-call | tf_op jit(solution)/shard_map/pallas_call | solution.py:541
  737.0 3.7 fusion.23
  740.8 2.2 convolution_convert_fusion.2
  743.0 2.1 copy.140
  745.2 1.6 copy-done.39
  746.7 2.1 copy.141
  750.1 1.7 copy.142
  754.1 1.3 copy.144
  757.5 2.1 copy.146
  759.6 1.6 copy-done.37
  761.2 2.0 copy.147
  (284 shorter events, 50.3 us)
Async XLA Ops:
  2.0 124.9 %copy-start.16 = (bf16[512,1024]{1,0:T(8,128)(2,1)S(1)}, bf16[512,1024]{1,0:T(8,128)(2,1)}, u32[]{:S(2)}) copy-start(bf16[512,1024]{1,0:T(8,128)(2,1)} %param.19) | copy-start | bytes 3145732
  126.9 18.7 %copy-start.63 = (f32[1,4,256]{2,0,1:T(1,128)}, f32[1,4,256]{2,0,1:T(1,128)S(1)}, u32[]{:S(2)}) copy-start(f32[1,4,256]{2,0,1:T(1,128)S(1)} %get-tuple-element.193) | copy-start | bytes 12292
  127.5 13.0 %copy-start.75 = (f32[512]{0:T(512)}, f32[512]{0:T(512)S(1)}, u32[]{:S(2)}) copy-start(f32[512]{0:T(512)S(1)} %add_rsqrt_fusion.5) | copy-start | bytes 6148
  127.6 13.0 %slice-start.4 = ((s8[8388608]{0:T(1024)(128)(4,1)}), s8[4194304]{0:T(1024)(128)(4,1)S(1)}, s32[]{:S(2)}) async-start(s8[8388608]{0:T(1024)(128)(4,1)} %bitcast.198), calls=%async_computation.4 | async-start | bytes 8388608
  127.6 18.7 %slice-start.8 = ((s8[6291456]{0:T(1024)(128)(4,1)}), s8[4194304]{0:T(1024)(128)(4,1)S(1)}, s32[]{:S(2)}) async-start(s8[6291456]{0:T(1024)(128)(4,1)} %bitcast.202), calls=%async_computation.8 | async-start | bytes 8388608
  129.0 11.5 %copy-start.35 = (bf16[512,1024]{1,0:T(8,128)(2,1)}, bf16[512,1024]{1,0:T(8,128)(2,1)S(1)}, u32[]{:S(2)}) copy-start(bf16[512,1024]{1,0:T(8,128)(2,1)S(1)} %get-tuple-element.178.refs_0_) | copy-start | bytes 3145732
  129.1 11.5 %slice-start.5 = ((s8[8388608]{0:T(1024)(128)(4,1)}), s8[4194304]{0:T(1024)(128)(4,1)S(1)}, s32[]{:S(2)}) async-start(s8[8388608]{0:T(1024)(128)(4,1)} %bitcast.198), calls=%async_computation.5 | async-start | bytes 8388608
  129.1 17.2 %slice-start.9 = ((s8[6291456]{0:T(1024)(128)(4,1)}), s8[2097152]{0:T(1024)(128)(4,1)S(1)}, s32[]{:S(2)}) async-start(s8[6291456]{0:T(1024)(128)(4,1)} %bitcast.202), calls=%async_computation.9 | async-start | bytes 4194304
  140.5 4.7 copy-start.23
  145.2 18.9 %copy-start.4 = (f32[512,1024]{1,0:T(8,128)}, f32[512,1024]{1,0:T(8,128)S(1)}, u32[]{:S(2)}) copy-start(f32[512,1024]{1,0:T(8,128)S(1)} %get-tuple-element.208) | copy-start | bytes 6291460
  145.6 4.3 copy-start.73
  146.2 3.7 copy-start.27
  151.7 4.0 copy-start.87
  159.0 3.4 copy-start
  159.0 3.4 copy-start.41
  165.5 3.3 copy-start.78
  171.2 4.5 copy-start.1
  172.5 3.2 copy-start.9
  172.5 3.2 copy-start.15
  173.1 5.0 copy-start.11
  173.1 5.0 copy-start.13
  197.1 2.8 copy-start.7
  197.1 2.8 copy-start.85
  199.1 2.8 slice-start.6
  199.8 3.1 slice-start.7
  201.9 8.6 %copy-start.30 = (bf16[512,1024]{1,0:T(8,128)(2,1)}, bf16[512,1024]{1,0:T(8,128)(2,1)S(1)}, u32[]{:S(2)}) copy-start(bf16[512,1024]{1,0:T(8,128)(2,1)S(1)} %multiply_convert_fusion.12.refs_6_) | copy-start | bytes 3145732
  210.5 8.5 %copy-start.24 = (bf16[512,4096]{1,0:T(8,128)(2,1)}, bf16[512,4096]{1,0:T(8,128)(2,1)S(1)}, u32[]{:S(2)}) copy-start(bf16[512,4096]{1,0:T(8,128)(2,1)S(1)} %get-tuple-element.215.refs_7_) | copy-start | bytes 12582916
  233.2 9.0 %copy-start.25 = (bf16[512,4096]{1,0:T(8,128)(2,1)}, bf16[512,4096]{1,0:T(8,128)(2,1)S(1)}, u32[]{:S(2)}) copy-start(bf16[512,4096]{1,0:T(8,128)(2,1)S(1)} %multiply_convert_fusion.2.refs_16_) | copy-start | bytes 12582916
  245.0 3.8 copy-start.52
  264.6 3.5 copy-start.2
  264.6 4.1 copy-start.10
  264.6 4.7 copy-start.12
  264.6 5.3 copy-start.14
  275.5 3.6 copy-start.79
  276.4 5.5 copy-start.45
  279.0 2.8 copy-start.22
  281.9 3.0 copy-start.84
  288.8 4.9 slice-start
  288.8 5.9 slice-start.1
  294.7 2.6 copy-start.19
  305.8 6.3 copy-start.64
  305.8 6.3 copy-start.70
  305.8 6.3 copy-start.74
  312.8 7.7 %copy-start.20 = (f32[512,1024]{1,0:T(8,128)S(1)}, f32[512,1024]{1,0:T(8,128)}, u32[]{:S(2)}) copy-start(f32[512,1024]{1,0:T(8,128)} %get-tuple-element.154) | copy-start | bytes 6291460
  322.5 10.8 %copy-start.33 = (bf16[512,1024]{1,0:T(8,128)(2,1)}, bf16[512,1024]{1,0:T(8,128)(2,1)S(1)}, u32[]{:S(2)}) copy-start(bf16[512,1024]{1,0:T(8,128)(2,1)S(1)} %get-tuple-element.151.refs_11_) | copy-start | bytes 3145732
  322.5 11.4 %copy-start.34 = (bf16[512,1024]{1,0:T(8,128)(2,1)S(1)}, bf16[512,1024]{1,0:T(8,128)(2,1)}, u32[]{:S(2)}) copy-start(bf16[512,1024]{1,0:T(8,128)(2,1)} %get-tuple-element.177.refs_8_) | copy-start | bytes 3145732
  322.5 11.5 %copy-start.82 = (bf16[1024,1024]{1,0:T(8,128)(2,1)S(1)}, bf16[1024,1024]{1,0:T(8,128)(2,1)}, u32[]{:S(2)}) copy-start(bf16[1024,1024]{1,0:T(8,128)(2,1)} %get-tuple-element.103) | copy-start | bytes 6291460
  322.5 11.5 %copy-start.86 = (bf16[512,1024]{1,0:T(8,128)(2,1)S(1)}, bf16[512,1024]{1,0:T(8,128)(2,1)}, u32[]{:S(2)}) copy-start(bf16[512,1024]{1,0:T(8,128)(2,1)} %param.21) | copy-start | bytes 3145732
  333.3 9.5 %copy-start.26 = (bf16[512,4096]{1,0:T(8,128)(2,1)}, bf16[512,4096]{1,0:T(8,128)(2,1)S(1)}, u32[]{:S(2)}) copy-start(bf16[512,4096]{1,0:T(8,128)(2,1)S(1)} %multiply_convert_fusion.refs_10_) | copy-start | bytes 12582916
  338.8 4.0 slice-start.2
  341.5 2.5 slice-start.3
  344.0 6.5 copy-start.55
  344.0 27.5 %copy-start.46 = (bf16[512,1024]{1,0:T(8,128)(2,1)S(1)}, bf16[512,1024]{1,0:T(8,128)(2,1)}, u32[]{:S(2)}) copy-start(bf16[512,1024]{1,0:T(8,128)(2,1)} %copy-done.45) | copy-start | bytes 3145732
  350.5 21.0 %copy-start.44 = (bf16[512,1024]{1,0:T(8,128)(2,1)S(1)}, bf16[512,1024]{1,0:T(8,128)(2,1)}, u32[]{:S(2)}) copy-start(bf16[512,1024]{1,0:T(8,128)(2,1)} %copy-done.43) | copy-start | bytes 3145732
  371.5 2.3 copy-start.50
  371.5 2.6 copy-start.51
  377.2 359.8 %copy-start.21 = (f32[512,1024]{1,0:T(8,128)S(1)}, f32[512,1024]{1,0:T(8,128)}, u32[]{:S(2)}) copy-start(f32[512,1024]{1,0:T(8,128)} %get-tuple-element.152) | copy-start | bytes 6291460
  737.0 3.8 copy-start.47
  737.0 3.8 copy-start.81
  743.0 3.7 copy-start.39
  746.7 3.4 copy-start.53
  752.1 3.3 copy-start.60
  754.1 3.4 copy-start.38
  757.5 3.7 copy-start.37
  (34 other events, 53.0 us)

commit v2 on v1

--- a/solution.py
+++ b/solution.py
@@ -27,7 +27,11 @@
     return size.bit_length() - 1
 
 
-def gather_kernel(count, direct, *refs):
+LAG = 2
+
+
+def gather_kernel(plan, *refs):
+    count = (len(refs) - 4) // 3
     shards, wholes = refs[:count], refs[count : 2 * count]
     send, recv, own_in, own_out = refs[2 * count : 2 * count + 4]
     held = refs[2 * count + 4 :]
@@ -42,12 +46,12 @@
     pl.semaphore_wait(barrier, 4)
     started = []
 
-    def start(k, slot, src, dst, peer):
+    def start(chunk, slot, src, dst, peer):
         copy = pltpu.make_async_remote_copy(
             src_ref=src,
             dst_ref=dst,
-            send_sem=send.at[k, slot],
-            recv_sem=recv.at[k, slot],
+            send_sem=send.at[chunk, slot],
+            recv_sem=recv.at[chunk, slot],
             device_id=peer,
             device_id_type=MESH,
         )
@@ -59,58 +63,63 @@
         begin = pl.multiple_of(block * shards[k].shape[0] + first, 16)
         return wholes[k].at[pl.ds(begin, size)]
 
-    plan, crossing = [], []
+    crossing, routes = [], []
     turn = 0
-    for k in range(count):
-        depth = shards[k].shape[0]
-        if direct[k]:
-            plan.append(None)
-            crossing.append(start(k, 0, shards[k], rows(k, me, 0, depth), far))
+    for chunk, (k, begin, size, direct) in enumerate(plan):
+        if direct:
+            routes.append(None)
+            piece = shards[k].at[pl.ds(begin, size)]
+            crossing.append(start(chunk, 0, piece, rows(k, me, begin, size), far))
         else:
             a, b = turn, 1 - turn
             turn = b
-            quarter = depth // 4
-            first = (side_bits[b] * 2 + side_bits[a]) * quarter
-            plan.append((a, b, quarter, first))
+            quarter = size // 4
+            first = begin + (side_bits[b] * 2 + side_bits[a]) * quarter
+            routes.append((a, b, quarter, first))
             piece = shards[k].at[pl.ds(pl.multiple_of(first, 16), quarter)]
-            crossing.append(start(k, 0, piece, rows(k, me, first, quarter), far))
+            crossing.append(start(chunk, 0, piece, rows(k, me, first, quarter), far))
     taken = [pltpu.make_async_copy(shards[k], held[k], own_in.at[k]) for k in range(count)]
     for copy in taken:
         copy.start()
     own = [
-        start(k, 1, shards[k], rows(k, me, 0, shards[k].shape[0]), near) for k in range(count)
+        start(len(plan) + k, 0, shards[k], rows(k, me, 0, shards[k].shape[0]), near)
+        for k in range(count)
     ]
     placed, second, third, last = [], {}, {}, []
-    for step in range(count + 2):
-        k = step
-        if k < count:
-            crossing[k].wait_recv()
-            depth = shards[k].shape[0]
-            if plan[k] is None:
-                block = rows(k, across, 0, depth)
-                last.append(start(k, 2, block, block, near))
-            else:
-                a, b, quarter, first = plan[k]
-                block = rows(k, across, first, quarter)
-                second[k] = start(k, 2, block, block, sides[a])
-            taken[k].wait()
+    for step in range(len(plan) + 2 * LAG):
+        if step < count:
+            taken[step].wait()
+            depth = shards[step].shape[0]
             placed.append(
-                pltpu.make_async_copy(held[k], rows(k, me, 0, depth), own_out.at[k])
+                pltpu.make_async_copy(held[step], rows(step, me, 0, depth), own_out.at[step])
             )
             placed[-1].start()
-        k = step - 1
-        if k in second:
-            second[k].wait_recv()
-            a, b, quarter, first = plan[k]
-            block = rows(k, across, side_bits[b] * 2 * quarter, 2 * quarter)
-            third[k] = start(k, 3, block, block, sides[b])
-            last.append(start(k, 4, block, block, near))
-        k = step - 2
-        if k in third:
-            third[k].wait_recv()
-            a, b, quarter, first = plan[k]
-            block = rows(k, across, (1 - side_bits[b]) * 2 * quarter, 2 * quarter)
-            last.append(start(k, 5, block, block, near))
+        chunk = step - 2 * LAG
+        if chunk in third:
+            third[chunk].wait_recv()
+            k, begin, size, _ = plan[chunk]
+            a, b, quarter, first = routes[chunk]
+            block = rows(k, across, begin + (1 - side_bits[b]) * 2 * quarter, 2 * quarter)
+            last.append(start(chunk, 5, block, block, near))
+        chunk = step - LAG
+        if chunk in second:
+            second[chunk].wait_recv()
+            k, begin, size, _ = plan[chunk]
+            a, b, quarter, first = routes[chunk]
+            block = rows(k, across, begin + side_bits[b] * 2 * quarter, 2 * quarter)
+            third[chunk] = start(chunk, 3, block, block, sides[b])
+            last.append(start(chunk, 4, block, block, near))
+        chunk = step
+        if chunk < len(plan):
+            crossing[chunk].wait_recv()
+            k, begin, size, direct = plan[chunk]
+            if direct:
+                block = rows(k, across, begin, size)
+                last.append(start(chunk, 2, block, block, near))
+            else:
+                a, b, quarter, first = routes[chunk]
+                block = rows(k, across, first, quarter)
+                second[chunk] = start(chunk, 2, block, block, sides[a])
     for copy in own + last:
         copy.wait_recv()
     for copy in started:
@@ -119,11 +128,19 @@
         copy.wait()
 
 
-def gather_all(shards, direct):
+def chunks_of(shards, pieces):
+    plan = []
+    for k, (shard, cuts) in enumerate(zip(shards, pieces)):
+        size = shard.shape[0] // max(cuts, 1)
+        plan += [(k, i * size, size, cuts == 0) for i in range(max(cuts, 1))]
+    return tuple(plan)
+
+
+def gather_all(shards, plan):
     count = len(shards)
     parts = lax.axis_size("narrow")
     return pl.pallas_call(
-        functools.partial(gather_kernel, count, direct),
+        functools.partial(gather_kernel, plan),
         out_shape=[
             jax.ShapeDtypeStruct((shard.shape[0] * parts, shard.shape[1]), shard.dtype)
             for shard in shards
@@ -131,8 +148,8 @@
         in_specs=[pl.BlockSpec(memory_space=pl.ANY)] * count,
         out_specs=[pl.BlockSpec(memory_space=pl.ANY)] * count,
         scratch_shapes=[
-            pltpu.SemaphoreType.DMA((count, 6)),
-            pltpu.SemaphoreType.DMA((count, 6)),
+            pltpu.SemaphoreType.DMA((len(plan) + count, 6)),
+            pltpu.SemaphoreType.DMA((len(plan) + count, 6)),
             pltpu.SemaphoreType.DMA((count,)),
             pltpu.SemaphoreType.DMA((count,)),
         ]
@@ -141,7 +158,7 @@
     )(*shards)
 
 
-def spread_kernel(across, within, sliced, mine_ref, all_ref, send, recv):
+def spread_kernel(across, within, mine_ref, all_ref, send, recv):
     total = across * within
     me = lax.axis_index("wide") * within + lax.axis_index("narrow")
 
@@ -160,7 +177,7 @@
 
     def copy_of(step):
         return pltpu.make_async_remote_copy(
-            src_ref=mine_ref.at[lax.rem(me + step, within) if sliced else 0],
+            src_ref=mine_ref,
             dst_ref=all_ref.at[me],
             send_sem=send.at[step],
             recv_sem=recv.at[step],
@@ -173,7 +190,7 @@
         return carry
 
     lax.fori_loop(1, total, begin, 0)
-    all_ref[me] = mine_ref[lax.axis_index("narrow") if sliced else 0]
+    all_ref[me] = mine_ref[...]
 
     def finish(step, carry):
         copy_of(step).wait()
@@ -182,32 +199,36 @@
     lax.fori_loop(1, total, finish, 0)
 
 
-def from_all(mine, identity, sliced=False):
+def columns_split(small, pieces):
+    rows, width = small.shape
+    split = jnp.transpose(small.reshape(rows, pieces, width // pieces), (1, 0, 2))
+    return split.reshape(pieces, rows * width // pieces // 128, 128)
+
+
+def from_all(mine, identity):
     across, within = lax.axis_size("wide"), lax.axis_size("narrow")
     total = across * within
-    rows, width = mine.shape
-    pieces = within if sliced else 1
-    split = jnp.transpose(mine.reshape(rows, pieces, width // pieces), (1, 0, 2))
-    split = split.reshape(pieces, rows * width // pieces // 128, 128)
+    flat = columns_split(mine, 1)[0]
     everyone = pl.pallas_call(
-        functools.partial(spread_kernel, across, within, sliced),
-        out_shape=jax.ShapeDtypeStruct((total,) + split.shape[1:], split.dtype),
+        functools.partial(spread_kernel, across, within),
+        out_shape=jax.ShapeDtypeStruct((total,) + flat.shape, flat.dtype),
         in_specs=[pl.BlockSpec(memory_space=pltpu.VMEM)],
         out_specs=pl.BlockSpec(memory_space=pltpu.VMEM),
         scratch_shapes=[pltpu.SemaphoreType.DMA((total,)), pltpu.SemaphoreType.DMA((total,))],
         compiler_params=pltpu.CompilerParams(collective_id=identity, has_side_effects=True),
-    )(split)
-    return everyone.reshape(total, rows, width // pieces)
-
-
-COLS = 512
+    )(flat)
+    return everyone.reshape((total,) + mine.shape)
+
+
+COLS = 256
 ROWS = 256
-LAGS = 10
-
-
-def gradient_kernel(plan, depth, extra, scale, *refs):
+LAGS = 16
+
+
+def gradient_kernel(plan, extra, across, within, *refs):
     count = len(plan)
-    lefts, rights, outs = refs[:count], refs[count : 2 * count], refs[2 * count : 3 * count]
+    lefts, rights = refs[:count], refs[count : 2 * count]
+    small, outs, smalls = refs[2 * count], refs[2 * count + 1 : 3 * count + 1], refs[3 * count + 1]
     (
         left_buf,
         right_buf,
@@ -239,17 +260,47 @@
         out_sem,
         sends,
         recvs,
-    ) = refs[3 * count :]
+        small_send,
+        small_recv,
+    ) = refs[3 * count + 2 :]
     total = sum(units for _, units, _, _ in plan)
     me, wide = lax.axis_index("narrow"), lax.axis_index("wide")
     core, side = bit_of(me, 0), bit_of(me, 1)
     near, far = {"narrow": flipped(me, 0)}, {"narrow": flipped(me, 1)}
     bits = [bit_of(wide, i) for i in range(3)]
-    peers = [near, far] + [{"wide": flipped(wide, i)} for i in range(3 + extra)]
+    devices = across * within
+    place = wide * within + me
+
+    def peer_of(step):
+        peer = lax.rem(place + step, devices)
+        return (peer // within, lax.rem(peer, within))
+
     barrier = pltpu.get_barrier_semaphore()
-    for peer in peers:
-        pl.semaphore_signal(barrier, inc=1, device_id=peer, device_id_type=MESH)
-    pl.semaphore_wait(barrier, len(peers))
+
+    def greet(step, carry):
+        pl.semaphore_signal(barrier, inc=1, device_id=peer_of(step), device_id_type=MESH)
+        return carry
+
+    lax.fori_loop(1, devices, greet, 0)
+    pl.semaphore_wait(barrier, devices - 1)
+
+    def small_copy(step):
+        return pltpu.make_async_remote_copy(
+            src_ref=small.at[lax.rem(place + step, within)],
+            dst_ref=smalls.at[place],
+            send_sem=small_send.at[step],
+            recv_sem=small_recv.at[step],
+            device_id=peer_of(step),
+            device_id_type=MESH,
+        )
+
+    def begin(step, carry):
+        small_copy(step).start()
+        return carry
+
+    def end(step, carry):
+        small_copy(step).wait()
+        return carry
 
     def order_of(unit):
         turn = lax.rem(unit, 2)
@@ -345,14 +396,12 @@
 
         by_rows(half, body)
 
-    def joined(rows, bit, mine, arrived, slot, target, convert):
+    def joined(rows, bit, mine, arrived, slot, target):
         half = rows // 2
 
         def body(r):
-            target[slot, pl.ds(bit * half + r, 32), :] = convert(mine[slot, pl.ds(r, 32), :])
-            target[slot, pl.ds((1 - bit) * half + r, 32), :] = convert(
-                arrived[slot, pl.ds(r, 32), :]
-            )
+            target[slot, pl.ds(bit * half + r, 32), :] = mine[slot, pl.ds(r, 32), :]
+            target[slot, pl.ds((1 - bit) * half + r, 32), :] = arrived[slot, pl.ds(r, 32), :]
 
         by_rows(half, body)
 
@@ -367,7 +416,6 @@
 
         joined(
             ROWS, first, back_half, back_half_recv, slot, out_buf,
-            lambda v: v.astype(jnp.float32) * scale,
         )
         for i, (start, units, _, _) in enumerate(plan):
 
@@ -380,7 +428,6 @@
         exchange(6, unit, 4, back_quarter, back_quarter_recv, second_peer).wait()
         joined(
             ROWS // 2, second, back_quarter, back_quarter_recv, lax.rem(unit, 4), back_half,
-            lambda v: v,
         )
         exchange(7, unit, 4, back_half, back_half_recv, first_peer).start()
 
@@ -389,7 +436,6 @@
         exchange(5, unit, 4, back_eighth, back_eighth_recv, third_peer).wait()
         joined(
             ROWS // 4, third, back_eighth, back_eighth_recv, lax.rem(unit, 4), back_quarter,
-            lambda v: v,
         )
         exchange(6, unit, 4, back_quarter, back_quarter_recv, second_peer).start()
 
@@ -474,14 +520,16 @@
                 held[slot, which, :, pl.ds(first, 256)] = product(block, first)
 
     fetch(me * 0)
+    lax.fori_loop(1, devices, begin, 0)
+    smalls[place] = small[me]
 
     def tick(step, carry):
-        stage_of(9, step, finish)
-        stage_of(8, step, double_last)
-        stage_of(7, step, double_first)
-        stage_of(6, step, turn_back)
-        stage_of(5, step, halve_third)
-        stage_of(4, step, halve_second)
+        stage_of(15, step, finish)
+        stage_of(13, step, double_last)
+        stage_of(11, step, double_first)
+        stage_of(9, step, turn_back)
+        stage_of(7, step, halve_third)
+        stage_of(5, step, halve_second)
         stage_of(3, step, halve_first)
         stage_of(1, step, cross)
         stage_of(0, step, multiply)
@@ -490,9 +538,10 @@
     lax.fori_loop(0, total + LAGS - 1, tick, 0)
     for slot in range(4):
         placing(0, me * 0, slot).wait()
-
-
-def gradients(pairs):
+    lax.fori_loop(1, devices, end, 0)
+
+
+def gradients(pairs, small):
     parts, copies = lax.axis_size("narrow"), lax.axis_size("wide")
     extra = bits_of(copies) - 3
     plan, begun = [], 0
@@ -530,25 +579,33 @@
         + pair_of(ROWS // 4)
         + pair_of(ROWS // 2)
         + [
-            pltpu.VMEM((4, ROWS, COLS), high),
+            pltpu.VMEM((4, ROWS, COLS), low),
             pltpu.SemaphoreType.DMA((2, 5)),
             pltpu.SemaphoreType.DMA((4,)),
             pltpu.SemaphoreType.DMA((8 + extra, 4)),
             pltpu.SemaphoreType.DMA((8 + extra, 4)),
+            pltpu.SemaphoreType.DMA((copies * parts,)),
+            pltpu.SemaphoreType.DMA((copies * parts,)),
         ]
     )
     count = len(pairs)
-    return pl.pallas_call(
-        functools.partial(gradient_kernel, tuple(plan), rows, extra, 1.0 / copies),
+    split = columns_split(small, parts)
+    results = pl.pallas_call(
+        functools.partial(gradient_kernel, tuple(plan), extra, copies, parts),
         out_shape=[
-            jax.ShapeDtypeStruct((left.shape[1] // parts, right.shape[1]), high)
+            jax.ShapeDtypeStruct((left.shape[1] // parts, right.shape[1]), low)
             for left, right in pairs
-        ],
-        in_specs=[pl.BlockSpec(memory_space=pl.ANY)] * (2 * count),
-        out_specs=[pl.BlockSpec(memory_space=pl.ANY)] * count,
+        ]
+        + [jax.ShapeDtypeStruct((copies * parts,) + split.shape[1:], high)],
+        in_specs=[pl.BlockSpec(memory_space=pl.ANY)] * (2 * count)
+        + [pl.BlockSpec(memory_space=pltpu.VMEM)],
+        out_specs=[pl.BlockSpec(memory_space=pl.ANY)] * count
+        + [pl.BlockSpec(memory_space=pltpu.VMEM)],
         scratch_shapes=scratch,
         compiler_params=pltpu.CompilerParams(collective_id=4, has_side_effects=True),
-    )(*[left for left, _ in pairs], *[right for _, right in pairs])
+    )(*[left for left, _ in pairs], *[right for _, right in pairs], split)
+    everyone = results[-1].reshape(copies * parts, small.shape[0], -1)
+    return tuple(whole.astype(high) / float(copies) for whole in results[:-1]) + (everyone,)
 
 
 def matmul(left, right):
@@ -928,7 +985,7 @@
         quantizer_in,
         codebook,
         small_blocks,
-    ) = gather_all(order, (False,) * 7 + (True,) * 4)
+    ) = gather_all(order, chunks_of(order, (1, 2, 2, 2, 2, 2, 2, 0, 0, 0, 0)))
     small_whole = (
         jnp.transpose(small_blocks.reshape(parts, small_rows + padding, -1), (1, 0, 2))
         .reshape(small_rows + padding, -1)
@@ -982,6 +1039,19 @@
     adjoint, first_up_pair, first_down_pair, first_gain_sum = feed_back(
         adjoint, first_kept, first_up, first_down, gains[1]
     )
+    frames_gradient = (adjoint + adjoint_inputs).astype(jnp.bfloat16)
+    small_sums = jnp.concatenate(
+        [
+            quantizer_gain_sum[None],
+            first_gain_sum[None],
+            attend_gain_sum[None],
+            conv_small_sum[:1],
+            second_gain_sum[None],
+            final_gain_sum[None],
+            conv_small_sum[1:],
+        ],
+        axis=0,
+    )
     (
         first_up_gradient,
         first_down_gradient,
@@ -993,6 +1063,7 @@
         second_down_gradient,
         quantizer_in_gradient,
         codebook_gradient,
+        small_gradients,
     ) = gradients(
         (
             first_up_pair,
@@ -1005,25 +1076,10 @@
             second_down_pair,
             (quantizer_entry, adjoint_logits),
             (chances_low, adjoint_codes),
-        )
-    )
-    frames_gradient = (adjoint + adjoint_inputs).astype(jnp.bfloat16)
-    small_sums = jnp.concatenate(
-        [
-            quantizer_gain_sum[None],
-            first_gain_sum[None],
-            attend_gain_sum[None],
-            conv_small_sum[:1],
-            second_gain_sum[None],
-            final_gain_sum[None],
-            conv_small_sum[1:],
-        ],
-        axis=0,
-    )
-    small_sums = jnp.pad(small_sums, ((0, padding), (0, 0)))
-    small_gradient = jnp.sum(from_all(small_sums, 3, sliced=True), axis=0) / float(
-        lax.axis_size("wide")
-    )
+        ),
+        jnp.pad(small_sums, ((0, padding), (0, 0))),
+    )
+    small_gradient = jnp.sum(small_gradients, axis=0) / float(lax.axis_size("wide"))
     norm_gains_gradient = small_gradient[:gain_rows]
     depthwise_kernel_gradient = small_gradient[gain_rows : gain_rows + taps]
     batch_affine_gradient = small_gradient[gain_rows + taps : small_rows]

time: 774 us -> 704 us (0.910)
  Pallas kernels: 529 us -> 461 us
  local copies, waits for them, and re-layouts: 65.4 us -> 43 us
  other arithmetic: 49.7 us -> 69.8 us
    pallas_call x5 -> x4, Pallas kernels: 529 us -> 461 us  [the longest x1 321 us: gradients(): pl.pallas_call(functools.partial(gradient_kernel, tuple(plan), extra, cop...]
    unnamed x207 -> x195, local copies, waits for them, and re-layouts: 45.7 us -> 23 us
    div x1 -> x11, other arithmetic: 0.01 us -> 20 us  [the longest x10 20 us: gradients(): whole.astype(high) / float(copies)]
where the time goes in v2:
time: 704 us; the launch traced here: 696 us
  Pallas kernels  461 us (65%)
  matrix products  119 us (17%)
  other arithmetic  69.8 us (10%)
  local copies, waits for them, and re-layouts  43 us (6%)
    pallas_call x1, Pallas kernels, gradients(): pl.pallas_call(functools.partial(gradient_kernel, tuple(plan), extra, cop...  321 us
    pallas_call x1, Pallas kernels, gather_all(): pl.pallas_call(functools.partial(gather_kernel, plan), out_shape=[jax.Sha...  112 us
    dot_general x10, matrix products, against(): lax.dot_general(left, right, (((1,), (1,)), ((), ())), preferred_element_...  55.4 us
    dot_general x10, matrix products, matmul(): return jnp.dot(left, right, preferred_element_type=jnp.float32)  44.5 us
    pallas_call x2, Pallas kernels, from_all(): pl.pallas_call(functools.partial(spread_kernel, across, within), out_shap...  27.8 us
    unnamed x195, local copies, waits for them, and re-layouts  23 us
    div x10, other arithmetic, gradients(): whole.astype(high) / float(copies)  20 us

profile of v2, /device:TPU:0, one launch (start us, length us, event | category | flops | bytes accessed | tf_op | source)
XLA Modules:
  0.0 695.6 jit_solution(13997692814340969220)
XLA Ops:
  0.6 1.3 fusion.54.refs_10_
  2.0 112.1 %shard_map.306 = (bf16[1024,1024]{1,0:T(8,128)(2,1)}, bf16[1024,2048]{1,0:T(8,128)(2,1)}, bf16[1024,3072]{1,0:T(8,128)(2,1)}, bf16[1024,4096]{1,0:T(8,128)(2,1)}...) custom-call(bf16[256,1024]{1,0:T(8,128)(2,1)} %refs_0_.1, ...), custom_call_target="tpu_custom_call" | custom-call | tf_op jit(solution)/shard_map/pallas_call | solution.py:142
  115.6 1.5 fusion.17
  117.1 11.4 %multiply_convert_fusion.4 = (bf16[512,4096]{1,0:T(8,128)(2,1)S(1)}, f32[512,4096]{1,0:T(8,128)}) fusion(bf16[512,1024]{1,0:T(8,128)(2,1)S(1)} %get-tuple-element.180.refs_0_, bf16[1024,4096]{1,0:T(8,128)(2,1)} %get-tuple-element.96), kind=kOutput, calls=%fused_computation.10 | convolution fusion | flops 4305453056 | bytes 22020096 | tf_op jit(solution)/shard_map/dot_general | solution.py:612
  128.6 4.7 fusion.72
  134.3 3.7 convolution_convert_fusion
  138.0 1.7 slice_bitcast_fusion
  139.7 1.5 copy.104
  141.2 2.5 copy.105
  144.2 2.9 fusion.73
  148.3 2.2 copy-done
  150.5 1.6 fusion.37
  152.2 1.4 fusion.74
  156.9 2.4 fusion.78
  162.5 1.3 fusion.58
  163.8 2.4 multiply_reduce_fusion.21
  166.2 1.3 fusion.55
  169.8 13.6 %shard_map.307 = f32[32,24,128]{2,1,0:T(8,128)} custom-call(f32[24,128]{1,0:T(8,128)} %squeeze_reshape_transpose_reshape.6.mine_ref), custom_call_target="tpu_custom_call" | custom-call | tf_op jit(solution)/shard_map/pallas_call | solution.py:212
  183.5 1.9 reshape.351
  185.4 1.9 slice_reduce_fusion
  188.2 1.4 fusion.75
  191.3 7.5 %multiply_convert_fusion.3 = (bf16[512,4096]{1,0:T(8,128)(2,1)S(1)}, f32[512,4096]{1,0:T(8,128)}) fusion(bf16[512,1024]{1,0:T(8,128)(2,1)S(1)} %multiply_convert_fusion.12.refs_6_, bf16[1024,4096]{1,0:T(8,128)(2,1)S(1)} %bitcast.201), kind=kOutput, calls=%fused_computation.5 | convolution fusion | flops 4305453056 | bytes 22020096 | tf_op jit(solution)/shard_map/dot_general | solution.py:612
  198.8 8.5 %fusion.76 = (f32[512]{0:T(512)S(1)}, f32[512,1024]{1,0:T(8,128)S(1)}) fusion(f32[512,1024]{1,0:T(8,128)S(1)} %get-tuple-element.216, bf16[512,4096]{1,0:T(8,128)(2,1)S(1)} %get-tuple-element.217.refs_7_, bf16[4096,1024]{1,0:T(8,128)(2,1)} %get-tuple-element.103), kind=kOutput, calls=%fused_computation.222 | convolution fusion | flops 4296539648 | bytes 16779264 | tf_op jit(solution)/shard_map/dot_general | solution.py:612
  211.4 10.1 %multiply_convert_fusion.2.refs_16_ = bf16[512,4096]{1,0:T(8,128)(2,1)S(1)} fusion(f32[512,4096]{1,0:T(8,128)} %get-tuple-element.218, bf16[512,1024]{1,0:T(8,128)(2,1)S(1)} %multiply_convert_fusion.10.refs_17_, bf16[4096,1024]{1,0:T(8,128)(2,1)} %get-tuple-element.103), kind=kOutput, calls=%fused_computation.4 | convolution fusion | flops 4313841664 | bytes 22020096 | tf_op jit(solution)/shard_map/dot_general | solution.py:622
  221.5 9.0 %multiply_reduce_fusion.8 = (f32[1024]{0:T(1024)S(1)}, f32[512]{0:T(512)S(1)}, f32[512]{0:T(512)S(1)}, f32[512,1024]{1,0:T(8,128)S(1)}) fusion(f32[512,1024]{1,0:T(8,128)S(1)} %get-tuple-element.216, f32[512]{0:T(512)S(1)} %add_rsqrt_fusion.2, f32[512]{0:T(512)S(1)} %broadcast_multiply_fusion.19, f32[1024]{0:T(1024)S(1)} %bitcast.163, ...), kind=kOutput, calls=%fused_computation.68 | convolution fusion | flops 4299159552 | bytes 16793600 | tf_op jit(solution)/shard_map/dot_general | solution.py:622
  230.6 2.8 fusion.66
  233.4 3.8 multiply_reduce_fusion.1
  237.8 14.2 %shard_map.308 = f32[32,16,128]{2,1,0:T(8,128)} custom-call(f32[16,128]{1,0:T(8,128)} %squeeze_reshape_transpose_reshape.7.mine_ref), custom_call_target="tpu_custom_call" | custom-call | tf_op jit(solution)/shard_map/pallas_call | solution.py:212
  253.0 3.4 multiply_reduce_fusion.2
  258.3 2.3 multiply_reduce_fusion.6
  262.0 1.9 multiply_convert_fusion.9
  266.1 1.4 copy-done.78
  267.5 2.8 multiply_reduce_fusion.9
  270.4 2.0 fusion.65
  273.4 2.3 convolution_convert_fusion.1
  275.7 1.6 copy.106
  277.3 4.8 multiply_reduce_fusion
  283.2 2.6 multiply_convert_fusion.1
  286.5 1.3 copy-done.3
  287.8 1.3 copy.96
  289.1 3.7 multiply_convert_fusion.6
  292.8 1.7 copy.97
  294.5 5.0 fusion.38
  299.5 1.3 copy.98
  301.4 7.6 %multiply_reduce_fusion.10 = (f32[1024]{0:T(1024)S(1)}, f32[512]{0:T(512)S(1)}, f32[512]{0:T(512)S(1)}, f32[512,1024]{1,0:T(8,128)S(1)}) fusion(f32[512,1024]{1,0:T(8,128)S(1)} %copy-done.5, f32[512]{0:T(512)S(1)} %copy-done.73, f32[512]{0:T(512)S(1)} %copy-done.69, f32[1024]{0:T(1024)S(1)} %bitcast.148, bf16[1024,3072]{1,0:T(8,128)(2,1)} %get-tuple-element.98, ...), kind=kOutput, calls=%fused_computation.70 | convolution fusion | flops 3234854912 | bytes 13647872 | tf_op jit(solution)/shard_map/dot_general | solution.py:622
  309.1 2.2 multiply_convert_fusion.5
  311.3 10.7 %multiply_convert_fusion.refs_10_ = bf16[512,4096]{1,0:T(8,128)(2,1)S(1)} fusion(f32[512,4096]{1,0:T(8,128)} %get-tuple-element.208, bf16[512,1024]{1,0:T(8,128)(2,1)S(1)} %get-tuple-element.153.refs_11_, bf16[4096,1024]{1,0:T(8,128)(2,1)} %get-tuple-element.97), kind=kOutput, calls=%fused_computation | convolution fusion | flops 4313841664 | bytes 22020096 | tf_op jit(solution)/shard_map/dot_general | solution.py:622
  322.6 1.4 fusion.77
  326.0 1.5 multiply_reduce_fusion.11
  327.5 1.7 divide_convert_fusion.2
  330.1 1.3 fusion.79
  332.6 6.4 fusion.28
  339.9 1.5 pad_maximum_fusion.1.refs_14_
  342.5 1.8 pad_maximum_fusion.refs_12_
  344.3 1.3 copy.95.refs_3_
  345.6 320.9 %shard_map.309 = (bf16[256,4096]{1,0:T(8,128)(2,1)}, bf16[1024,1024]{1,0:T(8,128)(2,1)}, bf16[256,3072]{1,0:T(8,128)(2,1)}, bf16[256,1024]{1,0:T(8,128)(2,1)}, b...) custom-call(bf16[512,1024]{1,0:T(8,128)(2,1)} %copy-done.35, ...), custom_call_target="tpu_custom_call" | custom-call | tf_op jit(solution)/shard_map/pallas_call | solution.py:593
  666.5 4.3 convert_multiply_fusion
  670.8 2.5 convert_multiply_fusion.1
  673.3 2.6 convert_multiply_fusion.2
  675.9 2.5 convert_multiply_fusion.3
  678.5 2.0 convert_multiply_fusion.4
  680.5 1.6 convert_multiply_fusion.5
  689.4 3.7 fusion.23
  693.2 2.2 convolution_convert_fusion.2
  (281 shorter events, 42.6 us)
Async XLA Ops:
  2.0 112.9 %copy-start.16 = (bf16[512,1024]{1,0:T(8,128)(2,1)S(1)}, bf16[512,1024]{1,0:T(8,128)(2,1)}, u32[]{:S(2)}) copy-start(bf16[512,1024]{1,0:T(8,128)(2,1)} %param.19) | copy-start | bytes 3145732
  114.9 18.7 %copy-start.62 = (f32[1,4,256]{2,0,1:T(1,128)}, f32[1,4,256]{2,0,1:T(1,128)S(1)}, u32[]{:S(2)}) copy-start(f32[1,4,256]{2,0,1:T(1,128)S(1)} %get-tuple-element.195) | copy-start | bytes 12292
  115.6 13.0 %copy-start.74 = (f32[512]{0:T(512)}, f32[512]{0:T(512)S(1)}, u32[]{:S(2)}) copy-start(f32[512]{0:T(512)S(1)} %add_rsqrt_fusion.5) | copy-start | bytes 6148
  115.6 13.0 %slice-start.4 = ((s8[8388608]{0:T(1024)(128)(4,1)}), s8[4194304]{0:T(1024)(128)(4,1)S(1)}, s32[]{:S(2)}) async-start(s8[8388608]{0:T(1024)(128)(4,1)} %bitcast.198), calls=%async_computation.4 | async-start | bytes 8388608
  115.6 18.7 %slice-start.8 = ((s8[6291456]{0:T(1024)(128)(4,1)}), s8[4194304]{0:T(1024)(128)(4,1)S(1)}, s32[]{:S(2)}) async-start(s8[6291456]{0:T(1024)(128)(4,1)} %bitcast.202), calls=%async_computation.8 | async-start | bytes 8388608
  117.1 11.5 %copy-start.35 = (bf16[512,1024]{1,0:T(8,128)(2,1)}, bf16[512,1024]{1,0:T(8,128)(2,1)S(1)}, u32[]{:S(2)}) copy-start(bf16[512,1024]{1,0:T(8,128)(2,1)S(1)} %get-tuple-element.180.refs_0_) | copy-start | bytes 3145732
  117.1 11.5 %slice-start.5 = ((s8[8388608]{0:T(1024)(128)(4,1)}), s8[4194304]{0:T(1024)(128)(4,1)S(1)}, s32[]{:S(2)}) async-start(s8[8388608]{0:T(1024)(128)(4,1)} %bitcast.198), calls=%async_computation.5 | async-start | bytes 8388608
  117.1 17.2 %slice-start.9 = ((s8[6291456]{0:T(1024)(128)(4,1)}), s8[2097152]{0:T(1024)(128)(4,1)S(1)}, s32[]{:S(2)}) async-start(s8[6291456]{0:T(1024)(128)(4,1)} %bitcast.202), calls=%async_computation.9 | async-start | bytes 4194304
  128.6 4.7 copy-start.23
  133.3 18.9 %copy-start.4 = (f32[512,1024]{1,0:T(8,128)}, f32[512,1024]{1,0:T(8,128)S(1)}, u32[]{:S(2)}) copy-start(f32[512,1024]{1,0:T(8,128)S(1)} %get-tuple-element.210) | copy-start | bytes 6291460
  133.6 4.3 copy-start.72
  134.3 3.7 copy-start.27
  139.7 4.0 copy-start.86
  147.1 3.4 copy-start
  147.1 3.4 copy-start.37
  153.6 3.3 copy-start.77
  159.3 4.5 copy-start.1
  160.6 3.2 copy-start.9
  160.6 3.2 copy-start.15
  161.2 5.0 copy-start.11
  161.2 5.0 copy-start.13
  185.4 2.8 copy-start.7
  185.4 2.8 copy-start.84
  187.5 2.8 slice-start.6
  188.2 3.1 slice-start.7
  190.2 8.6 %copy-start.30 = (bf16[512,1024]{1,0:T(8,128)(2,1)}, bf16[512,1024]{1,0:T(8,128)(2,1)S(1)}, u32[]{:S(2)}) copy-start(bf16[512,1024]{1,0:T(8,128)(2,1)S(1)} %multiply_convert_fusion.12.refs_6_) | copy-start | bytes 3145732
  198.8 8.5 %copy-start.24 = (bf16[512,4096]{1,0:T(8,128)(2,1)}, bf16[512,4096]{1,0:T(8,128)(2,1)S(1)}, u32[]{:S(2)}) copy-start(bf16[512,4096]{1,0:T(8,128)(2,1)S(1)} %get-tuple-element.217.refs_7_) | copy-start | bytes 12582916
  221.5 9.0 %copy-start.25 = (bf16[512,4096]{1,0:T(8,128)(2,1)}, bf16[512,4096]{1,0:T(8,128)(2,1)S(1)}, u32[]{:S(2)}) copy-start(bf16[512,4096]{1,0:T(8,128)(2,1)S(1)} %multiply_convert_fusion.2.refs_16_) | copy-start | bytes 12582916
  233.4 3.8 copy-start.48
  253.0 3.5 copy-start.2
  253.0 4.1 copy-start.10
  253.0 4.7 copy-start.12
  253.0 5.3 copy-start.14
  263.9 3.6 copy-start.78
  264.8 5.5 copy-start.42
  267.5 2.8 copy-start.22
  270.3 3.0 copy-start.83
  277.2 4.9 slice-start
  277.3 5.9 slice-start.1
  283.2 2.6 copy-start.19
  294.5 6.3 copy-start.63
  294.5 6.3 copy-start.69
  294.5 6.3 copy-start.73
  301.4 7.7 %copy-start.20 = (f32[512,1024]{1,0:T(8,128)S(1)}, f32[512,1024]{1,0:T(8,128)}, u32[]{:S(2)}) copy-start(f32[512,1024]{1,0:T(8,128)} %get-tuple-element.156) | copy-start | bytes 6291460
  311.3 10.7 %copy-start.33 = (bf16[512,1024]{1,0:T(8,128)(2,1)}, bf16[512,1024]{1,0:T(8,128)(2,1)S(1)}, u32[]{:S(2)}) copy-start(bf16[512,1024]{1,0:T(8,128)(2,1)S(1)} %get-tuple-element.153.refs_11_) | copy-start | bytes 3145732
  311.3 11.3 %copy-start.34 = (bf16[512,1024]{1,0:T(8,128)(2,1)S(1)}, bf16[512,1024]{1,0:T(8,128)(2,1)}, u32[]{:S(2)}) copy-start(bf16[512,1024]{1,0:T(8,128)(2,1)} %get-tuple-element.179.refs_8_) | copy-start | bytes 3145732
  311.3 11.4 %copy-start.81 = (bf16[1024,1024]{1,0:T(8,128)(2,1)S(1)}, bf16[1024,1024]{1,0:T(8,128)(2,1)}, u32[]{:S(2)}) copy-start(bf16[1024,1024]{1,0:T(8,128)(2,1)} %get-tuple-element.104) | copy-start | bytes 6291460
  311.3 11.4 %copy-start.85 = (bf16[512,1024]{1,0:T(8,128)(2,1)S(1)}, bf16[512,1024]{1,0:T(8,128)(2,1)}, u32[]{:S(2)}) copy-start(bf16[512,1024]{1,0:T(8,128)(2,1)} %param.21) | copy-start | bytes 3145732
  322.0 9.5 %copy-start.26 = (bf16[512,4096]{1,0:T(8,128)(2,1)}, bf16[512,4096]{1,0:T(8,128)(2,1)S(1)}, u32[]{:S(2)}) copy-start(bf16[512,4096]{1,0:T(8,128)(2,1)S(1)} %multiply_convert_fusion.refs_10_) | copy-start | bytes 12582916
  327.5 4.0 slice-start.2
  330.1 2.5 slice-start.3
  332.6 6.5 copy-start.52
  332.6 7.3 %copy-start.40 = (bf16[512,1024]{1,0:T(8,128)(2,1)S(1)}, bf16[512,1024]{1,0:T(8,128)(2,1)}, u32[]{:S(2)}) copy-start(bf16[512,1024]{1,0:T(8,128)(2,1)} %copy-done.39) | copy-start | bytes 3145732
  332.6 7.3 %copy-start.43 = (bf16[512,1024]{1,0:T(8,128)(2,1)S(1)}, bf16[512,1024]{1,0:T(8,128)(2,1)}, u32[]{:S(2)}) copy-start(bf16[512,1024]{1,0:T(8,128)(2,1)} %copy-done.42) | copy-start | bytes 3145732
  339.9 2.6 copy-start.47
  666.5 4.4 copy-start.51
  670.8 2.5 copy-start.50
  673.3 2.6 copy-start.49
  675.9 2.5 copy-start.53
  680.5 2.7 copy-start.60
  682.1 3.3 copy-start.58
  684.3 5.1 copy-start.21
  689.4 3.8 copy-start.41
  689.4 3.8 copy-start.80
  (33 other events, 51.3 us)

commit v3 on v2

--- a/solution.py
+++ b/solution.py
@@ -158,7 +158,7 @@
     )(*shards)
 
 
-def spread_kernel(across, within, mine_ref, all_ref, send, recv):
+def exchange_all(across, within, mine_ref, all_ref, send, recv):
     total = across * within
     me = lax.axis_index("wide") * within + lax.axis_index("narrow")
 
@@ -173,7 +173,6 @@
         return carry
 
     lax.fori_loop(1, total, greet, 0)
-    pl.semaphore_wait(barrier, total - 1)
 
     def copy_of(step):
         return pltpu.make_async_remote_copy(
@@ -189,35 +188,144 @@
         copy_of(step).start()
         return carry
 
-    lax.fori_loop(1, total, begin, 0)
-    all_ref[me] = mine_ref[...]
-
     def finish(step, carry):
         copy_of(step).wait()
         return carry
 
-    lax.fori_loop(1, total, finish, 0)
+    def run():
+        pl.semaphore_wait(barrier, total - 1)
+        lax.fori_loop(1, total, begin, 0)
+        all_ref[me] = mine_ref[...]
+        lax.fori_loop(1, total, finish, 0)
+
+    return run
+
+
+LANES = 128
+
+
+def row_masks(segments, taps, masks):
+    rows = segments.shape[0]
+    segment = jnp.broadcast_to(segments[...], (rows, LANES))
+    position = lax.broadcasted_iota(jnp.int32, (rows, LANES), 0)
+    for tap in range(taps):
+        offset = tap - taps // 2
+        there = pltpu.roll(segment, -offset % rows, 0) if offset else segment
+        inside = (position + offset >= 0) & (position + offset < rows)
+        masks[tap] = jnp.where(inside & (there == segment), 1.0, 0.0)
+
+
+def moved(value, offset):
+    return pltpu.roll(value, -offset % value.shape[0], 0) if offset else value
+
+
+def convolve_kernel(
+    across, within, taps, gates, segments, valids, small, active, hats, stats,
+    mine, everyone, convolved, masks, send, recv,
+):
+    share = exchange_all(across, within, mine, everyone, send, recv)
+    rows, width = hats.shape
+    chunks = width // LANES
+    row_masks(segments, taps, masks)
+    valid = jnp.broadcast_to(valids[...], (rows, LANES))
+    here = jnp.sum(valid, axis=0, keepdims=True)
+    mine[2 * chunks : 2 * chunks + 1, :] = here
+    for chunk in range(chunks):
+        at = pl.ds(chunk * LANES, LANES)
+        gated = gates[:, at] * jax.nn.sigmoid(gates[:, pl.ds(width + chunk * LANES, LANES)])
+        total = jnp.zeros_like(gated)
+        for tap in range(taps):
+            total += small[1 + tap : 2 + tap, at] * moved(gated, tap - taps // 2) * masks[tap]
+        convolved[:, at] = total
+        summed = jnp.sum(total * valid, axis=0, keepdims=True)
+        off = (total - summed / jnp.maximum(here, 1.0)) * valid
+        mine[chunk : chunk + 1, :] = summed
+        mine[chunks + chunk : chunks + chunk + 1, :] = jnp.sum(off * off, axis=0, keepdims=True)
+    share()
+    counts = everyone[:, 2 * chunks, :]
+    count = jnp.sum(counts, axis=0, keepdims=True)
+    for chunk in range(chunks):
+        at = pl.ds(chunk * LANES, LANES)
+        totals = everyone[:, chunk, :]
+        mean = jnp.sum(totals, axis=0, keepdims=True) / count
+        apart = totals / jnp.maximum(counts, 1.0) - mean
+        squares = everyone[:, chunks + chunk, :] + counts * apart * apart
+        inverse = lax.rsqrt(jnp.sum(squares, axis=0, keepdims=True) / count + EPSILON)
+        stats[0:1, at] = inverse
+        stats[1:2, at] = count
+        hat = (convolved[:, at] - mean) * inverse
+        hats[:, at] = hat
+        out = hat * small[1 + taps : 2 + taps, at] + small[2 + taps : 3 + taps, at]
+        active[:, at] = (out * jax.nn.sigmoid(out)).astype(jnp.bfloat16)
+
+
+def convolve_back_kernel(
+    across, within, taps, adjoint, gates, hats, stats, segments, valids, small, adjoint_gates, sums,
+    mine, everyone, adjoint_hats, masks, send, recv,
+):
+    share = exchange_all(across, within, mine, everyone, send, recv)
+    rows, width = hats.shape
+    chunks = width // LANES
+    row_masks(segments, taps, masks)
+    valid = jnp.broadcast_to(valids[...], (rows, LANES))
+    for chunk in range(chunks):
+        at = pl.ds(chunk * LANES, LANES)
+        hat, gain = hats[:, at], small[1 + taps : 2 + taps, at]
+        adjoint_batch = adjoint[:, at] * swish_slope(hat * gain + small[2 + taps : 3 + taps, at])
+        sums[taps : taps + 1, at] = jnp.sum(adjoint_batch * hat, axis=0, keepdims=True)
+        sums[taps + 1 : taps + 2, at] = jnp.sum(adjoint_batch, axis=0, keepdims=True)
+        adjoint_hat = adjoint_batch * gain
+        adjoint_hats[:, at] = adjoint_hat
+        counted = adjoint_hat * valid
+        mine[chunk : chunk + 1, :] = jnp.sum(counted, axis=0, keepdims=True)
+        mine[chunks + chunk : chunks + chunk + 1, :] = jnp.sum(counted * hat, axis=0, keepdims=True)
+    share()
+    for chunk in range(chunks):
+        at = pl.ds(chunk * LANES, LANES)
+        right_at = pl.ds(width + chunk * LANES, LANES)
+        first = jnp.sum(everyone[:, chunk, :], axis=0, keepdims=True)
+        second = jnp.sum(everyone[:, chunks + chunk, :], axis=0, keepdims=True)
+        adjoint_conv = stats[0:1, at] * (
+            adjoint_hats[:, at] - valid * (first + hats[:, at] * second) / stats[1:2, at]
+        )
+        sigmoid, left = jax.nn.sigmoid(gates[:, right_at]), gates[:, at]
+        gated = left * sigmoid
+        adjoint_gated = jnp.zeros_like(gated)
+        for tap in range(taps):
+            offset = tap - taps // 2
+            masked = adjoint_conv * masks[tap]
+            sums[tap : tap + 1, at] = jnp.sum(masked * moved(gated, offset), axis=0, keepdims=True)
+            adjoint_gated += moved(masked * small[1 + tap : 2 + tap, at], -offset)
+        adjoint_gates[:, at] = (adjoint_gated * sigmoid).astype(jnp.bfloat16)
+        adjoint_gates[:, right_at] = (adjoint_gated * gated * (1.0 - sigmoid)).astype(jnp.bfloat16)
+
+
+def convolution_call(kernel, identity, inputs, out_shape, shared_rows, taps):
+    across, within = lax.axis_size("wide"), lax.axis_size("narrow")
+    rows, width = inputs[0].shape[0], out_shape[1].shape[1]
+    here = pl.BlockSpec(memory_space=pltpu.VMEM)
+    high = jnp.float32
+    return pl.pallas_call(
+        functools.partial(kernel, across, within, taps),
+        out_shape=out_shape,
+        in_specs=[here] * len(inputs),
+        out_specs=[here] * len(out_shape),
+        scratch_shapes=[
+            pltpu.VMEM((shared_rows, LANES), high),
+            pltpu.VMEM((across * within, shared_rows, LANES), high),
+            pltpu.VMEM((rows, width), high),
+            pltpu.VMEM((taps, rows, LANES), high),
+            pltpu.SemaphoreType.DMA((across * within,)),
+            pltpu.SemaphoreType.DMA((across * within,)),
+        ],
+        compiler_params=pltpu.CompilerParams(collective_id=identity, has_side_effects=True),
+    )(*inputs)
 
 
 def columns_split(small, pieces):
     rows, width = small.shape
     split = jnp.transpose(small.reshape(rows, pieces, width // pieces), (1, 0, 2))
     return split.reshape(pieces, rows * width // pieces // 128, 128)
-
-
-def from_all(mine, identity):
-    across, within = lax.axis_size("wide"), lax.axis_size("narrow")
-    total = across * within
-    flat = columns_split(mine, 1)[0]
-    everyone = pl.pallas_call(
-        functools.partial(spread_kernel, across, within),
-        out_shape=jax.ShapeDtypeStruct((total,) + flat.shape, flat.dtype),
-        in_specs=[pl.BlockSpec(memory_space=pltpu.VMEM)],
-        out_specs=pl.BlockSpec(memory_space=pltpu.VMEM),
-        scratch_shapes=[pltpu.SemaphoreType.DMA((total,)), pltpu.SemaphoreType.DMA((total,))],
-        compiler_params=pltpu.CompilerParams(collective_id=identity, has_side_effects=True),
-    )(flat)
-    return everyone.reshape((total,) + mine.shape)
 
 
 COLS = 256
@@ -647,38 +755,6 @@
     return (adjoint_in, gain_sum)
 
 
-def shift_rows(values, offset, fill):
-    if offset == 0:
-        return values
-    padding = jnp.full((abs(offset),) + values.shape[1:], fill, values.dtype)
-    if offset > 0:
-        return jnp.concatenate([values[offset:], padding], axis=0)
-    return jnp.concatenate([padding, values[:offset]], axis=0)
-
-
-def depthwise(values, kernel, segment):
-    taps = kernel.shape[0]
-    total = jnp.zeros_like(values)
-    for tap_index in range(taps):
-        offset = tap_index - taps // 2
-        same_segment = (shift_rows(segment, offset, -1) == segment).astype(jnp.float32)[:, None]
-        total = total + kernel[tap_index] * shift_rows(values, offset, 0.0) * same_segment
-    return total
-
-
-def depthwise_back(adjoint, values, kernel, segment):
-    taps = kernel.shape[0]
-    adjoint_values = jnp.zeros_like(values)
-    kernel_rows = []
-    for tap_index in range(taps):
-        offset = tap_index - taps // 2
-        same_segment = (shift_rows(segment, offset, -1) == segment).astype(jnp.float32)[:, None]
-        masked = adjoint * same_segment
-        kernel_rows.append(jnp.sum(masked * shift_rows(values, offset, 0.0), axis=0))
-        adjoint_values = adjoint_values + shift_rows(masked * kernel[tap_index], -offset, 0.0)
-    return (adjoint_values, jnp.stack(kernel_rows))
-
-
 def feed_forward(values, weight_in, weight_out, gain):
     normed, normal_hat, scale = layer_norm(values, gain)
     entry = normed.astype(jnp.bfloat16)
@@ -705,12 +781,60 @@
     )
 
 
-def masked_scores(query_block, segment_block, keys, segment, factor):
-    scores = (
-        jnp.einsum("ihd,jhd->hij", query_block, keys, preferred_element_type=jnp.float32) * factor
-    )
-    allowed = segment_block[:, None] == segment[None, :]
-    return jnp.where(allowed[None], scores, NEGATIVE)
+def head_weights(query, key, rows, columns, factor):
+    scores = against(query, key) * factor
+    scores = jnp.where(rows == columns, scores, NEGATIVE)
+    exponent = jnp.exp(scores - jnp.max(scores, axis=-1, keepdims=True))
+    return exponent / jnp.sum(exponent, axis=-1, keepdims=True)
+
+
+def attend_kernel(factor, query, key, value, rows, columns, result):
+    weights = head_weights(query[...], key[...], rows[...], columns[...], factor)
+    result[...] = matmul(weights.astype(jnp.bfloat16), value[...]).astype(jnp.bfloat16)
+
+
+def attend_back_kernel(factor, heads, query, key, value, adjoint, rows, columns, result):
+    weights = head_weights(query[...], key[...], rows[...], columns[...], factor)
+    adjoint_weights = against(adjoint[...], value[...])
+    inner = jnp.sum(weights * adjoint_weights, axis=-1, keepdims=True)
+    adjoint_scores = (weights * (adjoint_weights - inner)).astype(jnp.bfloat16)
+    head_dim = query.shape[1]
+    head = pl.program_id(0)
+    for place, part in enumerate(
+        (
+            matmul(adjoint_scores, key[...]) * factor,
+            across_rows(adjoint_scores, query[...]) * factor,
+            across_rows(weights.astype(jnp.bfloat16), adjoint[...]),
+        )
+    ):
+        at = pl.multiple_of((place * heads + head) * head_dim, head_dim)
+        result[:, pl.ds(at, head_dim)] = part.astype(jnp.bfloat16)
+
+
+def over_heads(kernel, mixed, extra, segment, heads, out_shape, out_spec, products):
+    row_count = mixed.shape[0]
+    head_dim = mixed.shape[1] // 3 // heads
+
+    def block(place):
+        return pl.BlockSpec((row_count, head_dim), lambda head: (0, place * heads + head))
+
+    return pl.pallas_call(
+        kernel,
+        grid=(heads,),
+        out_shape=out_shape,
+        in_specs=[block(0), block(1), block(2)]
+        + [block(0)] * len(extra)
+        + [
+            pl.BlockSpec((row_count, 1), lambda head: (0, 0)),
+            pl.BlockSpec((1, row_count), lambda head: (0, 0)),
+        ],
+        out_specs=out_spec,
+        cost_estimate=pl.CostEstimate(
+            flops=products * 2 * heads * row_count * row_count * head_dim,
+            bytes_accessed=16 * row_count * heads * head_dim,
+            transcendentals=heads * row_count * row_count,
+        ),
+    )(mixed, mixed, mixed, *extra, segment[:, None], segment[None, :])
 
 
 def attention_forward(values, weight_in, weight_out, gain, segment, heads):
@@ -719,101 +843,35 @@
     mixed = matmul(entry, weight_in).astype(jnp.bfloat16)
     row_count, width = values.shape
     head_dim = width // heads
-    block = min(512, row_count)
-    blocks = row_count // block
-    queries = mixed[:, :width].reshape(blocks, block, heads, head_dim)
-    keys = mixed[:, width : 2 * width].reshape(row_count, heads, head_dim)
-    head_values = mixed[:, 2 * width :].reshape(row_count, heads, head_dim)
-    segment_blocks = segment.reshape(blocks, block)
-    factor = head_dim ** (-0.5)
-
-    def attend(pieces):
-        query_block, segment_block = pieces
-        scores = masked_scores(query_block, segment_block, keys, segment, factor)
-        top = jnp.max(scores, axis=-1, keepdims=True)
-        exponent = jnp.exp(scores - top)
-        total = jnp.sum(exponent, axis=-1, keepdims=True)
-        weights = (exponent / total).astype(jnp.bfloat16)
-        result = jnp.einsum(
-            "hij,jhd->ihd", weights, head_values, preferred_element_type=jnp.float32
-        )
-        return (result.astype(jnp.bfloat16), (top + jnp.log(total))[..., 0])
-
-    outputs, log_totals = lax.map(attend, (queries, segment_blocks))
-    heads_out = outputs.reshape(row_count, width)
+    heads_out = over_heads(
+        functools.partial(attend_kernel, head_dim ** (-0.5)),
+        mixed,
+        (),
+        segment,
+        heads,
+        jax.ShapeDtypeStruct((row_count, width), jnp.bfloat16),
+        pl.BlockSpec((row_count, head_dim), lambda head: (0, head)),
+        2,
+    )
     branch = matmul(heads_out, weight_out)
-    kept = (
-        entry,
-        normal_hat,
-        scale,
-        queries,
-        keys,
-        head_values,
-        segment_blocks,
-        log_totals,
-        heads_out,
-    )
-    return (values + branch, kept)
+    return (values + branch, (entry, normal_hat, scale, mixed, heads_out))
 
 
 def attention_back(adjoint, kept, weight_in, weight_out, gain, segment, heads):
-    entry, normal_hat, scale, queries, keys, head_values, segment_blocks, log_totals, heads_out = (
-        kept
-    )
-    row_count, width = adjoint.shape
-    blocks = queries.shape[0]
-    block = queries.shape[1]
-    head_dim = width // heads
-    factor = head_dim ** (-0.5)
+    entry, normal_hat, scale, mixed, heads_out = kept
+    head_dim = adjoint.shape[1] // heads
     adjoint_branch = adjoint.astype(jnp.bfloat16)
-    adjoint_heads = (
-        against(adjoint_branch, weight_out)
-        .astype(jnp.bfloat16)
-        .reshape(blocks, block, heads, head_dim)
-    )
-
-    def step_back(carry, pieces):
-        key_sum, value_sum = carry
-        query_block, segment_block, log_block, adjoint_block = pieces
-        scores = masked_scores(query_block, segment_block, keys, segment, factor)
-        weights = jnp.exp(scores - log_block[..., None])
-        value_sum = value_sum + jnp.einsum(
-            "hij,ihd->jhd",
-            weights.astype(jnp.bfloat16),
-            adjoint_block,
-            preferred_element_type=jnp.float32,
-        )
-        adjoint_weights = jnp.einsum(
-            "ihd,jhd->hij", adjoint_block, head_values, preferred_element_type=jnp.float32
-        )
-        adjoint_scores = (
-            weights * (adjoint_weights - jnp.sum(weights * adjoint_weights, axis=-1, keepdims=True))
-        ).astype(jnp.bfloat16)
-        query_adjoint = (
-            jnp.einsum("hij,jhd->ihd", adjoint_scores, keys, preferred_element_type=jnp.float32)
-            * factor
-        )
-        key_sum = (
-            key_sum
-            + jnp.einsum(
-                "hij,ihd->jhd", adjoint_scores, query_block, preferred_element_type=jnp.float32
-            )
-            * factor
-        )
-        return ((key_sum, value_sum), query_adjoint)
-
-    zeros = jnp.zeros((row_count, heads, head_dim), jnp.float32)
-    sums, query_adjoints = lax.scan(
-        step_back, (zeros, zeros), (queries, segment_blocks, log_totals, adjoint_heads)
-    )
-    adjoint_mixed = jnp.concatenate(
-        [
-            query_adjoints.reshape(row_count, width),
-            sums[0].reshape(row_count, width),
-            sums[1].reshape(row_count, width),
-        ],
-        axis=1,
-    ).astype(jnp.bfloat16)
+    adjoint_heads = against(adjoint_branch, weight_out).astype(jnp.bfloat16)
+    adjoint_mixed = over_heads(
+        functools.partial(attend_back_kernel, head_dim ** (-0.5), heads),
+        mixed,
+        (adjoint_heads,),
+        segment,
+        heads,
+        jax.ShapeDtypeStruct(mixed.shape, jnp.bfloat16),
+        pl.BlockSpec(mixed.shape, lambda head: (0, 0)),
+        5,
+    )
     adjoint_values, gain_sum = norm_back(against(adjoint_mixed, weight_in), normal_hat, scale, gain)
     return (
         adjoint + adjoint_values,
@@ -828,100 +886,44 @@
     normed, normal_hat, scale = layer_norm(values, small[0])
     entry = normed.astype(jnp.bfloat16)
     gates = matmul(entry, weight_in)
-    width = values.shape[1]
-    sigmoid_right = jax.nn.sigmoid(gates[:, width:])
-    gated = gates[:, :width] * sigmoid_right
-    convolved = depthwise(gated, small[1 : 1 + taps], segment)
-    here = jnp.sum(valid)
-    total_here = jnp.sum(convolved * valid, axis=0)
-    off = (convolved - total_here / jnp.maximum(here, 1.0)) * valid
-    mine = jnp.stack([jnp.full((width,), here), total_here, jnp.sum(off * off, axis=0)])
-    everyone = from_all(mine, 1)
-    counts, totals, squares = everyone[:, 0], everyone[:, 1], everyone[:, 2]
-    count = jnp.sum(counts, axis=0)
-    mean = jnp.sum(totals, axis=0) / count
-    apart = totals / jnp.maximum(counts, 1.0) - mean
-    spread = jnp.sum(squares + counts * apart * apart, axis=0) / count
-    centred = convolved - mean
-    inverse = lax.rsqrt(spread + EPSILON)
-    batch_hat = centred * inverse
-    batch_out = batch_hat * small[1 + taps] + small[2 + taps]
-    active = (batch_out * jax.nn.sigmoid(batch_out)).astype(jnp.bfloat16)
+    high = jnp.float32
+    columns = (segment[:, None], valid)
+    active, hats, stats = convolution_call(
+        convolve_kernel,
+        1,
+        (gates,) + columns + (small,),
+        [
+            jax.ShapeDtypeStruct(values.shape, jnp.bfloat16),
+            jax.ShapeDtypeStruct(values.shape, high),
+            jax.ShapeDtypeStruct((2, values.shape[1]), high),
+        ],
+        2 * values.shape[1] // LANES + 1,
+        taps,
+    )
     branch = matmul(active, weight_out)
-    kept = (
-        entry,
-        normal_hat,
-        scale,
-        gates,
-        sigmoid_right,
-        gated,
-        batch_hat,
-        batch_out,
-        active,
-        inverse,
-        count,
-    )
-    return (values + branch, kept)
-
-
-def convolution_back(adjoint, kept, weight_in, weight_out, small, segment, valid):
-    (
-        entry,
-        normal_hat,
-        scale,
-        gates,
-        sigmoid_right,
-        gated,
-        batch_hat,
-        batch_out,
-        active,
-        inverse,
-        count,
-    ) = kept
+    return (values + branch, (entry, normal_hat, scale, gates, hats, stats, active, columns))
+
+
+def convolution_back(adjoint, kept, weight_in, weight_out, small):
+    entry, normal_hat, scale, gates, hats, stats, active, columns = kept
     taps = small.shape[0] - 3
-    width = adjoint.shape[1]
     adjoint_branch = adjoint.astype(jnp.bfloat16)
-    adjoint_batch = against(adjoint_branch, weight_out) * swish_slope(batch_out)
-    shift_sum = jnp.sum(adjoint_batch, axis=0)
-    batch_gain_sum = jnp.sum(adjoint_batch * batch_hat, axis=0)
-    adjoint_hat = adjoint_batch * small[1 + taps]
-    sums = jnp.sum(
-        from_all(
-            jnp.stack(
-                [
-                    jnp.sum(adjoint_hat * valid, axis=0),
-                    jnp.sum(adjoint_hat * batch_hat * valid, axis=0),
-                ]
-            ),
-            2,
-        ),
-        axis=0,
-    )
-    first_total, second_total = sums[0], sums[1]
-    adjoint_conv = inverse * (
-        adjoint_hat - valid * (first_total + batch_hat * second_total) / count
-    )
-    adjoint_gated, kernel_sum = depthwise_back(adjoint_conv, gated, small[1 : 1 + taps], segment)
-    left_half = gates[:, :width]
-    adjoint_gates = jnp.concatenate(
+    adjoint_gates, sums = convolution_call(
+        convolve_back_kernel,
+        2,
+        (against(adjoint_branch, weight_out), gates, hats, stats) + columns + (small,),
         [
-            adjoint_gated * sigmoid_right,
-            adjoint_gated * left_half * sigmoid_right * (1.0 - sigmoid_right),
+            jax.ShapeDtypeStruct(gates.shape, jnp.bfloat16),
+            jax.ShapeDtypeStruct((taps + 2, adjoint.shape[1]), jnp.float32),
         ],
-        axis=1,
-    ).astype(jnp.bfloat16)
+        2 * adjoint.shape[1] // LANES,
+        taps,
+    )
     adjoint_values, gain_sum = norm_back(
         against(adjoint_gates, weight_in), normal_hat, scale, small[0]
     )
-    small_sum = jnp.concatenate(
-        [gain_sum[None], kernel_sum, batch_gain_sum[None], shift_sum[None]], axis=0
-    )
-    return (
-        adjoint + adjoint_values,
-        (entry, adjoint_gates),
-        (active, adjoint_branch),
-        small_sum,
-    )
+    small_sum = jnp.concatenate([gain_sum[None], sums], axis=0)
+    return (adjoint + adjoint_values, (entry, adjoint_gates), (active, adjoint_branch), small_sum)
 
 
 def per_device(
@@ -1031,7 +1033,7 @@
         adjoint, second_kept, second_up, second_down, gains[4]
     )
     adjoint, pointwise_in_pair, pointwise_out_pair, conv_small_sum = convolution_back(
-        adjoint, conv_kept, pointwise_in, pointwise_out, conv_small, segment, valid
+        adjoint, conv_kept, pointwise_in, pointwise_out, conv_small
     )
     adjoint, attention_in_pair, attention_out_pair, attend_gain_sum = attention_back(
         adjoint, attend_kept, attention_in, attention_out, gains[2], segment, HEADS

time: 704 us -> 671 us (0.953)
  Pallas kernels: 461 us -> 499 us
  local copies, waits for them, and re-layouts: 43 us -> 12.6 us
  other arithmetic: 69.8 us -> 44.7 us
  matrix products: 119 us -> 109 us
    pallas_call x2 -> x4, Pallas kernels: 27.8 us -> 65.3 us  [the longest x2 39.7 us: convolution_call(): pl.pallas_call(functools.partial(kernel, across, within, taps), out_shape...]
    dot_general x6 -> x0, matrix products: 18.7 us -> none  [the longest x1 4.96 us: step_back(): jnp.einsum('hij,ihd->jhd', weights.astype(jnp.bfloat16), adjoint_block, p...]
    unnamed x195 -> x130, local copies, waits for them, and re-layouts: 23 us -> 7.78 us
    reduce_sum x9 -> x0, other arithmetic: 13.9 us -> none  [the longest x2 5.69 us: depthwise_back(): jnp.sum(masked * shift_rows(values, offset, 0.0), axis=0)]
    reshape x6 -> x0, local copies, waits for them, and re-layouts: 10.1 us -> none  [the longest x1 2.47 us: attention_forward(): keys = mixed[:, width:2 * width].reshape(row_count, heads, head_dim)]
    dot_general x10, matrix products: 44.5 us -> 51.9 us  [matmul(): return jnp.dot(left, right, preferred_element_type=jnp.float32)]
where the time goes in v3:
time: 671 us; the launch traced here: 668 us
  Pallas kernels  499 us (74%)
  matrix products  109 us (16%)
  other arithmetic  44.7 us (7%)
  local copies, waits for them, and re-layouts  12.6 us (2%)
    pallas_call x1, Pallas kernels, gradients(): pl.pallas_call(functools.partial(gradient_kernel, tuple(plan), extra, cop...  321 us
    pallas_call x1, Pallas kernels, gather_all(): pl.pallas_call(functools.partial(gather_kernel, plan), out_shape=[jax.Sha...  112 us
    dot_general x10, matrix products, against(): lax.dot_general(left, right, (((1,), (1,)), ((), ())), preferred_element_...  57.3 us
    dot_general x10, matrix products, matmul(): return jnp.dot(left, right, preferred_element_type=jnp.float32)  51.9 us
    pallas_call x2, Pallas kernels, convolution_call(): pl.pallas_call(functools.partial(kernel, across, within, taps), out_shape...  39.7 us
    pallas_call x2, Pallas kernels, over_heads(): pl.pallas_call(kernel, grid=(heads,), out_shape=out_shape, in_specs=[bloc...  25.7 us
    div x10, other arithmetic, gradients(): whole.astype(high) / float(copies)  20 us

profile of v3, /device:TPU:0, one launch (start us, length us, event | category | flops | bytes accessed | tf_op | source)
XLA Modules:
  0.0 667.5 jit_solution(16838916665219113322)
XLA Ops:
  0.6 1.3 fusion.33.refs_10_
  2.0 112.1 %shard_map.306 = (bf16[1024,1024]{1,0:T(8,128)(2,1)}, bf16[1024,2048]{1,0:T(8,128)(2,1)}, bf16[1024,3072]{1,0:T(8,128)(2,1)}, bf16[1024,4096]{1,0:T(8,128)(2,1)}...) custom-call(bf16[256,1024]{1,0:T(8,128)(2,1)} %refs_0_.1, ...), custom_call_target="tpu_custom_call" | custom-call | tf_op jit(solution)/shard_map/pallas_call | solution.py:142
  114.1 0.8 copy.61
  115.6 1.5 fusion.11
  117.1 11.6 %multiply_convert_fusion.3 = (bf16[512,4096]{1,0:T(8,128)(2,1)S(1)}, f32[512,4096]{1,0:T(8,128)}) fusion(bf16[512,1024]{1,0:T(8,128)(2,1)S(1)} %get-tuple-element.101.refs_0_, bf16[1024,4096]{1,0:T(8,128)(2,1)} %get-tuple-element.44), kind=kOutput, calls=%fused_computation.4 | convolution fusion | flops 4305453056 | bytes 22020096 | tf_op jit(solution)/shard_map/dot_general | solution.py:720
  128.8 4.7 fusion.39
  134.2 4.8 convolution_convert_fusion.query.key.value
  139.2 0.9 copy.44.rows.segments
  140.1 10.6 %shard_map.307.refs_3_ = bf16[512,1024]{1,0:T(8,128)(2,1)} custom-call(bf16[512,3072]{1,0:T(8,128)(2,1)} %convolution_convert_fusion.query.key.value, bf16[512,3072]{1,0:T(8,128)(2,1)} %convolution_convert_fusion.query.key.value, bf16[512,3072]{1,0:T(8,128)(2,1)} %convolution_convert_fusion.query.key.value, s32[512,1]{1,0:T(8,128)} %copy.44.rows.segments, ...), custom_call_target="tpu_custom_call" | custom-call | flops 1073741824 | bytes 8388608 | tf_op jit(solution)/shard_map/pallas_call | solution.py:821
  150.7 3.3 fusion.40
  154.7 0.6 copy-done
  155.3 2.0 copy-done.44
  157.3 4.4 fusion.44.gates
  161.7 0.6 pad_maximum_fusion.small
  162.3 0.6 slice.69
  162.9 1.4 fusion.28.valids
  164.3 16.6 %shard_map.308 = (bf16[512,1024]{1,0:T(8,128)(2,1)}, f32[512,1024]{1,0:T(8,128)}, f32[2,1024]{1,0:T(2,128)}) custom-call(f32[512,2048]{1,0:T(8,128)} %fusion.44.gates, s32[512,1]{1,0:T(8,128)} %copy.44.rows.segments, f32[512,1]{1,0:T(8,128)} %fusion.28.valids, f32[8,1024]{1,0:T(8,128)} %pad_maximum_fusion.small), custom_call_target="tpu_custom_call" | custom-call | tf_op jit(solution)/shard_map/pallas_call | solution.py:308
  180.9 3.9 fusion.41
  185.5 11.1 %multiply_convert_fusion.2 = (bf16[512,4096]{1,0:T(8,128)(2,1)S(1)}, f32[512,4096]{1,0:T(8,128)}) fusion(bf16[512,1024]{1,0:T(8,128)(2,1)S(1)} %multiply_convert_fusion.7.refs_6_, bf16[1024,4096]{1,0:T(8,128)(2,1)} %get-tuple-element.51), kind=kOutput, calls=%fused_computation.2 | convolution fusion | flops 4305453056 | bytes 22020096 | tf_op jit(solution)/shard_map/dot_general | solution.py:720
  196.6 4.6 fusion.42
  201.6 0.7 fusion.34
  202.5 1.0 multiply_reduce_fusion
  203.5 0.8 multiply_convert_fusion.5.refs_17_
  204.3 1.0 copy-done.14
  205.3 10.1 %multiply_convert_fusion.1.refs_16_ = bf16[512,4096]{1,0:T(8,128)(2,1)S(1)} fusion(f32[512,4096]{1,0:T(8,128)} %get-tuple-element.118, bf16[512,1024]{1,0:T(8,128)(2,1)S(1)} %multiply_convert_fusion.5.refs_17_, bf16[4096,1024]{1,0:T(8,128)(2,1)} %get-tuple-element.52), kind=kOutput, calls=%fused_computation.1 | convolution fusion | flops 4313841664 | bytes 22020096 | tf_op jit(solution)/shard_map/dot_general | solution.py:730
  215.4 9.0 %multiply_reduce_fusion.1 = (f32[1024]{0:T(1024)S(1)}, f32[512]{0:T(512)S(1)}, f32[512]{0:T(512)S(1)}, f32[512,1024]{1,0:T(8,128)S(1)}) fusion(f32[512,1024]{1,0:T(8,128)S(1)} %get-tuple-element.116, f32[512]{0:T(512)S(1)} %add_rsqrt_fusion.1, f32[512]{0:T(512)S(1)} %broadcast_multiply_fusion.15, f32[1024]{0:T(1024)S(1)} %bitcast.111, ...), kind=kOutput, calls=%fused_computation.41 | convolution fusion | flops 4299159552 | bytes 16793600 | tf_op jit(solution)/shard_map/dot_general | solution.py:730
  224.4 2.8 fusion.38
  227.3 2.6 fusion.45.adjoint
  229.9 23.1 %shard_map.309 = (bf16[512,2048]{1,0:T(8,128)(2,1)}, f32[7,1024]{1,0:T(8,128)}) custom-call(f32[512,1024]{1,0:T(8,128)} %fusion.45.adjoint, f32[512,2048]{1,0:T(8,128)} %fusion.44.gates, f32[512,1024]{1,0:T(8,128)} %get-tuple-element.55.hats, f32[2,1024]{1,0:T(2,128)} %get-tuple-element.56.stats, s32[512,1]{1,0:T(8,128)} %copy.44.rows.segments, ...), custom_call_target="tpu_custom_call" | custom-call | tf_op jit(solution)/shard_map/pallas_call | solution.py:308
  253.0 6.4 multiply_reduce_fusion.2
  259.4 2.0 fusion.37
  261.5 1.0 copy-done.15
  262.5 2.3 convolution_convert_fusion.1.adjoint
  264.7 15.1 %shard_map.310.refs_12_ = bf16[512,3072]{1,0:T(8,128)(2,1)} custom-call(bf16[512,3072]{1,0:T(8,128)(2,1)} %convolution_convert_fusion.query.key.value, bf16[512,3072]{1,0:T(8,128)(2,1)} %convolution_convert_fusion.query.key.value, bf16[512,3072]{1,0:T(8,128)(2,1)} %convolution_convert_fusion.query.key.value, ...), custom_call_target="tpu_custom_call" | custom-call | flops 2684354560 | bytes 8388608 | tf_op jit(solution)/shard_map/pallas_call | solution.py:821
  279.8 7.3 %multiply_reduce_fusion.3 = (f32[1024]{0:T(1024)S(1)}, f32[512]{0:T(512)S(1)}, f32[512]{0:T(512)S(1)}, f32[512,1024]{1,0:T(8,128)S(1)}) fusion(f32[512,1024]{1,0:T(8,128)S(1)} %get-tuple-element.112, f32[512]{0:T(512)S(1)} %add_rsqrt_fusion.3, f32[512]{0:T(512)S(1)} %broadcast_multiply_fusion.17, f32[1024]{0:T(1024)S(1)} %bitcast.99, ...), kind=kOutput, calls=%fused_computation.43 | convolution fusion | flops 3225417728 | bytes 13647872 | tf_op jit(solution)/shard_map/dot_general | solution.py:730
  287.2 2.2 multiply_convert_fusion.4
  289.4 10.5 %multiply_convert_fusion.refs_10_ = bf16[512,4096]{1,0:T(8,128)(2,1)S(1)} fusion(f32[512,4096]{1,0:T(8,128)} %get-tuple-element.110, bf16[512,1024]{1,0:T(8,128)(2,1)S(1)} %get-tuple-element.91.refs_11_, bf16[4096,1024]{1,0:T(8,128)(2,1)} %get-tuple-element.45), kind=kOutput, calls=%fused_computation | convolution fusion | flops 4313841664 | bytes 22020096 | tf_op jit(solution)/shard_map/dot_general | solution.py:730
  300.6 1.4 fusion.43
  302.0 0.5 fusion.27
  302.5 0.7 copy-done.29
  303.4 0.6 copy-done.45
  303.9 1.4 multiply_reduce_fusion.4
  305.4 1.6 divide_convert_fusion
  307.1 1.3 fusion.46
  308.5 1.4 slice-done.1
  309.9 6.4 fusion.22
  316.5 0.6 reshape.201.refs_20_
  317.1 321.2 %shard_map.311 = (bf16[256,4096]{1,0:T(8,128)(2,1)}, bf16[1024,1024]{1,0:T(8,128)(2,1)}, bf16[256,3072]{1,0:T(8,128)(2,1)}, bf16[256,1024]{1,0:T(8,128)(2,1)}, b...) custom-call(bf16[512,1024]{1,0:T(8,128)(2,1)} %copy-done.18, ...), custom_call_target="tpu_custom_call" | custom-call | tf_op jit(solution)/shard_map/pallas_call | solution.py:701
  638.3 4.3 convert_multiply_fusion
  642.7 2.5 convert_multiply_fusion.1
  645.2 2.6 convert_multiply_fusion.2
  647.8 2.5 convert_multiply_fusion.3
  650.3 2.0 convert_multiply_fusion.4
  652.4 1.6 convert_multiply_fusion.5
  654.0 1.1 convert_multiply_fusion.10
  655.0 1.1 convert_multiply_fusion.7
  656.1 1.1 convert_multiply_fusion.8
  657.2 1.1 convert_multiply_fusion.9
  658.3 1.1 reduce_sum.327
  659.4 0.6 slice.77
  660.0 0.6 slice.79
  660.7 0.6 slice.81
  661.3 3.7 fusion.17
  665.0 2.2 convolution_convert_fusion.2
  (168 shorter events, 4.2 us)
Async XLA Ops:
  2.0 113.0 %copy-start.2 = (bf16[512,1024]{1,0:T(8,128)(2,1)S(1)}, bf16[512,1024]{1,0:T(8,128)(2,1)}, u32[]{:S(2)}) copy-start(bf16[512,1024]{1,0:T(8,128)(2,1)} %param.19) | copy-start | bytes 3145732
  114.9 2.2 copy-start.34
  114.9 2.2 copy-start.36
  115.2 1.9 copy-start.40
  115.6 13.1 %copy-start.42 = (f32[512]{0:T(512)}, f32[512]{0:T(512)S(1)}, u32[]{:S(2)}) copy-start(f32[512]{0:T(512)S(1)} %add_rsqrt_fusion.4) | copy-start | bytes 6148
  115.6 13.1 %slice-start.2 = ((s8[8388608]{0:T(1024)(128)(4,1)}), s8[4194304]{0:T(1024)(128)(4,1)S(1)}, s32[]{:S(2)}) async-start(s8[8388608]{0:T(1024)(128)(4,1)} %bitcast.127), calls=%async_computation.2 | async-start | bytes 8388608
  115.6 18.5 %slice-start.6 = ((s8[6291456]{0:T(1024)(128)(4,1)}), s8[4194304]{0:T(1024)(128)(4,1)S(1)}, s32[]{:S(2)}) async-start(s8[6291456]{0:T(1024)(128)(4,1)} %bitcast.131), calls=%async_computation.6 | async-start | bytes 8388608
  117.1 11.6 %copy-start.18 = (bf16[512,1024]{1,0:T(8,128)(2,1)}, bf16[512,1024]{1,0:T(8,128)(2,1)S(1)}, u32[]{:S(2)}) copy-start(bf16[512,1024]{1,0:T(8,128)(2,1)S(1)} %get-tuple-element.101.refs_0_) | copy-start | bytes 3145732
  117.1 11.6 %slice-start.3 = ((s8[8388608]{0:T(1024)(128)(4,1)}), s8[4194304]{0:T(1024)(128)(4,1)S(1)}, s32[]{:S(2)}) async-start(s8[8388608]{0:T(1024)(128)(4,1)} %bitcast.127), calls=%async_computation.3 | async-start | bytes 8388608
  117.1 17.0 %slice-start.7 = ((s8[6291456]{0:T(1024)(128)(4,1)}), s8[2097152]{0:T(1024)(128)(4,1)S(1)}, s32[]{:S(2)}) async-start(s8[6291456]{0:T(1024)(128)(4,1)} %bitcast.131), calls=%async_computation.7 | async-start | bytes 4194304
  128.7 4.7 copy-start.7
  134.1 4.8 copy-start.11
  134.2 4.8 copy-start.51
  139.2 0.9 copy-start.38
  153.9 1.3 copy-start
  154.0 3.3 copy-start.44
  155.3 6.4 copy-start.12
  185.1 11.5 %slice-start.4 = ((s8[8388608]{0:T(1024)(128)(4,1)}), s8[4194304]{0:T(1024)(128)(4,1)S(1)}, s32[]{:S(2)}) async-start(s8[8388608]{0:T(1024)(128)(4,1)} %bitcast.129), calls=%async_computation.4 | async-start | bytes 8388608
  185.5 11.1 %copy-start.13 = (bf16[512,1024]{1,0:T(8,128)(2,1)}, bf16[512,1024]{1,0:T(8,128)(2,1)S(1)}, u32[]{:S(2)}) copy-start(bf16[512,1024]{1,0:T(8,128)(2,1)S(1)} %multiply_convert_fusion.7.refs_6_) | copy-start | bytes 3145732
  185.5 11.1 %slice-start.5 = ((s8[8388608]{0:T(1024)(128)(4,1)}), s8[4194304]{0:T(1024)(128)(4,1)S(1)}, s32[]{:S(2)}) async-start(s8[8388608]{0:T(1024)(128)(4,1)} %bitcast.129), calls=%async_computation.5 | async-start | bytes 8388608
  196.6 4.7 copy-start.8
  201.2 1.2 copy-start.3
  204.3 1.0 copy-start.14
  215.4 9.0 %copy-start.9 = (bf16[512,4096]{1,0:T(8,128)(2,1)}, bf16[512,4096]{1,0:T(8,128)(2,1)S(1)}, u32[]{:S(2)}) copy-start(bf16[512,4096]{1,0:T(8,128)(2,1)S(1)} %multiply_convert_fusion.1.refs_16_) | copy-start | bytes 12582916
  224.4 2.8 copy-start.49
  227.2 2.6 copy-start.22
  252.9 6.4 copy-start.1
  253.0 6.4 copy-start.6
  259.4 3.1 copy-start.48
  261.5 1.0 copy-start.15
  279.8 7.4 %copy-start.4 = (f32[512,1024]{1,0:T(8,128)S(1)}, f32[512,1024]{1,0:T(8,128)}, u32[]{:S(2)}) copy-start(f32[512,1024]{1,0:T(8,128)} %get-tuple-element.94) | copy-start | bytes 6291460
  289.4 10.5 %copy-start.16 = (bf16[512,1024]{1,0:T(8,128)(2,1)}, bf16[512,1024]{1,0:T(8,128)(2,1)S(1)}, u32[]{:S(2)}) copy-start(bf16[512,1024]{1,0:T(8,128)(2,1)S(1)} %get-tuple-element.91.refs_11_) | copy-start | bytes 3145732
  289.4 11.2 %copy-start.17 = (bf16[512,1024]{1,0:T(8,128)(2,1)S(1)}, bf16[512,1024]{1,0:T(8,128)(2,1)}, u32[]{:S(2)}) copy-start(bf16[512,1024]{1,0:T(8,128)(2,1)} %get-tuple-element.100.refs_8_) | copy-start | bytes 3145732
  289.4 11.2 %copy-start.47 = (bf16[1024,1024]{1,0:T(8,128)(2,1)S(1)}, bf16[1024,1024]{1,0:T(8,128)(2,1)}, u32[]{:S(2)}) copy-start(bf16[1024,1024]{1,0:T(8,128)(2,1)} %get-tuple-element.53) | copy-start | bytes 6291460
  289.4 11.2 %copy-start.50 = (bf16[512,1024]{1,0:T(8,128)(2,1)S(1)}, bf16[512,1024]{1,0:T(8,128)(2,1)}, u32[]{:S(2)}) copy-start(bf16[512,1024]{1,0:T(8,128)(2,1)} %param.21) | copy-start | bytes 3145732
  299.9 8.5 %copy-start.10 = (bf16[512,4096]{1,0:T(8,128)(2,1)}, bf16[512,4096]{1,0:T(8,128)(2,1)S(1)}, u32[]{:S(2)}) copy-start(bf16[512,4096]{1,0:T(8,128)(2,1)S(1)} %multiply_convert_fusion.refs_10_) | copy-start | bytes 12582916
  302.0 1.2 copy-start.29
  302.0 1.9 copy-start.45
  303.9 1.5 copy-start.19
  305.4 3.0 slice-start
  307.1 1.3 copy-start.21
  307.1 1.4 copy-start.35
  307.1 1.4 copy-start.37
  307.1 1.4 copy-start.41
  307.1 1.4 copy-start.43
  307.1 2.8 slice-start.1
  309.9 6.4 copy-start.26
  309.9 6.4 copy-start.39
  638.3 4.4 copy-start.25
  642.7 2.5 copy-start.24
  645.2 2.6 copy-start.23
  647.8 2.5 copy-start.27
  650.3 2.0 copy-start.28
  652.4 1.6 copy-start.33
  652.4 2.7 copy-start.32
  653.9 2.2 copy-start.31
  654.0 3.3 copy-start.30
  656.1 5.1 copy-start.5
  661.3 3.8 copy-start.20
  661.3 3.8 copy-start.46
